TPU v7x, 128 devices: a whole 4x4x4 slice. The times are simulated.
128 devices in a mesh: seq: 32 (over z, x, y_hi), mp: 4 (over y_lo, core).
Axes of the slice: x: 4, y: 4 (y_hi: 2, y_lo: 2; y = y_hi * 2 + y_lo), z: 4, core: 2. Of those that a mesh axis runs over, the one named last changes fastest.
Arguments:
- layer_inputs: bfloat16 [16384, 4096], P('seq', 'mp'), may hold values from -6 to 6
- article_opening: int32 [32], P('seq'), may hold values from 1 to 512, as said below
- blending_ratios: float32 [5, 4096], replicated, may hold values from 0 to 1
- blending_narrow_operand: bfloat16 [4096, 256], P('mp'), may hold values from -0.09375 to 0.09375
- blending_widen_operand: bfloat16 [4, 64, 4096], replicated, may hold values from -0.75 to 0.75
- fading_narrow_operand: bfloat16 [4096, 128], P('mp'), may hold values from -0.09375 to 0.09375
- fading_widen_operand: bfloat16 [128, 2048], P(None, 'mp'), may hold values from -0.5 to 0.5
- fading_anchor: float32 [2048], P('mp'), may hold values from -14 to -3
- immediate_reward: float32 [2048], P('mp'), may hold values from 0.25 to 1.5
- acceptance_weights: bfloat16 [4096, 2048], P(None, 'mp'), may hold values from -0.09375 to 0.09375
- lookup_weights: bfloat16 [4096, 2048], P(None, 'mp'), may hold values from -0.09375 to 0.09375
- payload_weights: bfloat16 [4096, 2048], P(None, 'mp'), may hold values from -0.09375 to 0.09375
- group_scaling_weight: float32 [2048], P('mp'), may hold values from 0.5 to 1.5
- group_scaling_shift: float32 [2048], P('mp'), may hold values from -2 to 2
Outputs:
- time_mix: bfloat16 [16384, 2048], P('seq', 'mp')
Inputs may be any that keep to these rules, and one draw needn't show every extreme that they name: `article_opening`: entry j is the offset within shard j of the first token of a document that begins in shard j, or 512 where none begins there; at most one document begins in a shard.
All inputs are finite; a program needn't handle non-finite values.
Results may differ from a plain program's by a relative error of at most 0.0076.
Values may be sent and summed in bfloat16 or wider, within the bound.
No kernel may reach another device: no remote copies, remote signals or barrier semaphores. Data moves between devices by JAX's collectives and lax.ppermute only.
A program may use at most 128 MiB of HBM per device.

v0:
```python
import jax
import jax.numpy as jnp
from jax import lax
from jax.sharding import Mesh
from jax.sharding import PartitionSpec as P

GROUP_WIDTH = 64
SEQ = ("seq_0", "seq_1", "seq_2")


def joined_along(parts, dim):
    parts = jnp.moveaxis(parts, 0, dim)
    dims = parts.shape
    return parts.reshape(*dims[:dim], dims[dim] * dims[dim + 1], *dims[dim + 2 :])


def copy_for_each(array, axis):
    length = lax.axis_size(axis)
    return lax.all_to_all(
        jnp.broadcast_to(array[None], (length, *array.shape)), axis, 0, 0, tiled=True
    )


def collect(array, axis, dim):
    return joined_along(copy_for_each(array, axis), dim)


def side_by_side(arrays, axis, dim, along):
    widths = [a.shape[along] for a in arrays]
    both = jnp.concatenate(arrays, axis=along)
    whole = collect(both, axis, dim)
    return tuple(jnp.split(whole, [sum(widths[:k]) for k in range(1, len(widths))], axis=along))


def from_behind(array, axis, by):
    length = lax.axis_size(axis)
    pairs = [(i, i + by) for i in range(length) if 0 <= i + by < length]
    return lax.ppermute(array, axis, pairs)


def neutral_like(array, identity):
    return jax.tree.map(
        lambda part, zero: jnp.zeros_like(part) + jnp.asarray(zero, part.dtype), array, identity
    )


def entering_2(array, axes, combine, identity):
    before = start = neutral_like(array, identity)
    so_far = array
    for axis in reversed(axes):
        length, here = (lax.axis_size(axis), lax.axis_index(axis))
        pieces = jax.tree.map(lambda part: lax.all_gather(part, axis), so_far)
        inside, so_far = (start, start)
        for k in range(length):
            passed = k < here
            so_far = combine(so_far, jax.tree.map(lambda part: part[k], pieces))
            inside = jax.tree.map(lambda new, old: jnp.where(passed, new, old), so_far, inside)
        before = combine(inside, before)
    return before


def body(
    layer_inputs,
    article_opening,
    blending_ratios,
    blending_narrow_operand,
    blending_widen_operand,
    fading_narrow_operand,
    fading_widen_operand,
    fading_anchor,
    immediate_reward,
    acceptance_weights,
    lookup_weights,
    payload_weights,
    group_scaling_weight,
    group_scaling_shift,
):
    tok_rows, width_part = layer_inputs.shape
    channels_here = fading_anchor.shape[0]
    groups_in_piece = channels_here // GROUP_WIDTH
    mix_whole, decay_whole = side_by_side(
        (blending_narrow_operand, fading_narrow_operand), "mp", 0, 1
    )
    before_part = from_behind(layer_inputs[-1:], SEQ, 1)
    full_rows, before_row = side_by_side((layer_inputs, before_part), "mp", 1, 0)
    position = jnp.arange(tok_rows, dtype=jnp.int32)
    start_offset = article_opening[0]
    shifted = jnp.concatenate([before_row, full_rows[:-1]], axis=0)
    shifted = jnp.where((position != start_offset)[:, None], shifted, jnp.zeros_like(shifted))
    wide_rows = full_rows.astype(jnp.float32)
    difference = shifted.astype(jnp.float32) - wide_rows
    blended = (wide_rows + difference * blending_ratios[0]).astype(jnp.bfloat16)
    rank_total = jnp.dot(blended, mix_whole, preferred_element_type=jnp.float32)
    rank_hidden = jnp.tanh(rank_total).astype(jnp.bfloat16)
    rank_width = blending_widen_operand.shape[1]
    mixed_inputs = []
    for branch in range(4):
        delta_rows = jnp.dot(
            rank_hidden[:, branch * rank_width : (branch + 1) * rank_width],
            blending_widen_operand[branch],
            preferred_element_type=jnp.float32,
        )
        mixed_inputs.append(
            (wide_rows + difference * (blending_ratios[branch + 1] + delta_rows)).astype(
                jnp.bfloat16
            )
        )
    decay_total = jnp.dot(mixed_inputs[0], decay_whole, preferred_element_type=jnp.float32)
    decay_hidden = jnp.tanh(decay_total).astype(jnp.bfloat16)
    log_decay = -jnp.exp(
        fading_anchor
        + jnp.dot(decay_hidden, fading_widen_operand, preferred_element_type=jnp.float32)
    )
    recept_rows = jnp.dot(mixed_inputs[3], acceptance_weights, preferred_element_type=jnp.float32)
    key_rows = jnp.dot(mixed_inputs[1], lookup_weights, preferred_element_type=jnp.float32)
    value_rows = jnp.dot(mixed_inputs[2], payload_weights, preferred_element_type=jnp.float32)
    block_span = min(32, tok_rows)
    blocks = tok_rows // block_span
    acceptance_lines = recept_rows.reshape(blocks, block_span, groups_in_piece, GROUP_WIDTH)
    lookup_mapped = key_rows.reshape(blocks, block_span, groups_in_piece, GROUP_WIDTH)
    value_projected = value_rows.reshape(blocks, block_span, groups_in_piece, GROUP_WIDTH)
    decay_log = log_decay.reshape(blocks, block_span, groups_in_piece, GROUP_WIDTH)
    reward_by_group = immediate_reward.reshape(groups_in_piece, GROUP_WIDTH)
    segment = (position >= start_offset).astype(jnp.float32).reshape(blocks, block_span)
    inclusive = jnp.cumsum(decay_log, axis=1)
    exclusive = inclusive - decay_log
    earlier = jnp.arange(block_span)[None, :] < jnp.arange(block_span)[:, None]
    same_doc = segment[:, :, None] == segment[:, None, :]
    allowed = jnp.logical_and(earlier[None], same_doc)
    pair_log = jnp.minimum(exclusive[:, :, None] - inclusive[:, None, :], 0.0)
    pair_decay = jnp.where(allowed[:, :, :, None, None], jnp.exp(pair_log), 0.0)
    scores = jnp.sum(pair_decay * acceptance_lines[:, :, None] * lookup_mapped[:, None, :], axis=-1)
    intra = jnp.einsum("ntsh,nshj->nthj", scores, value_projected, precision=lax.Precision.HIGHEST)
    self_contribution = (
        jnp.sum(acceptance_lines * reward_by_group * lookup_mapped, axis=-1, keepdims=True)
        * value_projected
    )
    last_log = inclusive[:, -1]
    seg_last = segment[:, -1]
    seg_before = jnp.concatenate([jnp.zeros((1,), jnp.float32), segment[:-1, -1]])
    tail_weight = (
        jnp.exp(last_log[:, None] - inclusive)
        * (segment == seg_last[:, None]).astype(jnp.float32)[:, :, None, None]
    )
    block_state = jnp.einsum(
        "nshi,nshj->nhij",
        lookup_mapped * tail_weight,
        value_projected,
        precision=lax.Precision.HIGHEST,
    )
    block_decay = jnp.exp(last_log) * (seg_last == seg_before).astype(jnp.float32)[:, None, None]

    def advance(carried, pieces):
        decay_now, added = pieces
        return (decay_now[:, :, None] * carried + added, carried)

    initial = jnp.zeros((groups_in_piece, GROUP_WIDTH, GROUP_WIDTH), jnp.float32)
    shard_state, entering = lax.scan(advance, initial, (block_decay, block_state))
    reach = (
        jnp.exp(exclusive) * (segment == seg_before[:, None]).astype(jnp.float32)[:, :, None, None]
    )
    inter = jnp.einsum(
        "nthi,nhij->nthj", acceptance_lines * reach, entering, precision=lax.Precision.HIGHEST
    )
    local_out = intra + self_contribution + inter
    offsets = jnp.cumsum(last_log, axis=0) - last_log
    shard_decay = jnp.exp(jnp.sum(last_log, axis=0)) * (start_offset >= tok_rows).astype(
        jnp.float32
    )
    from_before = (
        jnp.exp(offsets[:, None] + exclusive)
        * (segment < 0.5).astype(jnp.float32)[:, :, None, None]
    )

    def combine(earlier_part, later_part):
        return (
            earlier_part[0] * later_part[0],
            later_part[0][:, :, None] * earlier_part[1] + later_part[1],
        )

    identity = (jnp.ones_like(shard_decay), jnp.zeros_like(shard_state))
    prefix_decay, incoming_state = entering_2((shard_decay, shard_state), SEQ, combine, identity)
    outputs = local_out + jnp.einsum(
        "nthi,hij->nthj",
        acceptance_lines * from_before,
        incoming_state,
        precision=lax.Precision.HIGHEST,
    )
    outputs = outputs.reshape(tok_rows, groups_in_piece, GROUP_WIDTH)
    centred = outputs - jnp.mean(outputs, axis=-1, keepdims=True)
    variance = jnp.mean(centred * centred, axis=-1, keepdims=True)
    normed = (centred / jnp.sqrt(variance + 0.00064)).reshape(tok_rows, channels_here)
    return (normed * group_scaling_weight + group_scaling_shift).astype(jnp.bfloat16)


def solution(mesh):
    torus = Mesh(mesh.devices.reshape(4, 4, 2, mesh.shape["mp"]), ("seq_0", "seq_1", "seq_2", "mp"))
    placed = (
        P(SEQ, "mp"),
        P(SEQ),
        P(),
        P("mp", None),
        P(),
        P("mp", None),
        P(None, "mp"),
        P("mp"),
        P("mp"),
        P(None, "mp"),
        P(None, "mp"),
        P(None, "mp"),
        P("mp"),
        P("mp"),
    )
    return jax.shard_map(body, mesh=torus, in_specs=placed, out_specs=P(SEQ, "mp"), check_vma=False)
```

profile of v0, /device:TPU:8, one launch (start us, length us, event | category | flops | bytes accessed | tf_op | source)
XLA Modules:
  0.0 362.6 jit_solution(473346973249839672)
XLA Ops:
  10.1 6.3 %all-to-all-start = ((bf16[4,513,1024]{2,1,0:T(8,128)(2,1)}), bf16[4,513,1024]{2,1,0:T(8,128)(2,1)}, u32[]{:S(2)}, u32[]{:S(2)}) async-start(bf16[4,513,1024]{2,1,0:T(8,128)(2,1)} %broadcast_in_dim.27), calls=%async_computation | async-start | bytes 8519680 | tf_op jit(solution)/shard_map/all_to_all | solution.py:19
  20.4 43.3 %all-to-all-done = bf16[4,513,1024]{2,1,0:T(8,128)(2,1)} async-done(((bf16[4,513,1024]{2,1,0:T(8,128)(2,1)}), bf16[4,513,1024]{2,1,0:T(8,128)(2,1)}, u32[]{:S(2)}, u32[]{:S(2)}) %all-to-all-start) | async-done | bytes 4202528 | tf_op jit(solution)/shard_map/all_to_all | solution.py:19
  65.7 6.3 %all-to-all-start.1 = ((bf16[4,1024,384]{2,1,0:T(8,128)(2,1)}), bf16[4,1024,384]{2,1,0:T(8,128)(2,1)}, u32[]{:S(2)}, u32[]{:S(2)}) async-start(bf16[4,1024,384]{2,1,0:T(8,128)(2,1)} %broadcast_in_dim.34), calls=%async_computation.1 | async-start | bytes 6291456 | tf_op jit(solution)/shard_map/all_to_all | solution.py:19
  72.8 7.6 %copy.141 = bf16[4,513,1024]{1,2,0:T(8,128)(2,1)} copy(bf16[4,513,1024]{2,1,0:T(8,128)(2,1)} %all-to-all-done) | data formatting | bytes 8404992 | tf_op jit(solution)/shard_map/all_to_all | solution.py:19
  87.7 6.5 %copy.142 = bf16[511,4096]{1,0:T(8,128)(2,1)} copy(bf16[511,4096]{0,1:T(8,128)(2,1)} %bitcast.164) | data formatting | bytes 8372224 | tf_op jit(solution)/shard_map/slice | solution.py:88
  94.1 6.6 %bitcast_convert_fusion = f32[512,4096]{0,1:T(8,128)} fusion(bf16[512,4,1024]{0,2,1:T(8,128)(2,1)} %split.19), kind=kLoop, calls=%fused_computation.12 | loop fusion | flops 2097152 | bytes 12582912 | tf_op jit(solution)/shard_map/convert_element_type | solution.py:90
  100.8 9.1 %copy.145 = f32[512,4096]{1,0:T(8,128)} copy(f32[512,4096]{0,1:T(8,128)} %bitcast_convert_fusion) | data formatting | bytes 16777216 | tf_op jit(solution)/shard_map/convert_element_type | solution.py:90
  109.9 8.0 %fusion.19 = bf16[512,256]{0,1:T(8,128)(2,1)S(1)} fusion(bf16[4096,384]{1,0:T(8,128)(2,1)} %bitcast.7, f32[512,4096]{1,0:T(8,128)} %copy.145, f32[4096]{0:T(1024)S(1)} %bitcast.172, bf16[511,4096]{1,0:T(8,128)(2,1)} %copy.142, bf16[1,4096]{1,0:T(2,128)(2,1)S(1)} %bitcast.173, pred[512]{0:T(512)(128)(4,1)S(1)} %iota_compare_fusion.1), kind=kOutput, calls=%fused_computation.36 | convolution fusion | flops 1094844416 | bytes 14967296 | tf_op jit(solution)/shard_map/dot_general | solution.py:93
  118.6 7.9 %fusion.24 = bf16[512,128]{1,0:T(8,128)(2,1)S(1)} fusion(f32[512,4096]{1,0:T(8,128)} %copy.145, f32[4096]{0:T(1024)S(1)} %bitcast.171, bf16[4096,384]{1,0:T(8,128)(2,1)} %bitcast.7, bf16[4,64,4096]{2,1,0:T(8,128)(2,1)} %param.20, bf16[512,256]{0,1:T(8,128)(2,1)S(1)} %fusion.19, bf16[511,4096]{1,0:T(8,128)(2,1)} %copy.142, ...), kind=kOutput, calls=%fused_computation.39 | convolution fusion | flops 828440576 | bytes 14385664 | tf_op jit(solution)/shard_map/dot_general | solution.py:108
  131.0 10.5 %fusion.27 = f32[512,512]{1,0:T(8,128)S(1)} fusion(bf16[4096,512]{1,0:T(8,128)(2,1)} %param.25, f32[512,4096]{1,0:T(8,128)} %copy.145, f32[4096]{0:T(1024)S(1)} %bitcast.170, bf16[4,64,4096]{2,1,0:T(8,128)(2,1)} %param.20, bf16[512,256]{0,1:T(8,128)(2,1)} %copy-done.28, bf16[511,4096]{1,0:T(8,128)(2,1)} %copy.142, bf16[1,4096]{1,0:T(2,128)(2,1)S(1)} %bitcast.175, ...), kind=kOutput, calls=%fused_computation.43 | convolution fusion | flops 2438987776 | bytes 18440704 | tf_op jit(solution)/shard_map/dot_general | solution.py:114
  143.2 10.9 %fusion.26 = f32[512,512]{1,0:T(8,128)S(1)} fusion(bf16[4096,512]{1,0:T(8,128)(2,1)} %param.27, f32[512,4096]{1,0:T(8,128)} %copy.145, f32[4096]{0:T(1024)S(1)} %bitcast.169, bf16[4,64,4096]{2,1,0:T(8,128)(2,1)} %param.20, bf16[512,256]{0,1:T(8,128)(2,1)} %copy-done.28, bf16[511,4096]{1,0:T(8,128)(2,1)} %copy.142, bf16[1,4096]{1,0:T(2,128)(2,1)S(1)} %bitcast.176, ...), kind=kOutput, calls=%fused_computation.42 | convolution fusion | flops 2438987776 | bytes 18440704 | tf_op jit(solution)/shard_map/dot_general | solution.py:116
  155.9 10.4 %fusion.28 = f32[512,512]{1,0:T(8,128)S(1)} fusion(bf16[4096,512]{1,0:T(8,128)(2,1)} %param.26, f32[512,4096]{1,0:T(8,128)} %copy.145, f32[4096]{0:T(1024)S(1)} %bitcast.168, bf16[4,64,4096]{2,1,0:T(8,128)(2,1)} %param.20, bf16[512,256]{0,1:T(8,128)(2,1)} %copy-done.28, bf16[511,4096]{1,0:T(8,128)(2,1)} %copy.142, bf16[1,4096]{1,0:T(2,128)(2,1)S(1)} %bitcast.177, ...), kind=kOutput, calls=%fused_computation.44 | convolution fusion | flops 2438987776 | bytes 18440704 | tf_op jit(solution)/shard_map/dot_general | solution.py:115
  168.2 5.9 %all-gather = f32[16,64]{1,0:T(8,128)S(1)} all-gather(f32[8,64]{1,0:T(8,128)S(1)} %exponential_multiply_fusion.1), channel_id=2, replica_groups=mesh['seq_0'=4,'seq_1'=4,'seq_2'=2,'mp'=4] {'seq_2'}, dimensions={0}, use_global_device_ids=true | all-gather | bytes 6144 | tf_op jit(solution)/shard_map/all_gather | solution.py:52
  174.0 13.8 %all-gather.2 = f32[32,64]{1,0:T(8,128)S(1)} all-gather(f32[8,64]{1,0:T(8,128)S(1)} %get-tuple-element.87), channel_id=4, replica_groups=mesh['seq_0'=4,'seq_1'=4,'seq_2'=2,'mp'=4] {'seq_1'}, dimensions={0}, use_global_device_ids=true | all-gather | bytes 10240 | tf_op jit(solution)/shard_map/all_gather | solution.py:52
  187.9 15.0 %all_gather.28 = f32[4,8,64]{2,1,0:T(8,128)S(1)} all-gather(f32[1,8,64]{2,1,0:T(8,128)S(1)} %get-tuple-element.81), channel_id=1, replica_groups=mesh['seq_0'=4,'seq_1'=4,'seq_2'=2,'mp'=4] {'seq_0'}, dimensions={0}, use_global_device_ids=true | all-gather | bytes 10240 | tf_op jit(solution)/shard_map/all_gather | solution.py:52
  208.0 43.7 %multiply_reduce_fusion = f32[16,32,32,8]{3,2,1,0:T(8,128)} fusion(f32[16,32,8,64]{3,2,1,0:T(8,128)S(1)} %copy-done.5, f32[16,32,8,64]{3,2,1,0:T(8,128)S(1)} %copy-done.3, f32[16,32,8,64]{3,2,1,0:T(8,128)S(1)} %fusion.126, f32[16,32,8,64]{3,2,1,0:T(8,128)S(1)} %get-tuple-element.64, pred[16,32,32]{2,1,0:T(8,128)(4,1)S(1)} %copy-done.11), kind=kLoop, calls=%fused_computation.3 | loop fusion | flops 50200576 | bytes 4734976 | tf_op jit(solution)/shard_map/reduce_sum | solution.py:132
  251.7 6.3 %copy.150 = f32[16,32,32,8]{2,1,3,0:T(8,128)} copy(f32[16,32,32,8]{3,2,1,0:T(8,128)} %multiply_reduce_fusion) | data formatting | bytes 1048576 | tf_op jit(solution)/shard_map/reduce_sum | solution.py:132
  258.0 4.9 %multiply_reduce_fusion.2 = (f32[16,32,8]{2,1,0:T(8,128)S(1)}, f32[16,32,8,64]{3,2,1,0:T(8,128)}, f32[16,32,8,64]{3,2,1,0:T(8,128)}) fusion(f32[16,32,8,64]{3,2,1,0:T(8,128)} %mul.334, f32[16,32,8,64]{3,2,1,0:T(8,128)} %mul.330, f32[8,64]{1,0:T(8,128)S(1)} %copy-done.15, f32[16,32]{1,0:T(8,128)S(1)} %get-tuple-element.92, f32[16,32,8,64]{3,2,1,0:T(8,128)} %copy-done.6, ...), kind=kLoop, calls=%fused_computation.28 | loop fusion | flops 2355200 | bytes 6379520 | tf_op jit(solution)/shard_map/reduce_sum | solution.py:135
  263.1 11.0 %fusion.7 = f32[16,8,64,64]{3,2,1,0:T(8,128)} fusion(f32[16,32,8,64]{3,2,1,0:T(8,128)} %get-tuple-element.69, f32[16,32,8,64]{3,2,1,0:T(8,128)} %reshape.260), kind=kOutput, calls=%fused_computation.22 | convolution fusion | flops 201326592 | bytes 4194304 | tf_op jit(solution)/shard_map/nshi,nshj->nhij/dot_general | solution.py:145
  274.1 30.2 %while.13 = (s32[]{:T(128)}, f32[8,64,64]{2,1,0:T(8,128)S(1)}, f32[16,8,64,64]{3,2,1,0:T(8,128)}, f32[16,8,64]{2,1,0:T(8,128)S(1)}, f32[16,8,64,64]{3,2,1,0:T(8,128)}, /*index=5*/s32[]{:T(128)}, s32[]{:T(128)}) while((s32[]{:T(128)}, f32[8,64,64]{2,1,0:T(8,128)S(1)}, f32[16,8,64,64]{3,2,1,0:T(8,128)}, f32[16,8,64]{2,1,0:T(8,128)S(1)}, ...), condition=%wide.region_4.5_spmd.clone, body=%wide.region_3.4_spmd.clone.sunk | while | flops 131075 | bytes 792684 | solution.py:158
  304.4 8.7 %all-gather.1 = f32[16,64,64]{2,1,0:T(8,128)S(1)} all-gather(f32[8,64,64]{2,1,0:T(8,128)S(1)} %get-tuple-element.34), channel_id=3, replica_groups=mesh['seq_0'=4,'seq_1'=4,'seq_2'=2,'mp'=4] {'seq_2'}, dimensions={0}, use_global_device_ids=true | all-gather | bytes 393216 | tf_op jit(solution)/shard_map/all_gather | solution.py:52
  313.2 13.8 %all_gather.31 = f32[4,8,64,64]{3,2,1,0:T(8,128)S(1)} all-gather(f32[1,8,64,64]{3,2,1,0:T(8,128)S(1)} %bitcast_add_fusion.8), channel_id=1, replica_groups=mesh['seq_0'=4,'seq_1'=4,'seq_2'=2,'mp'=4] {'seq_1'}, dimensions={0}, use_global_device_ids=true | all-gather | bytes 655360 | tf_op jit(solution)/shard_map/all_gather | solution.py:52
  327.4 13.8 %all_gather.32 = f32[4,8,64,64]{3,2,1,0:T(8,128)S(1)} all-gather(f32[1,8,64,64]{3,2,1,0:T(8,128)S(1)} %multiply_add_fusion), channel_id=1, replica_groups=mesh['seq_0'=4,'seq_1'=4,'seq_2'=2,'mp'=4] {'seq_0'}, dimensions={0}, use_global_device_ids=true | all-gather | bytes 655360 | tf_op jit(solution)/shard_map/all_gather | solution.py:52
  341.3 6.0 %fusion.5 = f32[16,8,64,32]{2,3,1,0:T(8,128)S(1)} fusion(f32[16,8,64,64]{3,2,1,0:T(8,128)} %get-tuple-element.33, f32[16,32,8,64]{3,2,1,0:T(8,128)S(1)} %copy-done.9), kind=kOutput, calls=%fused_computation.20 | convolution fusion | flops 201326592 | bytes 4194304 | tf_op jit(solution)/shard_map/nthi,nhij->nthj/dot_general | solution.py:162
  (166 shorter events, 84.4 us)
Async XLA Ops:
  0.0 126.5 %copy-start = (bf16[128,512]{1,0:T(8,128)(2,1)S(1)}, bf16[128,512]{1,0:T(8,128)(2,1)}, u32[]{:S(2)}) copy-start(bf16[128,512]{1,0:T(8,128)(2,1)} %param.22) | copy-start | bytes 393220
  0.8 5.5 %collective-permute-start = (bf16[1,1024]{1,0:T(2,128)(2,1)S(1)}, bf16[1,1024]{1,0:T(2,128)(2,1)S(1)}, u32[]{:S(2)}, u32[]{:S(2)}) collective-permute-start(bf16[1,1024]{1,0:T(2,128)(2,1)S(1)} %slice.120), channel_id=1, source_target_pairs={{0,4},{4,8},{8,12},{12,16},{16,20},{20,24},{24,28},{28,32},{32,36}... | collective-permute-start | bytes 6152 | tf_op jit(solution)/shard_map/ppermute | solution.py:38
  10.1 7.0 %copy-start.25 = (f32[512]{0:T(512)S(1)}, f32[512]{0:T(512)}, u32[]{:S(2)}) copy-start(f32[512]{0:T(512)} %param.24) | copy-start | bytes 6148
  10.1 8.1 %copy-start.10 = (bf16[1024,256]{1,0:T(8,128)(2,1)S(1)}, bf16[1024,256]{1,0:T(8,128)(2,1)}, u32[]{:S(2)}) copy-start(bf16[1024,256]{1,0:T(8,128)(2,1)} %param.19) | copy-start | bytes 1572868
  10.1 8.1 %copy-start.13 = (bf16[1024,128]{1,0:T(8,128)(2,1)S(1)}, bf16[1024,128]{1,0:T(8,128)(2,1)}, u32[]{:S(2)}) copy-start(bf16[1024,128]{1,0:T(8,128)(2,1)} %param.21) | copy-start | bytes 786436
  10.1 53.6 %all-to-all-start = ((bf16[4,513,1024]{2,1,0:T(8,128)(2,1)}), bf16[4,513,1024]{2,1,0:T(8,128)(2,1)}, u32[]{:S(2)}, u32[]{:S(2)}) async-start(bf16[4,513,1024]{2,1,0:T(8,128)(2,1)} %broadcast_in_dim.27), calls=%async_computation | async-start | bytes 8519680 | tf_op jit(solution)/shard_map/all_to_all | solution.py:19
  20.4 51.6 %copy-start.14 = (f32[5,4096]{1,0:T(8,128)S(1)}, f32[5,4096]{1,0:T(8,128)}, u32[]{:S(2)}) copy-start(f32[5,4096]{1,0:T(8,128)} %param.18) | copy-start | bytes 245764
  65.7 44.2 %all-to-all-start.1 = ((bf16[4,1024,384]{2,1,0:T(8,128)(2,1)}), bf16[4,1024,384]{2,1,0:T(8,128)(2,1)}, u32[]{:S(2)}, u32[]{:S(2)}) async-start(bf16[4,1024,384]{2,1,0:T(8,128)(2,1)} %broadcast_in_dim.34), calls=%async_computation.1 | async-start | bytes 6291456 | tf_op jit(solution)/shard_map/all_to_all | solution.py:19
  72.1 45.8 %copy-start.26 = (pred[512]{0:T(512)(128)(4,1)}, pred[512]{0:T(512)(128)(4,1)S(1)}, u32[]{:S(2)}) copy-start(pred[512]{0:T(512)(128)(4,1)S(1)} %iota_compare_fusion.1) | copy-start | bytes 1540
  80.3 4.7 %copy-start.2 = (bf16[4,513,1024]{1,2,0:T(8,128)(2,1)S(1)}, bf16[4,513,1024]{1,2,0:T(8,128)(2,1)}, u32[]{:S(2)}) copy-start(bf16[4,513,1024]{1,2,0:T(8,128)(2,1)} %copy.141) | copy-start | bytes 12607492
  87.7 30.3 %copy-start.19 = (bf16[1,1,4,1024]{3,1,2,0:T(2,128)(2,1)}, bf16[1,1,4,1024]{3,1,2,0:T(2,128)(2,1)S(1)}, u32[]{:S(2)}) copy-start(bf16[1,1,4,1024]{3,1,2,0:T(2,128)(2,1)S(1)} %copy.162) | copy-start | bytes 24580
  118.6 7.9 %copy-start.21 = (f32[512]{0:T(512)S(1)}, f32[512]{0:T(512)}, u32[]{:S(2)}) copy-start(f32[512]{0:T(512)} %param.23) | copy-start | bytes 6148
  126.8 4.1 %copy-start.18 = (f32[1,4096]{1,0:T(1,128)S(1)}, f32[1,4096]{1,0:T(1,128)}, u32[]{:S(2)}) copy-start(f32[1,4096]{1,0:T(1,128)} %get-tuple-element.76) | copy-start | bytes 49156
  131.0 12.2 %copy-start.17 = (f32[1,4096]{1,0:T(1,128)S(1)}, f32[1,4096]{1,0:T(1,128)}, u32[]{:S(2)}) copy-start(f32[1,4096]{1,0:T(1,128)} %get-tuple-element.72) | copy-start | bytes 49156
  143.2 12.7 %copy-start.16 = (f32[1,4096]{1,0:T(1,128)S(1)}, f32[1,4096]{1,0:T(1,128)}, u32[]{:S(2)}) copy-start(f32[1,4096]{1,0:T(1,128)} %get-tuple-element.75) | copy-start | bytes 49156
  155.9 12.2 %copy-start.24 = (f32[16]{0:T(128)S(1)}, f32[16]{0:T(128)}, u32[]{:S(2)}) copy-start(f32[16]{0:T(128)} %compare_convert_fusion) | copy-start | bytes 196
  202.9 5.1 %copy-start.3 = (f32[16,32,8,64]{3,2,1,0:T(8,128)S(1)}, f32[16,32,8,64]{3,2,1,0:T(8,128)}, u32[]{:S(2)}) copy-start(f32[16,32,8,64]{3,2,1,0:T(8,128)} %mul.330) | copy-start | bytes 3145732
  202.9 5.1 %copy-start.5 = (f32[16,32,8,64]{3,2,1,0:T(8,128)S(1)}, f32[16,32,8,64]{3,2,1,0:T(8,128)}, u32[]{:S(2)}) copy-start(f32[16,32,8,64]{3,2,1,0:T(8,128)} %mul.334) | copy-start | bytes 3145732
  202.9 5.1 %copy-start.11 = (pred[16,32,32]{2,1,0:T(8,128)(4,1)S(1)}, pred[16,32,32]{2,1,0:T(8,128)(4,1)}, u32[]{:S(2)}) copy-start(pred[16,32,32]{2,1,0:T(8,128)(4,1)} %compare_and_fusion) | copy-start | bytes 49156
  251.7 6.3 %copy-start.12 = (f32[16,8,64]{2,1,0:T(8,128)S(1)}, f32[16,8,64]{2,1,0:T(8,128)}, u32[]{:S(2)}) copy-start(f32[16,8,64]{2,1,0:T(8,128)} %get-tuple-element.71) | copy-start | bytes 98308
  251.7 6.3 %copy-start.15 = (f32[8,64]{1,0:T(8,128)S(1)}, f32[8,64]{1,0:T(8,128)}, u32[]{:S(2)}) copy-start(f32[8,64]{1,0:T(8,128)} %mul.337) | copy-start | bytes 6148
  304.4 36.9 %copy-start.9 = (f32[16,32,8,64]{3,2,1,0:T(8,128)S(1)}, f32[16,32,8,64]{3,2,1,0:T(8,128)}, u32[]{:S(2)}) copy-start(f32[16,32,8,64]{3,2,1,0:T(8,128)} %get-tuple-element.63) | copy-start | bytes 3145732
  341.3 6.0 %copy-start.8 = (f32[16,32,8,64]{3,2,1,0:T(8,128)S(1)}, f32[16,32,8,64]{3,2,1,0:T(8,128)}, u32[]{:S(2)}) copy-start(f32[16,32,8,64]{3,2,1,0:T(8,128)} %get-tuple-element.68) | copy-start | bytes 3145732
  358.1 4.2 %copy-start.1 = (bf16[128,512]{1,0:T(8,128)(2,1)S(1)}, bf16[128,512]{1,0:T(8,128)(2,1)}, u32[]{:S(2)}) copy-start(bf16[128,512]{1,0:T(8,128)(2,1)} %param.22) | copy-start | bytes 393220
  (8 other events, 21.6 us)
where the time goes:
time: 368 us; the launch traced here: 363 us
  other arithmetic  99 us (27%)
  matrix products  71.8 us (20%)
  blocking collectives  71 us (19%)
  local copies, waits for them, and re-layouts  57.4 us (16%)
  waiting for transfers between devices  44.6 us (12%)
  starting transfers between devices  16.8 us (5%)
    all_gather x6, blocking collectives, entering_2(): pieces = jax.tree.map(lambda part: lax.all_gather(part, axis), so_far)  71 us
    reduce_sum x1, other arithmetic, body(): jnp.sum(pair_decay * acceptance_lines[:, :, None] * lookup_mapped[:, None...  43.7 us
    all_to_all x2, waiting for transfers between devices, copy_for_each(): lax.all_to_all(jnp.broadcast_to(array[None], (length, *array.shape)), axi...  43.3 us
    add x16, other arithmetic, advance(): return (decay_now[:, :, None] * carried + added, carried)  17.9 us
    all_to_all x2, starting transfers between devices, copy_for_each(): lax.all_to_all(jnp.broadcast_to(array[None], (length, *array.shape)), axi...  12.7 us
    dynamic_update_slice x16, other arithmetic, body(): lax.scan(advance, initial, (block_decay, block_state))  11.8 us
    slice x2, local copies, waits for them, and re-layouts, body(): shifted = jnp.concatenate([before_row, full_rows[:-1]], axis=0)  11.1 us
    dot_general x1, matrix products, body(): jnp.einsum('nshi,nshj->nhij', lookup_mapped * tail_weight, value_projecte...  11 us
  transfers between devices with their start and end apart: 3, of which 2 were waited for; matrix products, arithmetic and copies ran while one was open for 11% of the time, Pallas kernels for 0%

commit v1 on v0

v1 whole, which is shorter than its diff:
```python
import functools

import jax
import jax.numpy as jnp
import numpy as np
from jax import lax
from jax.experimental import pallas as pl
from jax.experimental.pallas import tpu as pltpu
from jax.sharding import Mesh
from jax.sharding import PartitionSpec as P

F32 = jnp.float32
BF16 = jnp.bfloat16
GROUP = 64
SUB = 64
CHUNK = 128
CTX = 16
HALVES = (32, 16, 8, 4, 2, 1)
FLOOR = -100.0
SEQ = ("z", "x", "y_hi")
MP = ("y_lo", "core")


def xor_permute(array, axes, flip):
    length = lax.axis_size(axes)
    return lax.ppermute(array, axes, [(i, i ^ flip) for i in range(length)])


def dot(a, b):
    return jnp.dot(a, b, preferred_element_type=F32)


def dot_nt(a, b):
    return lax.dot_general(a, b, (((1,), (1,)), ((), ())), preferred_element_type=F32)


def dot_tn(a, b):
    return lax.dot_general(a, b, (((0,), (0,)), ((), ())), preferred_element_type=F32)


def sum_rows():
    t = np.arange(SUB)[:, None]
    j = np.arange(SUB)[None, :]
    blocks = []
    for half in HALVES:
        middle = (t // (2 * half)) * (2 * half) + half - 1
        right = t > middle
        blocks.append(np.where(right, (j > middle) & (j < t), (j > t) & (j <= middle)))
    blocks.append(j < t)
    blocks.append(j > t)
    one = np.concatenate(blocks, 0)
    return np.concatenate([one, one], 1).astype(np.float32)


def project_kernel(where_ref, *refs, first_token):
    mains, ctxs, narrows, fadings = refs[0:4], refs[4:8], refs[8:12], refs[12:16]
    (ratios, widen, w_r, w_k, w_v, fade_widen, anchor, out_r, out_k, out_v, out_w,
     rows, diffs, rank, hidden, mixed, acc) = refs[16:]
    step = pl.program_id(0)
    start = where_ref[1]
    count = rows.shape[1]

    for j in range(4):

        @pl.when(step == j)
        def _(j=j):
            x = mains[j][...].astype(F32)
            line = lax.broadcasted_iota(jnp.int32, x.shape, 0)
            before = pltpu.roll(x, 1, 0)
            before = jnp.where(line == 0, ctxs[j][CTX - 1 : CTX, :].astype(F32), before)
            before = jnp.where(line + first_token == start, 0.0, before)
            d = before - x
            rows[j] = x
            diffs[j] = d
            blended = (x + d * ratios[0:1, :]).astype(BF16)
            part = dot(blended, narrows[j][...])
            if j == 0:
                rank[...] = part
            else:
                rank[...] += part

    @pl.when(step == 4)
    def _():
        total = jnp.tanh(rank[...]).astype(BF16)
        for b in range(4):
            hidden[b] = total[:, 64 * b : 64 * b + 64]

    @pl.when(step >= 4)
    def _():
        j = step - 4
        for b in range(4):
            for n in range(4):
                cols = slice(256 * n, 256 * n + 256)
                delta = dot(hidden[b], widen[b, :, cols])
                mixed[b, :, cols] = (
                    rows[j, :, cols] + diffs[j, :, cols] * (ratios[b + 1 : b + 2, cols] + delta)
                ).astype(BF16)
        for i in range(4):

            @pl.when(j == i)
            def _(i=i):
                part = dot(mixed[0], fadings[i][...])
                if i == 0:
                    acc[...] = part
                else:
                    acc[...] += part

        for b, weights, out in ((1, w_k, out_k), (2, w_v, out_v), (3, w_r, out_r)):
            part = dot(mixed[b], weights[...])

            @pl.when(j == 0)
            def _(part=part, out=out):
                out[...] = part

            @pl.when(j > 0)
            def _(part=part, out=out):
                out[...] += part

    @pl.when(step == 7)
    def _():
        low = jnp.tanh(acc[...]).astype(BF16)
        out_w[...] = -jnp.exp(anchor[...] + dot(low, fade_widen[...]))


def project(where, first_token, mains, ctxs, narrows, fadings, ratios, widen, w_r, w_k, w_v, fade_widen, anchor):
    width = narrows[0].shape[0]
    channels = w_r.shape[1]

    def fixed(shape, index):
        return pl.BlockSpec(shape, lambda s, m: index)

    def late(s, m):
        return m[0] ^ jnp.maximum(s - 4, 0)

    in_specs = [fixed((CHUNK, width), (i, 0)) for _, i in mains]
    in_specs += [fixed((CTX, width), (i, 0)) for _, i in ctxs]
    in_specs += [fixed(a.shape, (0, 0)) for a in narrows + fadings]
    in_specs += [
        pl.BlockSpec((5, width), lambda s, m: (0, m[0] ^ (s % 4))),
        pl.BlockSpec((4, 64, width), lambda s, m: (0, 0, late(s, m))),
        pl.BlockSpec((width, channels), lambda s, m: (late(s, m), 0)),
        pl.BlockSpec((width, channels), lambda s, m: (late(s, m), 0)),
        pl.BlockSpec((width, channels), lambda s, m: (late(s, m), 0)),
        fixed(fade_widen.shape, (0, 0)),
        fixed(anchor.shape, (0, 0)),
    ]
    return pl.pallas_call(
        functools.partial(project_kernel, first_token=first_token),
        grid_spec=pltpu.PrefetchScalarGridSpec(
            num_scalar_prefetch=1,
            grid=(8,),
            in_specs=in_specs,
            out_specs=[fixed((CHUNK, channels), (0, 0))] * 4,
            scratch_shapes=[
                pltpu.VMEM((4, CHUNK, width), F32),
                pltpu.VMEM((4, CHUNK, width), F32),
                pltpu.VMEM((CHUNK, 256), F32),
                pltpu.VMEM((4, CHUNK, 64), BF16),
                pltpu.VMEM((4, CHUNK, width), BF16),
                pltpu.VMEM((CHUNK, 128), F32),
            ],
        ),
        out_shape=[jax.ShapeDtypeStruct((CHUNK, channels), F32)] * 4,
        compiler_params=pltpu.CompilerParams(
            dimension_semantics=("arbitrary",), vmem_limit_bytes=48 * 1024 * 1024
        ),
        cost_estimate=pl.CostEstimate(flops=3 * 10**9, bytes_accessed=17 * 10**6, transcendentals=0),
    )(where, *[a for a, _ in mains], *[a for a, _ in ctxs], *narrows, *fadings, ratios, widen, w_r, w_k, w_v, fade_widen, anchor)


def split_two(w):
    high = w.astype(BF16)
    low = (w - high.astype(F32)).astype(BF16)
    return jnp.concatenate([high, low], 0)


def states_kernel(where_ref, sums, *refs):
    ks, vs, ws = refs[0:4], refs[4:8], refs[8:12]
    entering, whole, packed = refs[12:]
    start = where_ref[1]
    channels = ks[0].shape[1]
    line = lax.broadcasted_iota(jnp.int32, (SUB, 1), 0)
    lane = lax.broadcasted_iota(jnp.int32, (SUB, 128), 1)
    state = jnp.zeros((SUB, channels), F32)
    decay = jnp.ones((1, channels), F32)
    for c in range(8):
        rows = slice(SUB * (c % 2), SUB * (c % 2) + SUB)
        w = jnp.maximum(ws[c // 2][rows, :], FLOOR)
        k = ks[c // 2][rows, :]
        v = vs[c // 2][rows, :].astype(BF16)
        tail = dot(sums[7 * SUB : 8 * SUB, :], split_two(w))
        ends_late = (c * SUB + SUB - 1) >= start
        begins_late = (c * SUB - 1) >= start if c else jnp.bool_(False)
        late = (line + c * SUB) >= start
        keep = late == ends_late
        total = jnp.where(begins_late == ends_late, jnp.exp(tail[0:1, :] + w[0:1, :]), 0.0)
        kk = jnp.where(keep, k * jnp.exp(tail), 0.0).astype(BF16)
        entering[c] = state.astype(BF16)
        pieces = []
        for p in range(channels // 128):
            cols = slice(128 * p, 128 * p + 128)
            both = dot_tn(v[:, cols], kk[:, cols])
            pieces.append(jnp.where(lane < GROUP, both[0:GROUP], both[GROUP:128]))
        state = state * total + jnp.concatenate(pieces, 1)
        decay = decay * total
    whole[0:SUB, :] = state
    whole[SUB : SUB + 8, :] = jnp.broadcast_to(decay, (8, channels))
    packed[0:SUB, :] = state.astype(BF16)
    high = decay.astype(BF16)
    low = (decay - high.astype(F32)).astype(BF16)
    packed[SUB : SUB + 8, :] = jnp.broadcast_to(high, (8, channels))
    packed[SUB + 8 : SUB + 16, :] = jnp.broadcast_to(low, (8, channels))


SMEM = pl.BlockSpec(memory_space=pltpu.SMEM)
VMEM = pl.BlockSpec(memory_space=pltpu.VMEM)


def shard_states(where, sums, ks, vs, ws):
    channels = ks[0].shape[1]
    return pl.pallas_call(
        states_kernel,
        in_specs=[SMEM] + [VMEM] * 13,
        out_specs=[VMEM] * 3,
        out_shape=[
            jax.ShapeDtypeStruct((8, SUB, channels), BF16),
            jax.ShapeDtypeStruct((SUB + 8, channels), F32),
            jax.ShapeDtypeStruct((SUB + 16, channels), BF16),
        ],
        compiler_params=pltpu.CompilerParams(vmem_limit_bytes=32 * 1024 * 1024),
        cost_estimate=pl.CostEstimate(flops=10**9, bytes_accessed=4 * 10**6, transcendentals=0),
    )(where, sums, *ks, *vs, *ws)


def local_kernel(where_ref, sums, reward, entering, *refs):
    rs, ks, vs, ws = refs[0:4], refs[4:8], refs[8:12], refs[12:16]
    local, queries = refs[16:]
    start = where_ref[1]
    channels = rs[0].shape[1]
    line = lax.broadcasted_iota(jnp.int32, (SUB, 1), 0)
    lane = lax.broadcasted_iota(jnp.int32, (SUB, 128), 1)
    two_t = lax.broadcasted_iota(jnp.int32, (2 * SUB, SUB), 0) % SUB
    two_s = lax.broadcasted_iota(jnp.int32, (2 * SUB, SUB), 1)
    before = jnp.zeros((1, channels), F32)

    def apart(a):
        zero = jnp.zeros_like(a)
        return jnp.concatenate([jnp.where(lane < GROUP, a, zero), jnp.where(lane < GROUP, zero, a)], 0)

    for c in range(8):
        rows = slice(SUB * (c % 2), SUB * (c % 2) + SUB)
        w = jnp.maximum(ws[c // 2][rows, :], FLOOR)
        r = rs[c // 2][rows, :]
        k = ks[c // 2][rows, :]
        v = vs[c // 2][rows, :].astype(BF16)
        sides = []
        exponents = dot(sums[0 : 7 * SUB, :], split_two(w))
        for level, half in enumerate(HALVES):
            right = (line // half) % 2 == 1
            e = jnp.exp(exponents[SUB * level : SUB * level + SUB, :])
            sides.append((jnp.where(right, r, k) * e).astype(BF16))
        before_here = exponents[6 * SUB : 7 * SUB, :]
        late = (line + c * SUB) >= start
        begins_late = (c * SUB - 1) >= start if c else jnp.bool_(False)
        reach = jnp.where(late == begins_late, r * jnp.exp(before_here), 0.0).astype(BF16)
        queries[SUB * c : SUB * c + SUB, :] = jnp.where(late, 0.0, r * jnp.exp(before + before_here)).astype(BF16)
        before = before + before_here[SUB - 1 : SUB, :] + w[SUB - 1 : SUB, :]
        own = (r * reward[...]).astype(BF16)
        k_own = k.astype(BF16)
        same = ((two_t + c * SUB) >= start) == ((two_s + c * SUB) >= start)
        for p in range(channels // 128):
            cols = slice(128 * p, 128 * p + 128)
            scores = jnp.where(two_t == two_s, dot_nt(apart(own[:, cols]), k_own[:, cols]), 0.0)
            for level, half in enumerate(HALVES):
                side = sides[level][:, cols]
                part = dot_nt(apart(side), side)
                here = (two_t // (2 * half) == two_s // (2 * half)) & ((two_t // half) % 2 == 1) & ((two_s // half) % 2 == 0)
                scores = jnp.where(here & same, part, scores)
            both = dot(scores.astype(BF16), v[:, cols])
            out = jnp.where(lane < GROUP, both[0:SUB], both[SUB : 2 * SUB])
            out = out + dot_nt(reach[:, cols], apart(entering[c, :, cols]))
            local[SUB * c : SUB * c + SUB, cols] = out


def local_outputs(where, sums, reward, entering, rs, ks, vs, ws):
    channels = ks[0].shape[1]
    tokens = CHUNK * len(ks)
    return pl.pallas_call(
        local_kernel,
        in_specs=[SMEM] + [VMEM] * 19,
        out_specs=[VMEM] * 2,
        out_shape=[
            jax.ShapeDtypeStruct((tokens, channels), F32),
            jax.ShapeDtypeStruct((tokens, channels), BF16),
        ],
        compiler_params=pltpu.CompilerParams(vmem_limit_bytes=40 * 1024 * 1024),
        cost_estimate=pl.CostEstimate(flops=6 * 10**9, bytes_accessed=6 * 10**6, transcendentals=0),
    )(where, sums, reward, entering, *rs, *ks, *vs, *ws)


def finish_kernel(local, queries, incoming, gain, shift, out):
    channels = local.shape[1]
    lane = lax.broadcasted_iota(jnp.int32, (SUB, 128), 1)
    row = lax.broadcasted_iota(jnp.int32, (128, 128), 0)
    col = lax.broadcasted_iota(jnp.int32, (128, 128), 1)
    average = jnp.where((row // GROUP) == (col // GROUP), 1.0 / GROUP, 0.0).astype(BF16)
    for p in range(channels // 128):
        cols = slice(128 * p, 128 * p + 128)
        st = incoming[:, cols].astype(BF16)
        zero = jnp.zeros_like(st)
        st = jnp.concatenate([jnp.where(lane < GROUP, st, zero), jnp.where(lane < GROUP, zero, st)], 0)
        o = local[:, cols] + dot_nt(queries[:, cols], st)
        high = o.astype(BF16)
        low = (o - high.astype(F32)).astype(BF16)
        centred = o - (dot(high, average) + dot(low, average))
        square = centred * centred
        high = square.astype(BF16)
        low = (square - high.astype(F32)).astype(BF16)
        variance = dot(high, average) + dot(low, average)
        normed = centred * lax.rsqrt(variance + 0.00064)
        out[:, cols] = (normed * gain[:, cols] + shift[:, cols]).astype(BF16)


def finish(local, queries, incoming, gain, shift):
    return pl.pallas_call(
        finish_kernel,
        in_specs=[VMEM] * 5,
        out_specs=VMEM,
        out_shape=jax.ShapeDtypeStruct(local.shape, BF16),
        compiler_params=pltpu.CompilerParams(vmem_limit_bytes=32 * 1024 * 1024),
        cost_estimate=pl.CostEstimate(flops=10**9, bytes_accessed=2 * 10**6, transcendentals=0),
    )(local, queries, incoming, gain, shift)


def unpack(packed):
    decay = packed[SUB : SUB + 1].astype(F32) + packed[SUB + 8 : SUB + 9].astype(F32)
    return decay, packed[0:SUB].astype(F32)


def pack(decay, state):
    high = decay.astype(BF16)
    low = (decay - high.astype(F32)).astype(BF16)
    wide = (8, decay.shape[1])
    return jnp.concatenate([state.astype(BF16), jnp.broadcast_to(high, wide), jnp.broadcast_to(low, wide)], 0)


def combine(earlier, later):
    return earlier[0] * later[0], later[0] * earlier[1] + later[1]


def choose(flag, a, b):
    return jax.tree.map(lambda u, v: jnp.where(flag, u, v), a, b)


def incoming_state(whole, packed):
    own = (whole[SUB : SUB + 1], whole[0:SUB])
    start = (jnp.ones_like(own[0]), jnp.zeros_like(own[1]))
    before = start
    for axis in reversed(SEQ):
        length, here = lax.axis_size(axis), lax.axis_index(axis)
        pieces = [own] + [unpack(xor_permute(packed, axis, k)) for k in range(1, length)]
        inside, so_far = start, start
        for m in range(length):
            from_m = pieces[m]
            for other in range(1, length):
                from_m = choose(here == other, pieces[m ^ other], from_m)
            inside = choose(m == here, so_far, inside)
            so_far = combine(so_far, from_m)
        before = combine(inside, before)
        own = so_far
        packed = pack(*own)
    return before[1]


def body(
    layer_inputs,
    article_opening,
    blending_ratios,
    blending_narrow_operand,
    blending_widen_operand,
    fading_narrow_operand,
    fading_widen_operand,
    fading_anchor,
    immediate_reward,
    acceptance_weights,
    lookup_weights,
    payload_weights,
    group_scaling_weight,
    group_scaling_shift,
):
    x = layer_inputs
    channels = fading_anchor.shape[0]
    where = jnp.stack([lax.axis_index(MP).astype(jnp.int32), article_opening[0]])
    shards = lax.axis_size(SEQ)

    def across_far(a):
        return lax.ppermute(a, ("y_hi", "y_lo"), [(i, i ^ 3) for i in range(4)])

    def partner(a):
        return xor_permute(a, MP, 1)

    def across(a):
        return xor_permute(a, MP, 2)

    part = [x[128 * c : 128 * c + 128] for c in range(4)]
    before = lax.ppermute(x[-CTX:], SEQ, [(i, i + 1) for i in range(shards - 1)])
    far_a = across(jnp.concatenate([part[1], x[128 - CTX : 128]], 0))
    far_narrow = across_far(blending_narrow_operand)
    near = partner(x)
    far_b = across(part[2])
    far_c = across(part[3])
    far_d = across(jnp.concatenate([part[0], before], 0))
    far_fading = across_far(fading_narrow_operand)
    narrows = [blending_narrow_operand, partner(blending_narrow_operand), far_narrow, partner(far_narrow)]
    fadings = [fading_narrow_operand, partner(fading_narrow_operand), far_fading, partner(far_fading)]
    near_before = partner(before)
    far = [far_d, far_a, far_b, far_c]
    cross = [partner(f) for f in far]
    done = [None] * 4
    for c in (1, 2, 3, 0):
        mains = [(x, c), (near, c), (far[c], 0), (cross[c], 0)]
        if c == 0:
            ctxs = [(before, 0), (near_before, 0), (far[0], 8), (cross[0], 8)]
        elif c == 1:
            ctxs = [(x, 7), (near, 7), (far[1], 8), (cross[1], 8)]
        else:
            ctxs = [(x, 8 * c - 1), (near, 8 * c - 1), (far[c - 1], 7), (cross[c - 1], 7)]
        done[c] = project(
            where, CHUNK * c, mains, ctxs, narrows, fadings, blending_ratios, blending_widen_operand,
            acceptance_weights, lookup_weights, payload_weights, fading_widen_operand, fading_anchor[None],
        )
    rs, ks, vs, ws = zip(*done)
    sums = jnp.asarray(sum_rows(), BF16)
    entering, whole, packed = shard_states(where, sums, ks, vs, ws)
    local, queries = local_outputs(where, sums, immediate_reward[None], entering, rs, ks, vs, ws)
    incoming = incoming_state(whole, packed)
    return finish(local, queries, incoming, group_scaling_weight[None], group_scaling_shift[None])


def solution(mesh):
    torus = Mesh(mesh.devices.reshape(4, 4, 2, 2, 2), ("z", "x", "y_hi", "y_lo", "core"))
    placed = (
        P(SEQ, MP),
        P(SEQ),
        P(),
        P(MP, None),
        P(),
        P(MP, None),
        P(None, MP),
        P(MP),
        P(MP),
        P(None, MP),
        P(None, MP),
        P(None, MP),
        P(MP),
        P(MP),
    )
    return jax.shard_map(body, mesh=torus, in_specs=placed, out_specs=P(SEQ, MP), check_vma=False)
```

time: 368 us -> 146 us (0.40)
  other arithmetic: 99 us -> 0.68 us
  matrix products: 71.8 us -> 0 us
  blocking collectives: 71 us -> 0 us
  Pallas kernels: 0 us -> 60.4 us
  local copies, waits for them, and re-layouts: 57.4 us -> 20.7 us
  waiting for transfers between devices: 44.6 us -> 34.6 us
  starting transfers between devices: 16.8 us -> 26.2 us
    dot_general x10 -> x0, matrix products: 71.8 us -> none  [the longest x1 11 us: body(): jnp.einsum('nshi,nshj->nhij', lookup_mapped * tail_weight, value_projecte...]
    all_gather x6 -> x0, blocking collectives: 71 us -> none  [entering_2(): pieces = jax.tree.map(lambda part: lax.all_gather(part, axis), so_far)]
    pallas_call x0 -> x7, Pallas kernels: none -> 60.4 us  [the longest x4 47 us: project(): pl.pallas_call(functools.partial(project_kernel, first_token=first_token)...]
    reduce_sum x4 -> x0, other arithmetic: 50.6 us -> none  [the longest x1 43.7 us: body(): jnp.sum(pair_decay * acceptance_lines[:, :, None] * lookup_mapped[:, None...]
    all_to_all x2 -> x0, waiting for transfers between devices: 43.3 us -> none  [copy_for_each(): lax.all_to_all(jnp.broadcast_to(array[None], (length, *array.shape)), axi...]
    ppermute x1 -> x24, waiting for transfers between devices: 1.31 us -> 34.6 us  [the longest x21 23.9 us: xor_permute(): return lax.ppermute(array, axes, [(i, i ^ flip) for i in range(length)])]
    ppermute x1 -> x24, starting transfers between devices: 4.19 us -> 26.2 us  [the longest x21 20.3 us: xor_permute(): return lax.ppermute(array, axes, [(i, i ^ flip) for i in range(length)])]
    add x18 -> x1, other arithmetic: 18.4 us -> 0.26 us  [combine(): return (earlier[0] * later[0], later[0] * earlier[1] + later[1])]
  transfers between devices with their start and end apart: 3 -> 24, of which waited for: 2 -> 9; matrix products, arithmetic and copies ran while one was open for 11% -> 1% of each run, Pallas kernels for 0% -> 31%
where the time goes in v1:
time: 146 us; the launch traced here: 144 us
  Pallas kernels  60.4 us (41%)
  waiting for transfers between devices  34.6 us (24%)
  starting transfers between devices  26.2 us (18%)
  local copies, waits for them, and re-layouts  20.7 us (14%)
    pallas_call x4, Pallas kernels, project(): pl.pallas_call(functools.partial(project_kernel, first_token=first_token)...  47 us
    ppermute x21, waiting for transfers between devices, xor_permute(): return lax.ppermute(array, axes, [(i, i ^ flip) for i in range(length)])  23.9 us
    ppermute x21, starting transfers between devices, xor_permute(): return lax.ppermute(array, axes, [(i, i ^ flip) for i in range(length)])  20.3 us
    unnamed x90, local copies, waits for them, and re-layouts  18.6 us
    pallas_call x1, Pallas kernels, local_outputs(): pl.pallas_call(local_kernel, in_specs=[SMEM] + [VMEM] * 19, out_specs=[VM...  8.78 us
    ppermute x2, waiting for transfers between devices, across_far(): return lax.ppermute(a, ('y_hi', 'y_lo'), [(i, i ^ 3) for i in range(4)])  8.34 us
    ppermute x1, starting transfers between devices, body(): lax.ppermute(x[-CTX:], SEQ, [(i, i + 1) for i in range(shards - 1)])  3.87 us
  transfers between devices with their start and end apart: 24, of which 9 were waited for; matrix products, arithmetic and copies ran while one was open for 1% of the time, Pallas kernels for 31%

profile of v1, /device:TPU:8, one launch (start us, length us, event | category | flops | bytes accessed | tf_op | source)
XLA Modules:
  0.0 143.7 jit_solution(16535287604082994356)
XLA Ops:
  0.0 1.6 %collective-permute-start.6 = (bf16[1024,256]{1,0:T(8,128)(2,1)}, bf16[1024,256]{1,0:T(8,128)(2,1)S(1)}, u32[]{:S(2)}, u32[]{:S(2)}) collective-permute-start(bf16[1024,256]{1,0:T(8,128)(2,1)} %refs_8_.7), channel_id=1, source_target_pairs={{0,6},{2,4},{4,2},{6,0},{1,7},{3,5},{5,3},{7,1},{8,14},{10,12},{12... | collective-permute-start | bytes 1572872 | tf_op jit(solution)/shard_map/ppermute | solution.py:397
  3.3 1.6 %collective-permute-start.13 = (bf16[128,1024]{1,0:T(8,128)(2,1)S(1)}, bf16[128,1024]{1,0:T(8,128)(2,1)S(1)}, u32[]{:S(2)}, u32[]{:S(2)}) collective-permute-start(bf16[128,1024]{1,0:T(8,128)(2,1)S(1)} %get-tuple-element.66), channel_id=1, source_target_pairs={{0,2},{1,3},{2,0},{3,1},{4,6},{5,7},{6,4},{7,5},{8,10},{9,11},{10,... | collective-permute-start | bytes 786440 | tf_op jit(solution)/shard_map/ppermute | solution.py:26
  5.7 3.9 %collective-permute-start.1 = (bf16[16,1024]{1,0:T(8,128)(2,1)S(1)}, bf16[16,1024]{1,0:T(8,128)(2,1)S(1)}, u32[]{:S(2)}, u32[]{:S(2)}) collective-permute-start(bf16[16,1024]{1,0:T(8,128)(2,1)S(1)} %get-tuple-element.70), channel_id=1, source_target_pairs={{0,4},{4,8},{8,12},{12,16},{16,20},{20,24},{24,28},{28,32},{32,36}... | collective-permute-start | bytes 98312 | tf_op jit(solution)/shard_map/ppermute | solution.py:406
  9.6 2.3 %collective-permute-done.1.refs_4_ = bf16[16,1024]{1,0:T(8,128)(2,1)S(1)} collective-permute-done((bf16[16,1024]{1,0:T(8,128)(2,1)S(1)}, bf16[16,1024]{1,0:T(8,128)(2,1)S(1)}, u32[]{:S(2)}, u32[]{:S(2)}) %collective-permute-start.1) | collective-permute-done | bytes 32800 | tf_op jit(solution)/shard_map/ppermute | solution.py:406
  11.9 8.3 %collective-permute-done.9.refs_14_ = bf16[1024,128]{1,0:T(8,128)(2,1)S(1)} collective-permute-done((bf16[1024,128]{1,0:T(8,128)(2,1)}, bf16[1024,128]{1,0:T(8,128)(2,1)S(1)}, u32[]{:S(2)}, u32[]{:S(2)}) %collective-permute-start.9) | collective-permute-done | bytes 262176 | tf_op jit(solution)/shard_map/ppermute | solution.py:397
  20.2 1.7 %collective-permute-start.15 = (bf16[128,1024]{1,0:T(8,128)(2,1)S(1)}, bf16[128,1024]{1,0:T(8,128)(2,1)S(1)}, u32[]{:S(2)}, u32[]{:S(2)}) collective-permute-start(bf16[128,1024]{1,0:T(8,128)(2,1)S(1)} %get-tuple-element.65), channel_id=1, source_target_pairs={{0,2},{1,3},{2,0},{3,1},{4,6},{5,7},{6,4},{7,5},{8,10},{9,11},{10,... | collective-permute-start | bytes 786440 | tf_op jit(solution)/shard_map/ppermute | solution.py:26
  22.4 1.8 %collective-permute-start.2 = (bf16[144,1024]{1,0:T(8,128)(2,1)S(1)}, bf16[144,1024]{1,0:T(8,128)(2,1)S(1)}, u32[]{:S(2)}, u32[]{:S(2)}) collective-permute-start(bf16[144,1024]{1,0:T(8,128)(2,1)S(1)} %pad_maximum_fusion), channel_id=1, source_target_pairs={{0,2},{1,3},{2,0},{3,1},{4,6},{5,7},{6,4},{7,5},{8,10},{9,11},{10,... | collective-permute-start | bytes 884744 | tf_op jit(solution)/shard_map/ppermute | solution.py:26
  24.2 5.2 %collective-permute-done.15.refs_2_ = bf16[128,1024]{1,0:T(8,128)(2,1)S(1)} collective-permute-done((bf16[128,1024]{1,0:T(8,128)(2,1)S(1)}, bf16[128,1024]{1,0:T(8,128)(2,1)S(1)}, u32[]{:S(2)}, u32[]{:S(2)}) %collective-permute-start.15) | collective-permute-done | bytes 262176 | tf_op jit(solution)/shard_map/ppermute | solution.py:26
  29.9 5.8 %collective-permute-done.11.refs_2_.refs_6_ = bf16[144,1024]{1,0:T(8,128)(2,1)S(1)} collective-permute-done((bf16[144,1024]{1,0:T(8,128)(2,1)S(1)}, bf16[144,1024]{1,0:T(8,128)(2,1)S(1)}, u32[]{:S(2)}, u32[]{:S(2)}) %collective-permute-start.11) | collective-permute-done | bytes 294944 | tf_op jit(solution)/shard_map/ppermute | solution.py:26
  35.7 4.5 %collective-permute-done.2.refs_2_.refs_6_ = bf16[144,1024]{1,0:T(8,128)(2,1)S(1)} collective-permute-done((bf16[144,1024]{1,0:T(8,128)(2,1)S(1)}, bf16[144,1024]{1,0:T(8,128)(2,1)S(1)}, u32[]{:S(2)}, u32[]{:S(2)}) %collective-permute-start.2) | collective-permute-done | bytes 294944 | tf_op jit(solution)/shard_map/ppermute | solution.py:26
  48.5 11.7 %shard_map.146 = (f32[128,512]{1,0:T(8,128)S(1)}, f32[128,512]{1,0:T(8,128)S(1)}, f32[128,512]{1,0:T(8,128)S(1)}, f32[128,512]{1,0:T(8,128)S(1)}) custom-call(s32[2]{0:T(128)S(1)} %pad_add_fusion.where_ref, bf16[512,1024]{1,0:T(8,128)(2,1)S(1)} %copy-done, bf16[512,1024]{1,0:T(8,128)(2,1)} %collective-permute-done.refs_1_.refs_5_, ...), custom_call_target="tpu_custom_call" | custom-call | flops 3000000000 | bytes 17000000 | tf_op jit(solution)/shard_map/pallas_call | solution.py:147
  60.9 11.8 %shard_map.147 = (f32[128,512]{1,0:T(8,128)S(1)}, f32[128,512]{1,0:T(8,128)S(1)}, f32[128,512]{1,0:T(8,128)S(1)}, f32[128,512]{1,0:T(8,128)S(1)}) custom-call(s32[2]{0:T(128)S(1)} %pad_add_fusion.where_ref, bf16[512,1024]{1,0:T(8,128)(2,1)} %refs_4_.5, bf16[512,1024]{1,0:T(8,128)(2,1)} %collective-permute-done.refs_1_.refs_5_, ...), custom_call_target="tpu_custom_call" | custom-call | flops 3000000000 | bytes 17000000 | tf_op jit(solution)/shard_map/pallas_call | solution.py:147
  73.6 11.9 %shard_map.148 = (f32[128,512]{1,0:T(8,128)S(1)}, f32[128,512]{1,0:T(8,128)S(1)}, f32[128,512]{1,0:T(8,128)S(1)}, f32[128,512]{1,0:T(8,128)S(1)}) custom-call(s32[2]{0:T(128)S(1)} %pad_add_fusion.where_ref, bf16[512,1024]{1,0:T(8,128)(2,1)} %refs_4_.5, bf16[512,1024]{1,0:T(8,128)(2,1)} %collective-permute-done.refs_1_.refs_5_, ...), custom_call_target="tpu_custom_call" | custom-call | flops 3000000000 | bytes 17000000 | tf_op jit(solution)/shard_map/pallas_call | solution.py:147
  85.5 11.7 %shard_map.145 = (f32[128,512]{1,0:T(8,128)S(1)}, f32[128,512]{1,0:T(8,128)S(1)}, f32[128,512]{1,0:T(8,128)S(1)}, f32[128,512]{1,0:T(8,128)S(1)}) custom-call(s32[2]{0:T(128)S(1)} %pad_add_fusion.where_ref, bf16[512,1024]{1,0:T(8,128)(2,1)S(1)} %copy-done.1, bf16[512,1024]{1,0:T(8,128)(2,1)} %collective-permute-done.refs_1_.refs_5_, ...), custom_call_target="tpu_custom_call" | custom-call | flops 3000000000 | bytes 17000000 | tf_op jit(solution)/shard_map/pallas_call | solution.py:147
  97.4 2.2 %shard_map.149 = (bf16[8,64,512]{2,1,0:T(8,128)(2,1)S(1)}, f32[72,512]{1,0:T(8,128)S(1)}, bf16[80,512]{1,0:T(8,128)(2,1)S(1)}) custom-call(s32[2]{0:T(128)S(1)} %pad_add_fusion.where_ref, bf16[512,128]{1,0:T(8,128)(2,1)S(1)} %copy-done.44, f32[128,512]{1,0:T(8,128)S(1)} %get-tuple-element.26.refs_0_.refs_4_, ...), custom_call_target="tpu_custom_call" | custom-call | flops 1000000000 | bytes 4000000 | tf_op jit(solution)/shard_map/pallas_call | solution.py:221
  99.6 3.4 %collective-permute-start.17 = (bf16[80,512]{1,0:T(8,128)(2,1)S(1)}, bf16[80,512]{1,0:T(8,128)(2,1)S(1)}, u32[]{:S(2)}, u32[]{:S(2)}) collective-permute-start(bf16[80,512]{1,0:T(8,128)(2,1)S(1)} %get-tuple-element.46), channel_id=1, source_target_pairs={{0,4},{4,0},{1,5},{5,1},{2,6},{6,2},{3,7},{7,3},{8,12},{12,8},{9,1... | collective-permute-start | bytes 245768 | tf_op jit(solution)/shard_map/ppermute | solution.py:26
  103.1 2.9 %collective-permute-done.17 = bf16[80,512]{1,0:T(8,128)(2,1)S(1)} collective-permute-done((bf16[80,512]{1,0:T(8,128)(2,1)S(1)}, bf16[80,512]{1,0:T(8,128)(2,1)S(1)}, u32[]{:S(2)}, u32[]{:S(2)}) %collective-permute-start.17) | collective-permute-done | bytes 81952 | tf_op jit(solution)/shard_map/ppermute | solution.py:26
  106.0 2.9 %collective-permute-start.18 = (bf16[80,512]{1,0:T(8,128)(2,1)S(1)}, bf16[80,512]{1,0:T(8,128)(2,1)S(1)}, u32[]{:S(2)}, u32[]{:S(2)}) collective-permute-start(bf16[80,512]{1,0:T(8,128)(2,1)S(1)} %pad_maximum_fusion.2), channel_id=1, source_target_pairs={{0,24},{8,16},{16,8},{24,0},{1,25},{9,17},{17,9},{25,1},{2,26},{10... | collective-permute-start | bytes 245768 | tf_op jit(solution)/shard_map/ppermute | solution.py:26
  110.2 1.6 %collective-permute-done.18 = bf16[80,512]{1,0:T(8,128)(2,1)S(1)} collective-permute-done((bf16[80,512]{1,0:T(8,128)(2,1)S(1)}, bf16[80,512]{1,0:T(8,128)(2,1)S(1)}, u32[]{:S(2)}, u32[]{:S(2)}) %collective-permute-start.18) | collective-permute-done | bytes 81952 | tf_op jit(solution)/shard_map/ppermute | solution.py:26
  111.8 3.2 %collective-permute-done.19 = bf16[80,512]{1,0:T(8,128)(2,1)S(1)} collective-permute-done((bf16[80,512]{1,0:T(8,128)(2,1)S(1)}, bf16[80,512]{1,0:T(8,128)(2,1)S(1)}, u32[]{:S(2)}, u32[]{:S(2)}) %collective-permute-start.19) | collective-permute-done | bytes 81952 | tf_op jit(solution)/shard_map/ppermute | solution.py:26
  115.2 2.0 %collective-permute-start.21 = (bf16[80,512]{1,0:T(8,128)(2,1)S(1)}, bf16[80,512]{1,0:T(8,128)(2,1)S(1)}, u32[]{:S(2)}, u32[]{:S(2)}) collective-permute-start(bf16[80,512]{1,0:T(8,128)(2,1)S(1)} %pad_maximum_fusion.3), channel_id=1, source_target_pairs={{0,32},{32,0},{64,96},{96,64},{1,33},{33,1},{65,97},{97,65},{2,34}... | collective-permute-start | bytes 245768 | tf_op jit(solution)/shard_map/ppermute | solution.py:26
  117.2 2.5 %collective-permute-start.22 = (bf16[80,512]{1,0:T(8,128)(2,1)S(1)}, bf16[80,512]{1,0:T(8,128)(2,1)S(1)}, u32[]{:S(2)}, u32[]{:S(2)}) collective-permute-start(bf16[80,512]{1,0:T(8,128)(2,1)S(1)} %pad_maximum_fusion.3), channel_id=1, source_target_pairs={{0,96},{32,64},{64,32},{96,0},{1,97},{33,65},{65,33},{97,1},{2,98}... | collective-permute-start | bytes 245768 | tf_op jit(solution)/shard_map/ppermute | solution.py:26
  132.2 8.8 %shard_map.150 = (f32[512,512]{1,0:T(8,128)S(1)}, bf16[512,512]{1,0:T(8,128)(2,1)S(1)}) custom-call(s32[2]{0:T(128)S(1)} %pad_add_fusion.where_ref, bf16[512,128]{1,0:T(8,128)(2,1)S(1)} %copy-done.44, f32[1,512]{1,0:T(1,128)S(1)} %bitcast.20, bf16[8,64,512]{2,1,0:T(8,128)(2,1)S(1)} %get-tuple-element.38.entering, f32[128,512]{1,0:T(8,128)S(1)} %copy-done.36, ...), custom_call_target="tpu_custom_call" | custom-call | flops 6000000000 | bytes 6000000 | tf_op jit(solution)/shard_map/pallas_call | solution.py:288
  141.4 2.3 %shard_map.151 = bf16[512,512]{1,0:T(8,128)(2,1)} custom-call(f32[512,512]{1,0:T(8,128)S(1)} %get-tuple-element.43.local, bf16[512,512]{1,0:T(8,128)(2,1)S(1)} %get-tuple-element.44.queries, f32[64,512]{1,0:T(8,128)S(1)} %fusion.8.incoming, f32[1,512]{1,0:T(1,128)S(1)} %bitcast.21, f32[1,512]{1,0:T(1,128)S(1)} %bitcast.22), custom_call_target="tpu_custom_call" | custom-call | flops 1000000000 | bytes 2000000 | tf_op jit(solution)/shard_map/pallas_call | solution.py:325
  (142 shorter events, 27.0 us)
Async XLA Ops:
  0.0 29.4 %collective-permute-start.6 = (bf16[1024,256]{1,0:T(8,128)(2,1)}, bf16[1024,256]{1,0:T(8,128)(2,1)S(1)}, u32[]{:S(2)}, u32[]{:S(2)}) collective-permute-start(bf16[1024,256]{1,0:T(8,128)(2,1)} %refs_8_.7), channel_id=1, source_target_pairs={{0,6},{2,4},{4,2},{6,0},{1,7},{3,5},{5,3},{7,1},{8,14},{10,12},{12... | collective-permute-start | bytes 1572872 | tf_op jit(solution)/shard_map/ppermute | solution.py:397
  1.6 18.6 %collective-permute-start.9 = (bf16[1024,128]{1,0:T(8,128)(2,1)}, bf16[1024,128]{1,0:T(8,128)(2,1)S(1)}, u32[]{:S(2)}, u32[]{:S(2)}) collective-permute-start(bf16[1024,128]{1,0:T(8,128)(2,1)} %refs_12_.7), channel_id=1, source_target_pairs={{0,6},{2,4},{4,2},{6,0},{1,7},{3,5},{5,3},{7,1},{8,14},{10,12},{12... | collective-permute-start | bytes 786440 | tf_op jit(solution)/shard_map/ppermute | solution.py:397
  2.0 40.7 %collective-permute-start = (bf16[512,1024]{1,0:T(8,128)(2,1)}, bf16[512,1024]{1,0:T(8,128)(2,1)}, u32[]{:S(2)}, u32[]{:S(2)}) collective-permute-start(bf16[512,1024]{1,0:T(8,128)(2,1)} %refs_4_.5), channel_id=1, source_target_pairs={{0,1},{1,0},{2,3},{3,2},{4,5},{5,4},{6,7},{7,6},{8,9},{9,8},{10,11... | collective-permute-start | bytes 3145736 | tf_op jit(solution)/shard_map/ppermute | solution.py:26
  3.3 18.7 %collective-permute-start.13 = (bf16[128,1024]{1,0:T(8,128)(2,1)S(1)}, bf16[128,1024]{1,0:T(8,128)(2,1)S(1)}, u32[]{:S(2)}, u32[]{:S(2)}) collective-permute-start(bf16[128,1024]{1,0:T(8,128)(2,1)S(1)} %get-tuple-element.66), channel_id=1, source_target_pairs={{0,2},{1,3},{2,0},{3,1},{4,6},{5,7},{6,4},{7,5},{8,10},{9,11},{10,... | collective-permute-start | bytes 786440 | tf_op jit(solution)/shard_map/ppermute | solution.py:26
  5.7 6.2 %collective-permute-start.1 = (bf16[16,1024]{1,0:T(8,128)(2,1)S(1)}, bf16[16,1024]{1,0:T(8,128)(2,1)S(1)}, u32[]{:S(2)}, u32[]{:S(2)}) collective-permute-start(bf16[16,1024]{1,0:T(8,128)(2,1)S(1)} %get-tuple-element.70), channel_id=1, source_target_pairs={{0,4},{4,8},{8,12},{12,16},{16,20},{20,24},{24,28},{28,32},{32,36}... | collective-permute-start | bytes 98312 | tf_op jit(solution)/shard_map/ppermute | solution.py:406
  11.9 10.5 %collective-permute-start.8 = (bf16[1024,128]{1,0:T(8,128)(2,1)}, bf16[1024,128]{1,0:T(8,128)(2,1)S(1)}, u32[]{:S(2)}, u32[]{:S(2)}) collective-permute-start(bf16[1024,128]{1,0:T(8,128)(2,1)} %refs_12_.7), channel_id=1, source_target_pairs={{0,1},{1,0},{2,3},{3,2},{4,5},{5,4},{6,7},{7,6},{8,9},{9,8},{10,11... | collective-permute-start | bytes 786440 | tf_op jit(solution)/shard_map/ppermute | solution.py:26
  20.2 9.2 %collective-permute-start.15 = (bf16[128,1024]{1,0:T(8,128)(2,1)S(1)}, bf16[128,1024]{1,0:T(8,128)(2,1)S(1)}, u32[]{:S(2)}, u32[]{:S(2)}) collective-permute-start(bf16[128,1024]{1,0:T(8,128)(2,1)S(1)} %get-tuple-element.65), channel_id=1, source_target_pairs={{0,2},{1,3},{2,0},{3,1},{4,6},{5,7},{6,4},{7,5},{8,10},{9,11},{10,... | collective-permute-start | bytes 786440 | tf_op jit(solution)/shard_map/ppermute | solution.py:26
  21.9 13.7 %collective-permute-start.11 = (bf16[144,1024]{1,0:T(8,128)(2,1)S(1)}, bf16[144,1024]{1,0:T(8,128)(2,1)S(1)}, u32[]{:S(2)}, u32[]{:S(2)}) collective-permute-start(bf16[144,1024]{1,0:T(8,128)(2,1)S(1)} %pad_maximum_fusion.1), channel_id=1, source_target_pairs={{0,2},{1,3},{2,0},{3,1},{4,6},{5,7},{6,4},{7,5},{8,10},{9,11},{10,... | collective-permute-start | bytes 884744 | tf_op jit(solution)/shard_map/ppermute | solution.py:26
  22.4 17.8 %collective-permute-start.2 = (bf16[144,1024]{1,0:T(8,128)(2,1)S(1)}, bf16[144,1024]{1,0:T(8,128)(2,1)S(1)}, u32[]{:S(2)}, u32[]{:S(2)}) collective-permute-start(bf16[144,1024]{1,0:T(8,128)(2,1)S(1)} %pad_maximum_fusion), channel_id=1, source_target_pairs={{0,2},{1,3},{2,0},{3,1},{4,6},{5,7},{6,4},{7,5},{8,10},{9,11},{10,... | collective-permute-start | bytes 884744 | tf_op jit(solution)/shard_map/ppermute | solution.py:26
  29.4 12.5 %collective-permute-start.5 = (bf16[1024,256]{1,0:T(8,128)(2,1)}, bf16[1024,256]{1,0:T(8,128)(2,1)S(1)}, u32[]{:S(2)}, u32[]{:S(2)}) collective-permute-start(bf16[1024,256]{1,0:T(8,128)(2,1)} %refs_8_.7), channel_id=1, source_target_pairs={{0,1},{1,0},{2,3},{3,2},{4,5},{5,4},{6,7},{7,6},{8,9},{9,8},{10,11... | collective-permute-start | bytes 1572872 | tf_op jit(solution)/shard_map/ppermute | solution.py:26
  29.4 13.0 %collective-permute-start.7 = (bf16[1024,256]{1,0:T(8,128)(2,1)S(1)}, bf16[1024,256]{1,0:T(8,128)(2,1)S(1)}, u32[]{:S(2)}, u32[]{:S(2)}) collective-permute-start(bf16[1024,256]{1,0:T(8,128)(2,1)S(1)} %collective-permute-done.6.refs_10_), channel_id=1, source_target_pairs={{0,1},{1,0},{2,3},{3,2},{4,5},{5,4},{6,7},{7,6},{8,9},{9,8},{10,11... | collective-permute-start | bytes 1572872 | tf_op jit(solution)/shard_map/ppermute | solution.py:26
  35.7 6.5 %collective-permute-start.12 = (bf16[144,1024]{1,0:T(8,128)(2,1)S(1)}, bf16[144,1024]{1,0:T(8,128)(2,1)S(1)}, u32[]{:S(2)}, u32[]{:S(2)}) collective-permute-start(bf16[144,1024]{1,0:T(8,128)(2,1)S(1)} %collective-permute-done.11.refs_2_.refs_6_), channel_id=1, source_target_pairs={{0,1},{1,0},{2,3},{3,2},{4,5},{5,4},{6,7},{7,6},{8,9},{9,8},{10,11... | collective-permute-start | bytes 884744 | tf_op jit(solution)/shard_map/ppermute | solution.py:26
  40.2 1.5 %collective-permute-start.10 = (bf16[1024,128]{1,0:T(8,128)(2,1)S(1)}, bf16[1024,128]{1,0:T(8,128)(2,1)S(1)}, u32[]{:S(2)}, u32[]{:S(2)}) collective-permute-start(bf16[1024,128]{1,0:T(8,128)(2,1)S(1)} %collective-permute-done.9.refs_14_), channel_id=1, source_target_pairs={{0,1},{1,0},{2,3},{3,2},{4,5},{5,4},{6,7},{7,6},{8,9},{9,8},{10,11... | collective-permute-start | bytes 786440 | tf_op jit(solution)/shard_map/ppermute | solution.py:26
  41.7 43.8 %collective-permute-start.4 = (bf16[16,1024]{1,0:T(8,128)(2,1)S(1)}, bf16[16,1024]{1,0:T(8,128)(2,1)S(1)}, u32[]{:S(2)}, u32[]{:S(2)}) collective-permute-start(bf16[16,1024]{1,0:T(8,128)(2,1)S(1)} %collective-permute-done.1.refs_4_), channel_id=1, source_target_pairs={{0,1},{1,0},{2,3},{3,2},{4,5},{5,4},{6,7},{7,6},{8,9},{9,8},{10,11... | collective-permute-start | bytes 98312 | tf_op jit(solution)/shard_map/ppermute | solution.py:26
  41.9 19.0 %collective-permute-start.14 = (bf16[128,1024]{1,0:T(8,128)(2,1)S(1)}, bf16[128,1024]{1,0:T(8,128)(2,1)S(1)}, u32[]{:S(2)}, u32[]{:S(2)}) collective-permute-start(bf16[128,1024]{1,0:T(8,128)(2,1)S(1)} %collective-permute-done.13.refs_2_.refs_6_), channel_id=1, source_target_pairs={{0,1},{1,0},{2,3},{3,2},{4,5},{5,4},{6,7},{7,6},{8,9},{9,8},{10,11... | collective-permute-start | bytes 786440 | tf_op jit(solution)/shard_map/ppermute | solution.py:26
  42.2 31.3 %collective-permute-start.16 = (bf16[128,1024]{1,0:T(8,128)(2,1)}, bf16[128,1024]{1,0:T(8,128)(2,1)S(1)}, u32[]{:S(2)}, u32[]{:S(2)}) collective-permute-start(bf16[128,1024]{1,0:T(8,128)(2,1)} %copy-done.10), channel_id=1, source_target_pairs={{0,1},{1,0},{2,3},{3,2},{4,5},{5,4},{6,7},{7,6},{8,9},{9,8},{10,11... | collective-permute-start | bytes 786440 | tf_op jit(solution)/shard_map/ppermute | solution.py:26
  42.4 43.1 %collective-permute-start.3 = (bf16[144,1024]{1,0:T(8,128)(2,1)S(1)}, bf16[144,1024]{1,0:T(8,128)(2,1)S(1)}, u32[]{:S(2)}, u32[]{:S(2)}) collective-permute-start(bf16[144,1024]{1,0:T(8,128)(2,1)S(1)} %collective-permute-done.2.refs_2_.refs_6_), channel_id=1, source_target_pairs={{0,1},{1,0},{2,3},{3,2},{4,5},{5,4},{6,7},{7,6},{8,9},{9,8},{10,11... | collective-permute-start | bytes 884744 | tf_op jit(solution)/shard_map/ppermute | solution.py:26
  99.6 6.3 %collective-permute-start.17 = (bf16[80,512]{1,0:T(8,128)(2,1)S(1)}, bf16[80,512]{1,0:T(8,128)(2,1)S(1)}, u32[]{:S(2)}, u32[]{:S(2)}) collective-permute-start(bf16[80,512]{1,0:T(8,128)(2,1)S(1)} %get-tuple-element.46), channel_id=1, source_target_pairs={{0,4},{4,0},{1,5},{5,1},{2,6},{6,2},{3,7},{7,3},{8,12},{12,8},{9,1... | collective-permute-start | bytes 245768 | tf_op jit(solution)/shard_map/ppermute | solution.py:26
  106.0 5.7 %collective-permute-start.18 = (bf16[80,512]{1,0:T(8,128)(2,1)S(1)}, bf16[80,512]{1,0:T(8,128)(2,1)S(1)}, u32[]{:S(2)}, u32[]{:S(2)}) collective-permute-start(bf16[80,512]{1,0:T(8,128)(2,1)S(1)} %pad_maximum_fusion.2), channel_id=1, source_target_pairs={{0,24},{8,16},{16,8},{24,0},{1,25},{9,17},{17,9},{25,1},{2,26},{10... | collective-permute-start | bytes 245768 | tf_op jit(solution)/shard_map/ppermute | solution.py:26
  108.9 6.1 %collective-permute-start.19 = (bf16[80,512]{1,0:T(8,128)(2,1)S(1)}, bf16[80,512]{1,0:T(8,128)(2,1)S(1)}, u32[]{:S(2)}, u32[]{:S(2)}) collective-permute-start(bf16[80,512]{1,0:T(8,128)(2,1)S(1)} %pad_maximum_fusion.2), channel_id=1, source_target_pairs={{0,16},{8,24},{16,0},{24,8},{1,17},{9,25},{17,1},{25,9},{2,18},{10... | collective-permute-start | bytes 245768 | tf_op jit(solution)/shard_map/ppermute | solution.py:26
  109.7 5.3 %collective-permute-start.20 = (bf16[80,512]{1,0:T(8,128)(2,1)S(1)}, bf16[80,512]{1,0:T(8,128)(2,1)S(1)}, u32[]{:S(2)}, u32[]{:S(2)}) collective-permute-start(bf16[80,512]{1,0:T(8,128)(2,1)S(1)} %pad_maximum_fusion.2), channel_id=1, source_target_pairs={{0,8},{8,0},{16,24},{24,16},{1,9},{9,1},{17,25},{25,17},{2,10},{10... | collective-permute-start | bytes 245768 | tf_op jit(solution)/shard_map/ppermute | solution.py:26
  115.2 25.8 %collective-permute-start.21 = (bf16[80,512]{1,0:T(8,128)(2,1)S(1)}, bf16[80,512]{1,0:T(8,128)(2,1)S(1)}, u32[]{:S(2)}, u32[]{:S(2)}) collective-permute-start(bf16[80,512]{1,0:T(8,128)(2,1)S(1)} %pad_maximum_fusion.3), channel_id=1, source_target_pairs={{0,32},{32,0},{64,96},{96,64},{1,33},{33,1},{65,97},{97,65},{2,34}... | collective-permute-start | bytes 245768 | tf_op jit(solution)/shard_map/ppermute | solution.py:26
  117.2 23.8 %collective-permute-start.22 = (bf16[80,512]{1,0:T(8,128)(2,1)S(1)}, bf16[80,512]{1,0:T(8,128)(2,1)S(1)}, u32[]{:S(2)}, u32[]{:S(2)}) collective-permute-start(bf16[80,512]{1,0:T(8,128)(2,1)S(1)} %pad_maximum_fusion.3), channel_id=1, source_target_pairs={{0,96},{32,64},{64,32},{96,0},{1,97},{33,65},{65,33},{97,1},{2,98}... | collective-permute-start | bytes 245768 | tf_op jit(solution)/shard_map/ppermute | solution.py:26
  119.7 21.3 %collective-permute-start.23 = (bf16[80,512]{1,0:T(8,128)(2,1)S(1)}, bf16[80,512]{1,0:T(8,128)(2,1)S(1)}, u32[]{:S(2)}, u32[]{:S(2)}) collective-permute-start(bf16[80,512]{1,0:T(8,128)(2,1)S(1)} %pad_maximum_fusion.3), channel_id=1, source_target_pairs={{0,64},{32,96},{64,0},{96,32},{1,65},{33,97},{65,1},{97,33},{2,66}... | collective-permute-start | bytes 245768 | tf_op jit(solution)/shard_map/ppermute | solution.py:26
  (45 other events, 427.8 us)

commit v2 on v1

v2 whole, which is shorter than its diff:
```python
import functools

import jax
import jax.numpy as jnp
import numpy as np
from jax import lax
from jax.experimental import pallas as pl
from jax.experimental.pallas import tpu as pltpu
from jax.sharding import Mesh
from jax.sharding import PartitionSpec as P


F32 = jnp.float32
BF16 = jnp.bfloat16
GROUP = 64
SUB = 64
LAST = 192
SPLIT = 160
CTX = 16
HALVES = (32, 16, 8, 4, 2, 1)
FLOOR = -100.0
SEQ = ("z", "x", "y_hi")
MP = ("y_lo", "core")


def xor_permute(array, axes, flip):
    length = lax.axis_size(axes)
    return lax.ppermute(array, axes, [(i, i ^ flip) for i in range(length)])


def dot(a, b):
    return jnp.dot(a, b, preferred_element_type=F32)


def dot_nt(a, b):
    return lax.dot_general(a, b, (((1,), (1,)), ((), ())), preferred_element_type=F32)


def dot_tn(a, b):
    return lax.dot_general(a, b, (((0,), (0,)), ((), ())), preferred_element_type=F32)


def sum_rows():
    t = np.arange(SUB)[:, None]
    j = np.arange(SUB)[None, :]
    blocks = []
    for half in HALVES:
        middle = (t // (2 * half)) * (2 * half) + half - 1
        right = t > middle
        blocks.append(np.where(right, (j > middle) & (j < t), (j > t) & (j <= middle)))
    blocks.append(j < t)
    blocks.append(j > t)
    one = np.concatenate(blocks, 0)
    return np.concatenate([one, one], 1).astype(np.float32)


SMEM = pl.BlockSpec(memory_space=pltpu.SMEM)
VMEM = pl.BlockSpec(memory_space=pltpu.VMEM)


def in_hbm(array):
    return pltpu.with_memory_space_constraint(array, pltpu.HBM)


def in_vmem(array):
    return pltpu.with_memory_space_constraint(array, pltpu.VMEM)


def load_kernel(where_ref, widen_far, w_r_far, w_k_far, w_v_far, *refs):
    count = (len(refs) - 5) // 2
    small_far, (widen, w_r, w_k, w_v), small, ready = refs[:count], refs[count : count + 4], refs[count + 4 : -1], refs[-1]
    width = w_r.shape[1]
    copies = [pltpu.make_async_copy(a, b, ready.at[4, i]) for i, (a, b) in enumerate(zip(small_far, small))]
    for j in range(4):
        there = pl.ds(pl.multiple_of((where_ref[0] ^ j) * width, width), width)
        copies.append(pltpu.make_async_copy(widen_far.at[:, :, there], widen.at[j], ready.at[j, 0]))
        for i, source, target in ((1, w_k_far, w_k), (2, w_v_far, w_v), (3, w_r_far, w_r)):
            copies.append(pltpu.make_async_copy(source.at[there, :], target.at[j], ready.at[j, i]))
    for copy in copies:
        copy.start()
    for copy in copies:
        copy.wait()


def load(where, widen, w_r, w_k, w_v, *small):
    channels = w_r.shape[1]
    width = w_r.shape[0] // 4
    return pl.pallas_call(
        load_kernel,
        in_specs=[SMEM] + [pl.BlockSpec(memory_space=pltpu.HBM)] * (4 + len(small)),
        out_specs=[VMEM] * (4 + len(small)),
        scratch_shapes=[pltpu.SemaphoreType.DMA((5, max(4, len(small))))],
        out_shape=[pltpu.VMEM((4, 4, 64, width), BF16)]
        + [pltpu.VMEM((4, width, channels), BF16)] * 3
        + [pltpu.VMEM(a.shape, a.dtype) for a in small],
        compiler_params=pltpu.CompilerParams(vmem_limit_bytes=2**20),
        cost_estimate=pl.CostEstimate(flops=5 * 10**9, bytes_accessed=15 * 10**6, transcendentals=0),
    )(where, *map(in_hbm, (widen, w_r, w_k, w_v, *small)))


def read_rows(refs, cols):
    parts = [ref[:, cols] for ref in refs]
    return parts[0] if len(parts) == 1 else jnp.concatenate(parts, 0)


def project_rows(me, start, first_token, pieces, narrows, fadings, weights, out, scratch):
    ratios, fade_widen, anchor, widen, w_r, w_k, w_v = weights
    diffs, mixed_a, mixed_b = scratch
    tokens, width = diffs.shape[1:]
    channels = w_r.shape[2]
    tile = 256
    line = lax.broadcasted_iota(jnp.int32, (tokens, tile), 0)
    first = line == 0
    opens = line + first_token == start

    rank = jnp.zeros((tokens, 256), F32)
    for j in range(4):
        base = (me ^ j) * width
        parts = []
        for n in range(width // tile):
            cols = slice(tile * n, tile * n + tile)
            rows = read_rows(pieces[j], cols).astype(F32)
            x = rows[CTX:]
            before = jnp.where(first, rows[CTX - 1 : CTX], pltpu.roll(x, 1, 0))
            d = jnp.where(opens, 0.0, before) - x
            diffs[j, :, cols] = d
            ratio = ratios[0:1, pl.ds(pl.multiple_of(base + tile * n, tile), tile)]
            parts.append((x + d * ratio).astype(BF16))
        rank = rank + dot(jnp.concatenate(parts, 1), narrows[j][...])
    total = jnp.tanh(rank).astype(BF16)
    hidden = [total[:, 64 * b : 64 * b + 64] for b in range(4)]

    def mix(j, mixed):
        base = (me ^ j) * width
        for n in range(width // tile):
            cols = slice(tile * n, tile * n + tile)
            there = pl.ds(pl.multiple_of(base + tile * n, tile), tile)
            x = read_rows(pieces[j], cols)[CTX:].astype(F32)
            d = diffs[j, :, cols]
            for b in range(4):
                delta = dot(hidden[b], widen[j, b, :, cols])
                mixed[b, :, cols] = (x + d * (ratios[b + 1 : b + 2, there] + delta)).astype(BF16)

    def project_piece(j, mixed, low):
        low = low + dot(mixed[0], fadings[j][...])
        for b, w, at in ((1, w_k, 1), (2, w_v, 2), (3, w_r, 0)):
            part = dot(mixed[b], w[j])
            cols = slice(channels * at, channels * at + channels)
            if j == 0:
                out[:, cols] = part
            else:
                out[:, cols] += part
        return low

    slots = (mixed_a, mixed_b)
    low = jnp.zeros((tokens, 128), F32)
    mix(0, slots[0])
    for j in range(4):
        if j < 3:
            mix(j + 1, slots[(j + 1) % 2])
        low = project_piece(j, slots[j % 2], low)
    low = jnp.tanh(low).astype(BF16)
    out[:, 3 * channels :] = -jnp.exp(anchor[...] + dot(low, fade_widen[...]))


def take_pieces(refs, counts):
    pieces = []
    for count in counts:
        pieces.append(refs[:count])
        refs = refs[count:]
    return pieces, refs


def late_kernel(where_ref, *refs, first_token, counts):
    pieces, refs = take_pieces(refs, counts)
    project_rows(where_ref[0], where_ref[1], first_token, pieces, refs[0:4], refs[4:8], refs[8:15], refs[15], refs[16:])


def early_kernel(where_ref, *refs, counts):
    pieces, refs = take_pieces(refs, counts)
    sums, late, out, entering, offsets, whole, packed = refs[15:22]
    project_rows(where_ref[0], where_ref[1], 0, pieces, refs[0:4], refs[4:8], refs[8:15], out, refs[22:])
    states(where_ref[1], sums, (out, late), entering, offsets, whole, packed)


def project_scratch(tokens, width):
    return [pltpu.VMEM((4, tokens, width), F32)] + [pltpu.VMEM((4, tokens, width), BF16)] * 2


def project_late(where, pieces, narrows, fadings, weights, tokens):
    width, channels = narrows[0].shape[0], weights[4].shape[2]
    counts = tuple(len(p) for p in pieces)
    operands = [a for p in pieces for a in p] + [*narrows, *fadings, *weights]
    return pl.pallas_call(
        functools.partial(late_kernel, first_token=LAST, counts=counts),
        in_specs=[SMEM] + [VMEM] * len(operands),
        out_specs=VMEM,
        scratch_shapes=project_scratch(tokens, width),
        out_shape=pltpu.VMEM((tokens, 4 * channels), F32),
        compiler_params=pltpu.CompilerParams(vmem_limit_bytes=(2 * 1024 + 48 * tokens) * 1024),
        cost_estimate=pl.CostEstimate(flops=25 * 10**6 * tokens, bytes_accessed=17 * 10**6, transcendentals=0),
    )(where, *operands[: -len(weights)], *map(in_vmem, weights))


def project_early(where, pieces, narrows, fadings, weights, sums, late):
    width, channels = narrows[0].shape[0], weights[4].shape[2]
    counts = tuple(len(p) for p in pieces)
    operands = [a for p in pieces for a in p] + [*narrows, *fadings, *weights, sums, late]
    return pl.pallas_call(
        functools.partial(early_kernel, counts=counts),
        in_specs=[SMEM] + [VMEM] * len(operands),
        out_specs=[VMEM] * 5,
        scratch_shapes=project_scratch(LAST, width),
        out_shape=[
            pltpu.VMEM((LAST, 4 * channels), F32),
            pltpu.VMEM((8, SUB, channels), BF16),
            pltpu.VMEM((8, channels), F32),
            jax.ShapeDtypeStruct((SUB + 8, channels), F32),
            jax.ShapeDtypeStruct((SUB + 16, channels), BF16),
        ],
        compiler_params=pltpu.CompilerParams(vmem_limit_bytes=(2 * 1024 + 48 * LAST) * 1024),
        cost_estimate=pl.CostEstimate(flops=25 * 10**6 * LAST, bytes_accessed=17 * 10**6, transcendentals=0),
    )(where, *operands[: -2 - len(weights)], *map(in_vmem, operands[-2 - len(weights) :]))


def split_two(w):
    high = w.astype(BF16)
    low = (w - high.astype(F32)).astype(BF16)
    return jnp.concatenate([high, low], 0)


def sub_chunk(chunks, c, channels):
    ref, at = (chunks[0], SUB * c) if SUB * c < LAST else (chunks[1], SUB * c - LAST)
    r, k, v, w = [ref[at : at + SUB, channels * i : channels * i + channels] for i in range(4)]
    return r, k, v.astype(BF16), jnp.maximum(w, FLOOR)


def states(start, sums, chunks, entering, offsets, whole, packed):
    channels = entering.shape[2]
    line = lax.broadcasted_iota(jnp.int32, (SUB, 1), 0)
    lane = lax.broadcasted_iota(jnp.int32, (SUB, 128), 1)
    state = jnp.zeros((SUB, channels), F32)
    decay = jnp.ones((1, channels), F32)
    offset = jnp.zeros((1, channels), F32)
    for c in range(8):
        _, k, v, w = sub_chunk(chunks, c, channels)
        tail = dot(sums[7 * SUB : 8 * SUB, :], split_two(w))
        ends_late = (c * SUB + SUB - 1) >= start
        begins_late = (c * SUB - 1) >= start if c else jnp.bool_(False)
        late = (line + c * SUB) >= start
        keep = late == ends_late
        log_total = tail[0:1, :] + w[0:1, :]
        total = jnp.where(begins_late == ends_late, jnp.exp(log_total), 0.0)
        offsets[c : c + 1, :] = offset
        offset = offset + log_total
        kk = jnp.where(keep, k * jnp.exp(tail), 0.0).astype(BF16)
        entering[c] = state.astype(BF16)
        pieces = []
        for p in range(channels // 128):
            cols = slice(128 * p, 128 * p + 128)
            both = dot_tn(v[:, cols], kk[:, cols])
            pieces.append(jnp.where(lane < GROUP, both[0:GROUP], both[GROUP:128]))
        state = state * total + jnp.concatenate(pieces, 1)
        decay = decay * total
    whole[0:SUB, :] = state
    whole[SUB : SUB + 8, :] = jnp.broadcast_to(decay, (8, channels))
    packed[0:SUB, :] = state.astype(BF16)
    high = decay.astype(BF16)
    low = (decay - high.astype(F32)).astype(BF16)
    packed[SUB : SUB + 8, :] = jnp.broadcast_to(high, (8, channels))
    packed[SUB + 8 : SUB + 16, :] = jnp.broadcast_to(low, (8, channels))


def local_kernel(where_ref, sums, reward, entering, offsets, chunk, local, queries, *, numbers, first_token):
    start = where_ref[1]
    channels = local.shape[1]
    line = lax.broadcasted_iota(jnp.int32, (SUB, 1), 0)
    lane = lax.broadcasted_iota(jnp.int32, (SUB, 128), 1)
    two_t = lax.broadcasted_iota(jnp.int32, (2 * SUB, SUB), 0) % SUB
    two_s = lax.broadcasted_iota(jnp.int32, (2 * SUB, SUB), 1)

    def apart(a):
        zero = jnp.zeros_like(a)
        return jnp.concatenate([jnp.where(lane < GROUP, a, zero), jnp.where(lane < GROUP, zero, a)], 0)

    for n, c in enumerate(numbers):
        at = SUB * c - first_token
        r, k, v, w = [chunk[at : at + SUB, channels * i : channels * i + channels] for i in range(4)]
        v = v.astype(BF16)
        w = jnp.maximum(w, FLOOR)
        sides = []
        exponents = dot(sums[0 : 7 * SUB, :], split_two(w))
        for level, half in enumerate(HALVES):
            right = (line // half) % 2 == 1
            e = jnp.exp(exponents[SUB * level : SUB * level + SUB, :])
            sides.append((jnp.where(right, r, k) * e).astype(BF16))
        before_here = exponents[6 * SUB : 7 * SUB, :]
        late = (line + c * SUB) >= start
        begins_late = (c * SUB - 1) >= start if c else jnp.bool_(False)
        reach = jnp.where(late == begins_late, r * jnp.exp(before_here), 0.0).astype(BF16)
        offset = offsets[c : c + 1, :]
        rows = slice(SUB * n, SUB * n + SUB)
        queries[rows, :] = jnp.where(late, 0.0, r * jnp.exp(offset + before_here)).astype(BF16)
        own = (r * reward[...]).astype(BF16)
        k_own = k.astype(BF16)
        same = ((two_t + c * SUB) >= start) == ((two_s + c * SUB) >= start)
        for p in range(channels // 128):
            cols = slice(128 * p, 128 * p + 128)
            scores = jnp.where(two_t == two_s, dot_nt(apart(own[:, cols]), k_own[:, cols]), 0.0)
            for level, half in enumerate(HALVES):
                side = sides[level][:, cols]
                part = dot_nt(apart(side), side)
                here = (two_t // (2 * half) == two_s // (2 * half)) & ((two_t // half) % 2 == 1) & ((two_s // half) % 2 == 0)
                scores = jnp.where(here & same, part, scores)
            both = dot(scores.astype(BF16), v[:, cols])
            out = jnp.where(lane < GROUP, both[0:SUB], both[SUB : 2 * SUB])
            local[rows, cols] = out + dot_nt(reach[:, cols], apart(entering[c, :, cols]))


def local_outputs(where, sums, reward, entering, offsets, chunk, numbers, first_token):
    channels = entering.shape[2]
    tokens = len(numbers) * SUB
    return pl.pallas_call(
        functools.partial(local_kernel, numbers=numbers, first_token=first_token),
        in_specs=[SMEM] + [VMEM] * 5,
        out_specs=[VMEM] * 2,
        out_shape=[pltpu.VMEM((tokens, channels), F32), pltpu.VMEM((tokens, channels), BF16)],
        compiler_params=pltpu.CompilerParams(vmem_limit_bytes=6 * 1024 * 1024),
        cost_estimate=pl.CostEstimate(flops=2 * 10**9, bytes_accessed=3 * 10**6, transcendentals=0),
    )(where, *map(in_vmem, (sums, reward, entering, offsets, chunk)))


def unpack(ref):
    return ref[SUB : SUB + 1].astype(F32) + ref[SUB + 8 : SUB + 9].astype(F32), ref[0:SUB].astype(F32)


def pack(ref, decay, state):
    high = decay.astype(BF16)
    low = (decay - high.astype(F32)).astype(BF16)
    wide = (8, decay.shape[1])
    ref[0:SUB, :] = state.astype(BF16)
    ref[SUB : SUB + 8, :] = jnp.broadcast_to(high, wide)
    ref[SUB + 8 : SUB + 16, :] = jnp.broadcast_to(low, wide)


def store(ref, decay, state):
    ref[0:SUB, :] = state
    ref[SUB : SUB + 8, :] = jnp.broadcast_to(decay, (8, decay.shape[1]))


def combine(earlier, later):
    return earlier[0] * later[0], later[0] * earlier[1] + later[1]


def choose(flag, a, b):
    return tuple(jnp.where(flag, u, v) for u, v in zip(a, b))


def along_axis(here, own, received, before):
    pieces = [own] + [unpack(ref) for ref in received]
    length = len(pieces)
    start = (jnp.ones_like(own[0]), jnp.zeros_like(own[1]))
    inside, so_far = start, None
    for m in range(length):
        from_m = pieces[m]
        for other in range(1, length):
            from_m = choose(here == other, pieces[m ^ other], from_m)
        if m:
            inside = choose(here == m, so_far, inside)
        so_far = from_m if so_far is None else combine(so_far, from_m)
    return inside if before is None else combine(inside, before), so_far


def merge_kernel(where_ref, *refs, place, count, opening):
    whole, refs = refs[0], refs[1:]
    before = None
    if not opening:
        before, refs = (refs[0][SUB : SUB + 1], refs[0][0:SUB]), refs[1:]
    received, (whole_out, packed_out, before_out) = refs[:count], refs[count:]
    own = (whole[SUB : SUB + 1], whole[0:SUB])
    before, total = along_axis(where_ref[place], own, received, before)
    store(whole_out, *total)
    pack(packed_out, *total)
    store(before_out, *before)


def merge(where, place, whole, before, received):
    channels = whole.shape[1]
    operands = [whole] + ([] if before is None else [before]) + received
    return pl.pallas_call(
        functools.partial(merge_kernel, place=place, count=len(received), opening=before is None),
        in_specs=[SMEM] + [VMEM] * len(operands),
        out_specs=[VMEM] * 3,
        out_shape=[
            jax.ShapeDtypeStruct((SUB + 8, channels), F32),
            jax.ShapeDtypeStruct((SUB + 16, channels), BF16),
            jax.ShapeDtypeStruct((SUB + 8, channels), F32),
        ],
        compiler_params=pltpu.CompilerParams(vmem_limit_bytes=4 * 1024 * 1024),
        cost_estimate=pl.CostEstimate(flops=10**8, bytes_accessed=10**6, transcendentals=0),
    )(where, *operands)


def finish_kernel(where_ref, *refs, parts, place):
    locals_, queries, refs = refs[:parts], refs[parts : 2 * parts], refs[2 * parts :]
    gain, shift, whole, before, *received, out, held, ready = refs
    own = (whole[SUB : SUB + 1], whole[0:SUB])
    (_, incoming), _ = along_axis(where_ref[place], own, received, (before[SUB : SUB + 1], before[0:SUB]))
    incoming = incoming.astype(BF16)
    channels = gain.shape[1]
    lane = lax.broadcasted_iota(jnp.int32, (SUB, 128), 1)
    row = lax.broadcasted_iota(jnp.int32, (128, 128), 0)
    col = lax.broadcasted_iota(jnp.int32, (128, 128), 1)
    average = jnp.where((row // GROUP) == (col // GROUP), 1.0 / GROUP, 0.0).astype(BF16)
    copies = []
    at = 0
    for i in range(parts):
        rows = slice(at, at + locals_[i].shape[0])
        at = rows.stop
        for p in range(channels // 128):
            cols = slice(128 * p, 128 * p + 128)
            st = incoming[:, cols]
            zero = jnp.zeros_like(st)
            st = jnp.concatenate([jnp.where(lane < GROUP, st, zero), jnp.where(lane < GROUP, zero, st)], 0)
            o = locals_[i][:, cols] + dot_nt(queries[i][:, cols], st)
            high = o.astype(BF16)
            low = (o - high.astype(F32)).astype(BF16)
            centred = o - (dot(high, average) + dot(low, average))
            square = centred * centred
            high = square.astype(BF16)
            low = (square - high.astype(F32)).astype(BF16)
            variance = dot(high, average) + dot(low, average)
            normed = centred * lax.rsqrt(variance + 0.00064)
            held[rows, cols] = (normed * gain[:, cols] + shift[:, cols]).astype(BF16)
        copies.append(pltpu.make_async_copy(held.at[rows, :], out.at[rows, :], ready.at[i]))
        copies[-1].start()
    for copy in copies:
        copy.wait()


def finish(where, place, locals_, queries, gain, shift, whole, before, received):
    parts = len(locals_)
    tokens, channels = sum(a.shape[0] for a in locals_), gain.shape[1]
    return pl.pallas_call(
        functools.partial(finish_kernel, parts=parts, place=place),
        in_specs=[SMEM] + [VMEM] * (2 * parts + 4 + len(received)),
        out_specs=pl.BlockSpec(memory_space=pltpu.HBM),
        scratch_shapes=[pltpu.VMEM((tokens, channels), BF16), pltpu.SemaphoreType.DMA((parts,))],
        out_shape=jax.ShapeDtypeStruct((tokens, channels), BF16),
        compiler_params=pltpu.CompilerParams(vmem_limit_bytes=6 * 1024 * 1024),
        cost_estimate=pl.CostEstimate(flops=10**9, bytes_accessed=2 * 10**6, transcendentals=0),
    )(where, *map(in_vmem, (*locals_, *queries, gain, shift)), whole, before, *received)


def inner(
    layer_inputs,
    article_opening,
    blending_ratios,
    blending_narrow_operand,
    blending_widen_operand,
    fading_narrow_operand,
    fading_widen_operand,
    fading_anchor,
    immediate_reward,
    acceptance_weights,
    lookup_weights,
    payload_weights,
    group_scaling_weight,
    group_scaling_shift,
):
    x = layer_inputs
    places = [lax.axis_index(axis).astype(jnp.int32) for axis in (MP, *SEQ)]
    where = jnp.stack([places[0], article_opening[0], *places[1:]])
    shards = lax.axis_size(SEQ)

    def across_far(a):
        return lax.ppermute(a, ("y_hi", "y_lo"), [(i, i ^ 3) for i in range(4)])

    def partner(a):
        return xor_permute(a, MP, 1)

    def across(a):
        return xor_permute(a, MP, 2)

    late_rows = x.shape[0] - LAST
    cut = LAST + SPLIT
    own_late = [x[LAST - CTX : cut], x[cut:]]
    far_late_a = across(own_late[0])
    far_narrow = across_far(blending_narrow_operand)
    near_narrow = partner(blending_narrow_operand)
    near_late_a = partner(own_late[0])
    before = lax.ppermute(x[-CTX:], SEQ, [(i, i + 1) for i in range(shards - 1)])
    far_late_b = across(own_late[1])
    near_late_b = partner(own_late[1])
    far_fading = across_far(fading_narrow_operand)
    near_fading = partner(fading_narrow_operand)
    own_early = jnp.concatenate([before, x[:LAST]], 0)
    far_early = across(own_early)
    near_early = partner(own_early)
    next_late_a = partner(far_late_a)
    next_narrow = partner(far_narrow)
    next_late_b = partner(far_late_b)
    next_fading = partner(far_fading)
    sums = jnp.asarray(sum_rows(), BF16)
    (widen, w_r, w_k, w_v, narrow, fading, ratios, fade_widen, anchor, sums, reward, gain, shift) = load(
        where, blending_widen_operand, acceptance_weights, lookup_weights, payload_weights,
        blending_narrow_operand, fading_narrow_operand, blending_ratios, fading_widen_operand, fading_anchor[None],
        sums, immediate_reward[None], group_scaling_weight[None], group_scaling_shift[None],
    )
    narrows = [narrow, near_narrow, far_narrow, next_narrow]
    fadings = [fading, near_fading, far_fading, next_fading]
    weights = (ratios, fade_widen, anchor, widen, w_r, w_k, w_v)
    pieces = [own_late, [near_late_a, near_late_b], [far_late_a, far_late_b], [next_late_a, next_late_b]]
    late = project_late(where, pieces, narrows, fadings, weights, late_rows)
    far_early, late = lax.optimization_barrier((far_early, late))
    next_early = partner(far_early)
    pieces = [[own_early], [near_early], [far_early], [next_early]]
    early, entering, offsets, whole, packed = project_early(where, pieces, narrows, fadings, weights, sums, late)
    outputs = []
    for chunk, numbers, first_token in ((early, (0, 1, 2), 0), (late, (3, 4), LAST), (late, (5, 6, 7), LAST)):
        outputs.append(local_outputs(where, sums, reward, entering, offsets, chunk, numbers, first_token))
    before = None
    for axis in reversed(SEQ):
        received = []
        for k in range(1, lax.axis_size(axis)):
            received.append(xor_permute(packed, axis, k))
        place = 2 + SEQ.index(axis)
        if axis != SEQ[0]:
            whole, packed, before = merge(where, place, whole, before, received)
    locals_, queries = zip(*outputs)
    return finish(where, place, locals_, queries, gain, shift, whole, before, received)


def solution(mesh):
    torus = Mesh(mesh.devices.reshape(4, 4, 2, 2, 2), ("z", "x", "y_hi", "y_lo", "core"))
    placed = (
        P(SEQ, MP),
        P(SEQ),
        P(),
        P(MP, None),
        P(),
        P(MP, None),
        P(None, MP),
        P(MP),
        P(MP),
        P(None, MP),
        P(None, MP),
        P(None, MP),
        P(MP),
        P(MP),
    )
    return jax.shard_map(inner, mesh=torus, in_specs=placed, out_specs=P(SEQ, MP), check_vma=False)
```

time: 146 us -> 88.5 us (0.61)
  Pallas kernels: 60.4 us -> 41.7 us
  local copies, waits for them, and re-layouts: 20.7 us -> 2.85 us
  waiting for transfers between devices: 34.6 us -> 18.8 us
  starting transfers between devices: 26.2 us -> 22.8 us
    pallas_call x7 -> x9, Pallas kernels: 60.4 us -> 41.7 us  [the longest x1 10.9 us: project_late(): pl.pallas_call(functools.partial(late_kernel, first_token=LAST, counts=co...]
    unnamed x90 -> x0, local copies, waits for them, and re-layouts: 18.6 us -> none
    ppermute x2, waiting for transfers between devices: 8.34 us -> 0.01 us  [across_far(): return lax.ppermute(a, ('y_hi', 'y_lo'), [(i, i ^ 3) for i in range(4)])]
    ppermute x21 -> x20, waiting for transfers between devices: 23.9 us -> 18.4 us  [xor_permute(): return lax.ppermute(array, axes, [(i, i ^ flip) for i in range(length)])]
    ppermute x21 -> x20, starting transfers between devices: 20.3 us -> 15.3 us  [xor_permute(): return lax.ppermute(array, axes, [(i, i ^ flip) for i in range(length)])]
    ppermute x1, waiting for transfers between devices: 2.28 us -> 0.35 us  [inner(): lax.ppermute(x[-CTX:], SEQ, [(i, i + 1) for i in range(shards - 1)])]
    ppermute x1, starting transfers between devices: 3.87 us -> 5.4 us  [inner(): lax.ppermute(x[-CTX:], SEQ, [(i, i + 1) for i in range(shards - 1)])]
  transfers between devices with their start and end apart: 24 -> 23, of which waited for: 9 -> 7; matrix products, arithmetic and copies ran while one was open for 1% -> 3% of each run, Pallas kernels for 31% -> 32%
where the time goes in v2:
time: 88.5 us; the launch traced here: 87.1 us
  Pallas kernels  41.7 us (47%)
  starting transfers between devices  22.8 us (26%)
  waiting for transfers between devices  18.8 us (21%)
  local copies, waits for them, and re-layouts  2.85 us (3%)
  between operations  0.99 us (1%)
    ppermute x20, waiting for transfers between devices, xor_permute(): return lax.ppermute(array, axes, [(i, i ^ flip) for i in range(length)])  18.4 us
    ppermute x20, starting transfers between devices, xor_permute(): return lax.ppermute(array, axes, [(i, i ^ flip) for i in range(length)])  15.3 us
    pallas_call x1, Pallas kernels, project_late(): pl.pallas_call(functools.partial(late_kernel, first_token=LAST, counts=co...  10.9 us
    pallas_call x3, Pallas kernels, local_outputs(): pl.pallas_call(functools.partial(local_kernel, numbers=numbers, first_tok...  10.6 us
    pallas_call x1, Pallas kernels, project_early(): pl.pallas_call(functools.partial(early_kernel, counts=counts), in_specs=[...  8.45 us
    pallas_call x1, Pallas kernels, load(): pl.pallas_call(load_kernel, in_specs=[SMEM] + [pl.BlockSpec(memory_space=...  6.54 us
    ppermute x1, starting transfers between devices, inner(): lax.ppermute(x[-CTX:], SEQ, [(i, i + 1) for i in range(shards - 1)])  5.4 us
    pallas_call x1, Pallas kernels, finish(): pl.pallas_call(functools.partial(finish_kernel, parts=parts, place=place)...  3.88 us
  transfers between devices with their start and end apart: 23, of which 7 were waited for; matrix products, arithmetic and copies ran while one was open for 3% of the time, Pallas kernels for 32%

profile of v2, /device:TPU:8, one launch (start us, length us, event | category | flops | bytes accessed | tf_op | source)
XLA Modules:
  0.0 87.1 jit_solution(15297169916024760275)
XLA Ops:
  0.0 1.6 %collective-permute-start.13 = (bf16[1024,128]{1,0:T(8,128)(2,1)}, bf16[1024,128]{1,0:T(8,128)(2,1)S(1)}, u32[]{:S(2)}, u32[]{:S(2)}) collective-permute-start(bf16[1024,128]{1,0:T(8,128)(2,1)} %refs_1_.1), channel_id=1, source_target_pairs={{0,6},{2,4},{4,2},{6,0},{1,7},{3,5},{5,3},{7,1},{8,14},{10,12},{12... | collective-permute-start | bytes 786440 | tf_op jit(solution)/shard_map/ppermute | solution.py:477
  2.0 0.8 slice.12
  2.8 5.4 %collective-permute-start = (bf16[16,1024]{1,0:T(8,128)(2,1)S(1)}, bf16[16,1024]{1,0:T(8,128)(2,1)S(1)}, u32[]{:S(2)}, u32[]{:S(2)}) collective-permute-start(bf16[16,1024]{1,0:T(8,128)(2,1)S(1)} %slice.12), channel_id=1, source_target_pairs={{0,4},{4,8},{8,12},{12,16},{16,20},{20,24},{24,28},{28,32},{32,36}... | collective-permute-start | bytes 98312 | tf_op jit(solution)/shard_map/ppermute | solution.py:492
  8.2 1.0 %slice.14.refs_0_ = bf16[176,1024]{1,0:T(8,128)(2,1)S(1)} slice(bf16[512,1024]{1,0:T(8,128)(2,1)} %param.15), slice={[176:352], [0:1024]} | slice | bytes 720896 | tf_op jit(solution)/shard_map/slice | solution.py:487
  9.8 1.0 %slice.15.refs_1_ = bf16[160,1024]{1,0:T(8,128)(2,1)S(1)} slice(bf16[512,1024]{1,0:T(8,128)(2,1)} %param.15), slice={[352:512], [0:1024]} | slice | bytes 655360 | tf_op jit(solution)/shard_map/slice | solution.py:487
  10.8 1.6 %collective-permute-start.6 = (bf16[160,1024]{1,0:T(8,128)(2,1)S(1)}, bf16[160,1024]{1,0:T(8,128)(2,1)S(1)}, u32[]{:S(2)}, u32[]{:S(2)}) collective-permute-start(bf16[160,1024]{1,0:T(8,128)(2,1)S(1)} %slice.15.refs_1_), channel_id=1, source_target_pairs={{0,2},{1,3},{2,0},{3,1},{4,6},{5,7},{6,4},{7,5},{8,10},{9,11},{10,... | collective-permute-start | bytes 983048 | tf_op jit(solution)/shard_map/ppermute | solution.py:28
  13.4 13.2 %collective-permute-done.6.refs_5_ = bf16[160,1024]{1,0:T(8,128)(2,1)S(1)} collective-permute-done((bf16[160,1024]{1,0:T(8,128)(2,1)S(1)}, bf16[160,1024]{1,0:T(8,128)(2,1)S(1)}, u32[]{:S(2)}, u32[]{:S(2)}) %collective-permute-start.6) | collective-permute-done | bytes 327712 | tf_op jit(solution)/shard_map/ppermute | solution.py:28
  27.7 6.5 %shard_map.145 = (bf16[4,4,64,1024]{3,2,1,0:T(8,128)(2,1)S(1)}, bf16[4,1024,512]{2,1,0:T(8,128)(2,1)S(1)}, bf16[4,1024,512]{2,1,0:T(8,128)(2,1)S(1)}, bf16[4,102...) custom-call(s32[5]{0:T(128)S(1)} %stack.19.where_ref, ...), custom_call_target="tpu_custom_call" | custom-call | flops 5000000000 | bytes 15000000 | tf_op jit(solution)/shard_map/pallas_call | solution.py:88
  35.1 10.9 %shard_map.146.refs_20_.chunk = f32[320,2048]{1,0:T(8,128)S(1)} custom-call(s32[5]{0:T(128)S(1)} %stack.19.where_ref, bf16[176,1024]{1,0:T(8,128)(2,1)S(1)} %slice.14.refs_0_, bf16[160,1024]{1,0:T(8,128)(2,1)S(1)} %slice.15.refs_1_, bf16[176,1024]{1,0:T(8,128)(2,1)S(1)} %collective-permute-done.3.refs_2_, ...), custom_call_target="tpu_custom_call" | custom-call | flops 8000000000 | bytes 17000000 | tf_op jit(solution)/shard_map/pallas_call | solution.py:194
  46.5 1.8 %collective-permute-done.15.refs_3_ = bf16[208,1024]{1,0:T(8,128)(2,1)S(1)} collective-permute-done((bf16[208,1024]{1,0:T(8,128)(2,1)S(1)}, bf16[208,1024]{1,0:T(8,128)(2,1)S(1)}, u32[]{:S(2)}, u32[]{:S(2)}) %collective-permute-start.15) | collective-permute-done | bytes 426016 | tf_op jit(solution)/shard_map/ppermute | solution.py:28
  48.3 8.5 %shard_map.147 = (f32[192,2048]{1,0:T(8,128)S(1)}, bf16[8,64,512]{2,1,0:T(8,128)(2,1)S(1)}, f32[8,512]{1,0:T(8,128)S(1)}, f32[72,512]{1,0:T(8,128)S(1)}, bf16[80,512]{1,0:T(8,128)(2,1)S(1)}) custom-call(s32[5]{0:T(128)S(1)} %stack.19.where_ref, bf16[208,1024]{1,0:T(8,128)(2,1)S(1)} %pad_maximum_fusion.refs_0_, ...), custom_call_target="tpu_custom_call" | custom-call | flops 4800000000 | bytes 17000000 | tf_op jit(solution)/shard_map/pallas_call | solution.py:209
  56.8 2.1 %collective-permute-start.16 = (bf16[80,512]{1,0:T(8,128)(2,1)S(1)}, bf16[80,512]{1,0:T(8,128)(2,1)S(1)}, u32[]{:S(2)}, u32[]{:S(2)}) collective-permute-start(bf16[80,512]{1,0:T(8,128)(2,1)S(1)} %get-tuple-element.62), channel_id=1, source_target_pairs={{0,4},{4,0},{1,5},{5,1},{2,6},{6,2},{3,7},{7,3},{8,12},{12,8},{9,1... | collective-permute-start | bytes 245768 | tf_op jit(solution)/shard_map/ppermute | solution.py:28
  58.9 2.9 %shard_map.149 = (f32[128,512]{1,0:T(8,128)S(1)}, bf16[128,512]{1,0:T(8,128)(2,1)S(1)}) custom-call(s32[5]{0:T(128)S(1)} %stack.19.where_ref, bf16[512,128]{1,0:T(8,128)(2,1)S(1)} %get-tuple-element.37.refs_19_.sums, f32[1,512]{1,0:T(1,128)S(1)} %get-tuple-element.38.reward, bf16[8,64,512]{2,1,0:T(8,128)(2,1)S(1)} %get-tuple-element.50.entering, ...), custom_call_target="tpu_custom_call" | custom-call | flops 2000000000 | bytes 3000000 | tf_op jit(solution)/shard_map/pallas_call | solution.py:323
  61.8 1.1 %collective-permute-done.16.refs_1_ = bf16[80,512]{1,0:T(8,128)(2,1)S(1)} collective-permute-done((bf16[80,512]{1,0:T(8,128)(2,1)S(1)}, bf16[80,512]{1,0:T(8,128)(2,1)S(1)}, u32[]{:S(2)}, u32[]{:S(2)}) %collective-permute-start.16) | collective-permute-done | bytes 81952 | tf_op jit(solution)/shard_map/ppermute | solution.py:28
  63.4 2.8 %collective-permute-start.19 = (bf16[80,512]{1,0:T(8,128)(2,1)S(1)}, bf16[80,512]{1,0:T(8,128)(2,1)S(1)}, u32[]{:S(2)}, u32[]{:S(2)}) collective-permute-start(bf16[80,512]{1,0:T(8,128)(2,1)S(1)} %get-tuple-element.65), channel_id=1, source_target_pairs={{0,24},{8,16},{16,8},{24,0},{1,25},{9,17},{17,9},{25,1},{2,26},{10... | collective-permute-start | bytes 245768 | tf_op jit(solution)/shard_map/ppermute | solution.py:28
  66.3 0.8 collective-permute-start.18
  67.6 3.9 %shard_map.150 = (f32[192,512]{1,0:T(8,128)S(1)}, bf16[192,512]{1,0:T(8,128)(2,1)S(1)}) custom-call(s32[5]{0:T(128)S(1)} %stack.19.where_ref, bf16[512,128]{1,0:T(8,128)(2,1)S(1)} %get-tuple-element.37.refs_19_.sums, f32[1,512]{1,0:T(1,128)S(1)} %get-tuple-element.38.reward, bf16[8,64,512]{2,1,0:T(8,128)(2,1)S(1)} %get-tuple-element.50.entering, ...), custom_call_target="tpu_custom_call" | custom-call | flops 2000000000 | bytes 3000000 | tf_op jit(solution)/shard_map/pallas_call | solution.py:323
  71.5 0.7 collective-permute-done.18.refs_3_
  72.2 0.7 shard_map.152
  72.9 4.1 %collective-permute-start.22 = (bf16[80,512]{1,0:T(8,128)(2,1)S(1)}, bf16[80,512]{1,0:T(8,128)(2,1)S(1)}, u32[]{:S(2)}, u32[]{:S(2)}) collective-permute-start(bf16[80,512]{1,0:T(8,128)(2,1)S(1)} %get-tuple-element.68), channel_id=1, source_target_pairs={{0,96},{32,64},{64,32},{96,0},{1,97},{33,65},{65,33},{97,1},{2,98}... | collective-permute-start | bytes 245768 | tf_op jit(solution)/shard_map/ppermute | solution.py:28
  77.0 0.9 %collective-permute-start.20 = (bf16[80,512]{1,0:T(8,128)(2,1)S(1)}, bf16[80,512]{1,0:T(8,128)(2,1)S(1)}, u32[]{:S(2)}, u32[]{:S(2)}) collective-permute-start(bf16[80,512]{1,0:T(8,128)(2,1)S(1)} %get-tuple-element.68), channel_id=1, source_target_pairs={{0,32},{32,0},{64,96},{96,64},{1,33},{33,1},{65,97},{97,65},{2,34}... | collective-permute-start | bytes 245768 | tf_op jit(solution)/shard_map/ppermute | solution.py:28
  78.0 3.9 %shard_map.148 = (f32[192,512]{1,0:T(8,128)S(1)}, bf16[192,512]{1,0:T(8,128)(2,1)S(1)}) custom-call(s32[5]{0:T(128)S(1)} %stack.19.where_ref, bf16[512,128]{1,0:T(8,128)(2,1)S(1)} %get-tuple-element.37.refs_19_.sums, f32[1,512]{1,0:T(1,128)S(1)} %get-tuple-element.38.reward, bf16[8,64,512]{2,1,0:T(8,128)(2,1)S(1)} %get-tuple-element.50.entering, ...), custom_call_target="tpu_custom_call" | custom-call | flops 2000000000 | bytes 3000000 | tf_op jit(solution)/shard_map/pallas_call | solution.py:323
  81.9 1.1 %collective-permute-done.21.refs_11_ = bf16[80,512]{1,0:T(8,128)(2,1)S(1)} collective-permute-done((bf16[80,512]{1,0:T(8,128)(2,1)S(1)}, bf16[80,512]{1,0:T(8,128)(2,1)S(1)}, u32[]{:S(2)}, u32[]{:S(2)}) %collective-permute-start.21) | collective-permute-done | bytes 81952 | tf_op jit(solution)/shard_map/ppermute | solution.py:28
  83.0 3.9 %shard_map.153 = bf16[512,512]{1,0:T(8,128)(2,1)} custom-call(s32[5]{0:T(128)S(1)} %stack.19.where_ref, f32[192,512]{1,0:T(8,128)S(1)} %get-tuple-element.53.refs_0_, f32[128,512]{1,0:T(8,128)S(1)} %get-tuple-element.54.refs_1_, f32[192,512]{1,0:T(8,128)S(1)} %get-tuple-element.55.refs_2_, bf16[192,512]{1,0:T(8,128)(2,1)S(1)} %get-tuple-element.56.refs_3_, ...), custom_call_target="tpu_custom_call" | custom-call | flops 1000000000 | bytes 2000000 | tf_op jit(solution)/shard_map/pallas_call | solution.py:444
  (38 shorter events, 4.9 us)
Async XLA Ops:
  0.0 10.8 %collective-permute-start.13 = (bf16[1024,128]{1,0:T(8,128)(2,1)}, bf16[1024,128]{1,0:T(8,128)(2,1)S(1)}, u32[]{:S(2)}, u32[]{:S(2)}) collective-permute-start(bf16[1024,128]{1,0:T(8,128)(2,1)} %refs_1_.1), channel_id=1, source_target_pairs={{0,6},{2,4},{4,2},{6,0},{1,7},{3,5},{5,3},{7,1},{8,14},{10,12},{12... | collective-permute-start | bytes 786440 | tf_op jit(solution)/shard_map/ppermute | solution.py:477
  1.6 10.8 %collective-permute-start.12 = (bf16[1024,128]{1,0:T(8,128)(2,1)}, bf16[1024,128]{1,0:T(8,128)(2,1)S(1)}, u32[]{:S(2)}, u32[]{:S(2)}) collective-permute-start(bf16[1024,128]{1,0:T(8,128)(2,1)} %refs_1_.1), channel_id=1, source_target_pairs={{0,1},{1,0},{2,3},{3,2},{4,5},{5,4},{6,7},{7,6},{8,9},{9,8},{10,11... | collective-permute-start | bytes 786440 | tf_op jit(solution)/shard_map/ppermute | solution.py:28
  1.6 26.0 %collective-permute-start.10 = (bf16[1024,256]{1,0:T(8,128)(2,1)}, bf16[1024,256]{1,0:T(8,128)(2,1)S(1)}, u32[]{:S(2)}, u32[]{:S(2)}) collective-permute-start(bf16[1024,256]{1,0:T(8,128)(2,1)} %refs_0_.1), channel_id=1, source_target_pairs={{0,6},{2,4},{4,2},{6,0},{1,7},{3,5},{5,3},{7,1},{8,14},{10,12},{12... | collective-permute-start | bytes 1572872 | tf_op jit(solution)/shard_map/ppermute | solution.py:477
  2.8 7.0 %collective-permute-start = (bf16[16,1024]{1,0:T(8,128)(2,1)S(1)}, bf16[16,1024]{1,0:T(8,128)(2,1)S(1)}, u32[]{:S(2)}, u32[]{:S(2)}) collective-permute-start(bf16[16,1024]{1,0:T(8,128)(2,1)S(1)} %slice.12), channel_id=1, source_target_pairs={{0,4},{4,8},{8,12},{12,16},{16,20},{20,24},{24,28},{28,32},{32,36}... | collective-permute-start | bytes 98312 | tf_op jit(solution)/shard_map/ppermute | solution.py:492
  9.2 17.9 %collective-permute-start.5 = (bf16[176,1024]{1,0:T(8,128)(2,1)S(1)}, bf16[176,1024]{1,0:T(8,128)(2,1)S(1)}, u32[]{:S(2)}, u32[]{:S(2)}) collective-permute-start(bf16[176,1024]{1,0:T(8,128)(2,1)S(1)} %slice.14.refs_0_), channel_id=1, source_target_pairs={{0,2},{1,3},{2,0},{3,1},{4,6},{5,7},{6,4},{7,5},{8,10},{9,11},{10,... | collective-permute-start | bytes 1081352 | tf_op jit(solution)/shard_map/ppermute | solution.py:28
  9.8 17.4 %collective-permute-start.3 = (bf16[176,1024]{1,0:T(8,128)(2,1)S(1)}, bf16[176,1024]{1,0:T(8,128)(2,1)S(1)}, u32[]{:S(2)}, u32[]{:S(2)}) collective-permute-start(bf16[176,1024]{1,0:T(8,128)(2,1)S(1)} %slice.14.refs_0_), channel_id=1, source_target_pairs={{0,1},{1,0},{2,3},{3,2},{4,5},{5,4},{6,7},{7,6},{8,9},{9,8},{10,11... | collective-permute-start | bytes 1081352 | tf_op jit(solution)/shard_map/ppermute | solution.py:28
  10.8 15.8 %collective-permute-start.6 = (bf16[160,1024]{1,0:T(8,128)(2,1)S(1)}, bf16[160,1024]{1,0:T(8,128)(2,1)S(1)}, u32[]{:S(2)}, u32[]{:S(2)}) collective-permute-start(bf16[160,1024]{1,0:T(8,128)(2,1)S(1)} %slice.15.refs_1_), channel_id=1, source_target_pairs={{0,2},{1,3},{2,0},{3,1},{4,6},{5,7},{6,4},{7,5},{8,10},{9,11},{10,... | collective-permute-start | bytes 983048 | tf_op jit(solution)/shard_map/ppermute | solution.py:28
  12.4 14.2 %collective-permute-start.4 = (bf16[160,1024]{1,0:T(8,128)(2,1)S(1)}, bf16[160,1024]{1,0:T(8,128)(2,1)S(1)}, u32[]{:S(2)}, u32[]{:S(2)}) collective-permute-start(bf16[160,1024]{1,0:T(8,128)(2,1)S(1)} %slice.15.refs_1_), channel_id=1, source_target_pairs={{0,1},{1,0},{2,3},{3,2},{4,5},{5,4},{6,7},{7,6},{8,9},{9,8},{10,11... | collective-permute-start | bytes 983048 | tf_op jit(solution)/shard_map/ppermute | solution.py:28
  26.6 8.1 %collective-permute-start.9 = (bf16[1024,256]{1,0:T(8,128)(2,1)}, bf16[1024,256]{1,0:T(8,128)(2,1)S(1)}, u32[]{:S(2)}, u32[]{:S(2)}) collective-permute-start(bf16[1024,256]{1,0:T(8,128)(2,1)} %refs_0_.1), channel_id=1, source_target_pairs={{0,1},{1,0},{2,3},{3,2},{4,5},{5,4},{6,7},{7,6},{8,9},{9,8},{10,11... | collective-permute-start | bytes 1572872 | tf_op jit(solution)/shard_map/ppermute | solution.py:28
  26.6 7.7 %collective-permute-start.14 = (bf16[1024,128]{1,0:T(8,128)(2,1)S(1)}, bf16[1024,128]{1,0:T(8,128)(2,1)S(1)}, u32[]{:S(2)}, u32[]{:S(2)}) collective-permute-start(bf16[1024,128]{1,0:T(8,128)(2,1)S(1)} %collective-permute-done.13.refs_14_.refs_10_), channel_id=1, source_target_pairs={{0,1},{1,0},{2,3},{3,2},{4,5},{5,4},{6,7},{7,6},{8,9},{9,8},{10,11... | collective-permute-start | bytes 786440 | tf_op jit(solution)/shard_map/ppermute | solution.py:28
  27.1 8.0 %collective-permute-start.8 = (bf16[160,1024]{1,0:T(8,128)(2,1)S(1)}, bf16[160,1024]{1,0:T(8,128)(2,1)S(1)}, u32[]{:S(2)}, u32[]{:S(2)}) collective-permute-start(bf16[160,1024]{1,0:T(8,128)(2,1)S(1)} %collective-permute-done.6.refs_5_), channel_id=1, source_target_pairs={{0,1},{1,0},{2,3},{3,2},{4,5},{5,4},{6,7},{7,6},{8,9},{9,8},{10,11... | collective-permute-start | bytes 983048 | tf_op jit(solution)/shard_map/ppermute | solution.py:28
  27.2 7.9 %collective-permute-start.7 = (bf16[176,1024]{1,0:T(8,128)(2,1)S(1)}, bf16[176,1024]{1,0:T(8,128)(2,1)S(1)}, u32[]{:S(2)}, u32[]{:S(2)}) collective-permute-start(bf16[176,1024]{1,0:T(8,128)(2,1)S(1)} %collective-permute-done.5.refs_4_), channel_id=1, source_target_pairs={{0,1},{1,0},{2,3},{3,2},{4,5},{5,4},{6,7},{7,6},{8,9},{9,8},{10,11... | collective-permute-start | bytes 1081352 | tf_op jit(solution)/shard_map/ppermute | solution.py:28
  27.6 7.5 %collective-permute-start.11 = (bf16[1024,256]{1,0:T(8,128)(2,1)S(1)}, bf16[1024,256]{1,0:T(8,128)(2,1)S(1)}, u32[]{:S(2)}, u32[]{:S(2)}) collective-permute-start(bf16[1024,256]{1,0:T(8,128)(2,1)S(1)} %collective-permute-done.10.refs_10_.refs_6_), channel_id=1, source_target_pairs={{0,1},{1,0},{2,3},{3,2},{4,5},{5,4},{6,7},{7,6},{8,9},{9,8},{10,11... | collective-permute-start | bytes 1572872 | tf_op jit(solution)/shard_map/ppermute | solution.py:28
  27.7 6.6 %slice-start = ((bf16[512,1024]{1,0:T(8,128)(2,1)}), bf16[192,1024]{1,0:T(8,128)(2,1)S(1)}, s32[]{:S(2)}) async-start(bf16[512,1024]{1,0:T(8,128)(2,1)} %param.15), calls=%async_computation | async-start | bytes 786432 | tf_op jit(solution)/shard_map/slice | solution.py:497
  34.3 12.2 %collective-permute-start.2 = (bf16[208,1024]{1,0:T(8,128)(2,1)S(1)}, bf16[208,1024]{1,0:T(8,128)(2,1)S(1)}, u32[]{:S(2)}, u32[]{:S(2)}) collective-permute-start(bf16[208,1024]{1,0:T(8,128)(2,1)S(1)} %pad_maximum_fusion.refs_0_), channel_id=1, source_target_pairs={{0,2},{1,3},{2,0},{3,1},{4,6},{5,7},{6,4},{7,5},{8,10},{9,11},{10,... | collective-permute-start | bytes 1277960 | tf_op jit(solution)/shard_map/ppermute | solution.py:28
  34.7 11.9 %collective-permute-start.1 = (bf16[208,1024]{1,0:T(8,128)(2,1)S(1)}, bf16[208,1024]{1,0:T(8,128)(2,1)S(1)}, u32[]{:S(2)}, u32[]{:S(2)}) collective-permute-start(bf16[208,1024]{1,0:T(8,128)(2,1)S(1)} %pad_maximum_fusion.refs_0_), channel_id=1, source_target_pairs={{0,1},{1,0},{2,3},{3,2},{4,5},{5,4},{6,7},{7,6},{8,9},{9,8},{10,11... | collective-permute-start | bytes 1277960 | tf_op jit(solution)/shard_map/ppermute | solution.py:28
  46.5 1.8 %collective-permute-start.15 = (bf16[208,1024]{1,0:T(8,128)(2,1)S(1)}, bf16[208,1024]{1,0:T(8,128)(2,1)S(1)}, u32[]{:S(2)}, u32[]{:S(2)}) collective-permute-start(bf16[208,1024]{1,0:T(8,128)(2,1)S(1)} %collective-permute-done.2.refs_2_), channel_id=1, source_target_pairs={{0,1},{1,0},{2,3},{3,2},{4,5},{5,4},{6,7},{7,6},{8,9},{9,8},{10,11... | collective-permute-start | bytes 1277960 | tf_op jit(solution)/shard_map/ppermute | solution.py:28
  56.8 6.1 %collective-permute-start.16 = (bf16[80,512]{1,0:T(8,128)(2,1)S(1)}, bf16[80,512]{1,0:T(8,128)(2,1)S(1)}, u32[]{:S(2)}, u32[]{:S(2)}) collective-permute-start(bf16[80,512]{1,0:T(8,128)(2,1)S(1)} %get-tuple-element.62), channel_id=1, source_target_pairs={{0,4},{4,0},{1,5},{5,1},{2,6},{6,2},{3,7},{7,3},{8,12},{12,8},{9,1... | collective-permute-start | bytes 245768 | tf_op jit(solution)/shard_map/ppermute | solution.py:28
  63.4 8.0 %collective-permute-start.19 = (bf16[80,512]{1,0:T(8,128)(2,1)S(1)}, bf16[80,512]{1,0:T(8,128)(2,1)S(1)}, u32[]{:S(2)}, u32[]{:S(2)}) collective-permute-start(bf16[80,512]{1,0:T(8,128)(2,1)S(1)} %get-tuple-element.65), channel_id=1, source_target_pairs={{0,24},{8,16},{16,8},{24,0},{1,25},{9,17},{17,9},{25,1},{2,26},{10... | collective-permute-start | bytes 245768 | tf_op jit(solution)/shard_map/ppermute | solution.py:28
  66.3 5.9 %collective-permute-start.18 = (bf16[80,512]{1,0:T(8,128)(2,1)S(1)}, bf16[80,512]{1,0:T(8,128)(2,1)S(1)}, u32[]{:S(2)}, u32[]{:S(2)}) collective-permute-start(bf16[80,512]{1,0:T(8,128)(2,1)S(1)} %get-tuple-element.65), channel_id=1, source_target_pairs={{0,16},{8,24},{16,0},{24,8},{1,17},{9,25},{17,1},{25,9},{2,18},{10... | collective-permute-start | bytes 245768 | tf_op jit(solution)/shard_map/ppermute | solution.py:28
  67.1 5.2 %collective-permute-start.17 = (bf16[80,512]{1,0:T(8,128)(2,1)S(1)}, bf16[80,512]{1,0:T(8,128)(2,1)S(1)}, u32[]{:S(2)}, u32[]{:S(2)}) collective-permute-start(bf16[80,512]{1,0:T(8,128)(2,1)S(1)} %get-tuple-element.65), channel_id=1, source_target_pairs={{0,8},{8,0},{16,24},{24,16},{1,9},{9,1},{17,25},{25,17},{2,10},{10... | collective-permute-start | bytes 245768 | tf_op jit(solution)/shard_map/ppermute | solution.py:28
  72.9 8.9 %collective-permute-start.22 = (bf16[80,512]{1,0:T(8,128)(2,1)S(1)}, bf16[80,512]{1,0:T(8,128)(2,1)S(1)}, u32[]{:S(2)}, u32[]{:S(2)}) collective-permute-start(bf16[80,512]{1,0:T(8,128)(2,1)S(1)} %get-tuple-element.68), channel_id=1, source_target_pairs={{0,96},{32,64},{64,32},{96,0},{1,97},{33,65},{65,33},{97,1},{2,98}... | collective-permute-start | bytes 245768 | tf_op jit(solution)/shard_map/ppermute | solution.py:28
  77.0 5.9 %collective-permute-start.21 = (bf16[80,512]{1,0:T(8,128)(2,1)S(1)}, bf16[80,512]{1,0:T(8,128)(2,1)S(1)}, u32[]{:S(2)}, u32[]{:S(2)}) collective-permute-start(bf16[80,512]{1,0:T(8,128)(2,1)S(1)} %get-tuple-element.68), channel_id=1, source_target_pairs={{0,64},{32,96},{64,0},{96,32},{1,65},{33,97},{65,1},{97,33},{2,66}... | collective-permute-start | bytes 245768 | tf_op jit(solution)/shard_map/ppermute | solution.py:28
  77.0 5.9 %collective-permute-start.20 = (bf16[80,512]{1,0:T(8,128)(2,1)S(1)}, bf16[80,512]{1,0:T(8,128)(2,1)S(1)}, u32[]{:S(2)}, u32[]{:S(2)}) collective-permute-start(bf16[80,512]{1,0:T(8,128)(2,1)S(1)} %get-tuple-element.68), channel_id=1, source_target_pairs={{0,32},{32,0},{64,96},{96,64},{1,33},{33,1},{65,97},{97,65},{2,34}... | collective-permute-start | bytes 245768 | tf_op jit(solution)/shard_map/ppermute | solution.py:28

commit v3 on v2

v3 whole, which is shorter than its diff:
```python
import functools

import jax
import jax.numpy as jnp
import numpy as np
from jax import lax
from jax.experimental import pallas as pl
from jax.experimental.pallas import tpu as pltpu
from jax.sharding import Mesh
from jax.sharding import PartitionSpec as P


F32 = jnp.float32
BF16 = jnp.bfloat16
GROUP = 64
SUB = 64
LAST = 256
SPLIT = 128
CTX = 16
HALVES = (32, 16, 8, 4, 2, 1)
FLOOR = -100.0
SEQ = ("z", "x", "y_hi")
MP = ("y_lo", "core")


def xor_permute(array, axes, flip):
    length = lax.axis_size(axes)
    return lax.ppermute(array, axes, [(i, i ^ flip) for i in range(length)])


def dot(a, b):
    return jnp.dot(a, b, preferred_element_type=F32)


def dot_nt(a, b):
    return lax.dot_general(a, b, (((1,), (1,)), ((), ())), preferred_element_type=F32)


def dot_tn(a, b):
    return lax.dot_general(a, b, (((0,), (0,)), ((), ())), preferred_element_type=F32)


def sum_rows():
    t = np.arange(SUB)[:, None]
    j = np.arange(SUB)[None, :]
    blocks = []
    for half in HALVES:
        middle = (t // (2 * half)) * (2 * half) + half - 1
        right = t > middle
        blocks.append(np.where(right, (j > middle) & (j < t), (j > t) & (j <= middle)))
    blocks.append(j < t)
    blocks.append(j > t)
    one = np.concatenate(blocks, 0)
    return np.concatenate([one, one], 1).astype(np.float32)


SMEM = pl.BlockSpec(memory_space=pltpu.SMEM)
VMEM = pl.BlockSpec(memory_space=pltpu.VMEM)


def in_hbm(array):
    return pltpu.with_memory_space_constraint(array, pltpu.HBM)


def in_vmem(array):
    return pltpu.with_memory_space_constraint(array, pltpu.VMEM)


def cut_kernel(where_ref, x, late_a, late_b, early, last, ready):
    tokens = x.shape[0]
    moves = (
        (x.at[LAST - CTX : LAST + SPLIT, :], late_a),
        (x.at[tokens - CTX :, :], last),
        (x.at[LAST + SPLIT :, :], late_b),
        (x.at[0:LAST, :], early.at[CTX:, :]),
    )
    copies = [pltpu.make_async_copy(a, b, ready.at[i]) for i, (a, b) in enumerate(moves)]
    for copy in copies:
        copy.start()
    early[0:CTX, :] = jnp.zeros((CTX, early.shape[1]), BF16)
    for copy in copies:
        copy.wait()


def cut(where, x):
    tokens, width = x.shape
    return pl.pallas_call(
        cut_kernel,
        in_specs=[SMEM, pl.BlockSpec(memory_space=pltpu.HBM)],
        out_specs=[VMEM] * 4,
        scratch_shapes=[pltpu.SemaphoreType.DMA((4,))],
        out_shape=[
            pltpu.VMEM((CTX + SPLIT, width), BF16),
            pltpu.VMEM((tokens - LAST - SPLIT, width), BF16),
            pltpu.VMEM((CTX + LAST, width), BF16),
            pltpu.VMEM((CTX, width), BF16),
        ],
        compiler_params=pltpu.CompilerParams(vmem_limit_bytes=2**20),
        cost_estimate=pl.CostEstimate(flops=10**6, bytes_accessed=2 * 10**6, transcendentals=0),
    )(where, in_hbm(x))


def load_kernel(where_ref, *refs, kinds):
    count = len(kinds)
    ready = refs[2 * count]
    copies = []
    for i, kind in enumerate(kinds):
        source, target = refs[i], refs[count + i]
        if kind == "plain":
            copies.append(pltpu.make_async_copy(source, target, ready.at[i, 0]))
            continue
        width = target.shape[-1] if kind == "lanes" else target.shape[1]
        for j in range(4):
            there = pl.ds(pl.multiple_of((where_ref[0] ^ j) * width, width), width)
            block = source.at[:, :, there] if kind == "lanes" else source.at[there, :]
            copies.append(pltpu.make_async_copy(block, target.at[j], ready.at[i, j]))
    for copy in copies:
        copy.start()
    for copy in copies:
        copy.wait()


def load(where, *jobs):
    kinds, arrays = zip(*jobs)
    shapes = []
    for kind, a in jobs:
        if kind == "rows":
            shapes.append((4, a.shape[0] // 4, a.shape[1]))
        elif kind == "lanes":
            shapes.append((4, *a.shape[:2], a.shape[2] // 4))
        else:
            shapes.append(a.shape)
    return pl.pallas_call(
        functools.partial(load_kernel, kinds=kinds),
        in_specs=[SMEM] + [pl.BlockSpec(memory_space=pltpu.HBM)] * len(jobs),
        out_specs=[VMEM] * len(jobs),
        scratch_shapes=[pltpu.SemaphoreType.DMA((len(jobs), 4))],
        out_shape=[pltpu.VMEM(shape, a.dtype) for shape, a in zip(shapes, arrays)],
        compiler_params=pltpu.CompilerParams(vmem_limit_bytes=2**20),
        cost_estimate=pl.CostEstimate(flops=3 * 10**9, bytes_accessed=8 * 10**6, transcendentals=0),
    )(where, *map(in_hbm, arrays))


def read_rows(refs, cols):
    parts = [ref[:, cols] for ref in refs]
    return parts[0] if len(parts) == 1 else jnp.concatenate(parts, 0)


def mix_rows(me, start, first_token, pieces, narrows, weights, diffs, slots, consume, branches=(0, 1, 2, 3)):
    ratios, widen = weights
    tokens, width = diffs.shape[1:]
    tile = 256
    line = lax.broadcasted_iota(jnp.int32, (tokens, tile), 0)
    first = line == 0
    opens = line + first_token == start

    rank = jnp.zeros((tokens, 256), F32)
    for j in range(4):
        base = (me ^ j) * width
        parts = []
        for n in range(width // tile):
            cols = slice(tile * n, tile * n + tile)
            rows = read_rows(pieces[j], cols).astype(F32)
            x = rows[CTX:]
            before = jnp.where(first, rows[CTX - 1 : CTX], pltpu.roll(x, 1, 0))
            d = jnp.where(opens, 0.0, before) - x
            diffs[j, :, cols] = d
            ratio = ratios[0:1, pl.ds(pl.multiple_of(base + tile * n, tile), tile)]
            parts.append((x + d * ratio).astype(BF16))
        rank = rank + dot(jnp.concatenate(parts, 1), narrows[j][...])
    total = jnp.tanh(rank).astype(BF16)
    hidden = [total[:, 64 * b : 64 * b + 64] for b in range(4)]

    def mix(j):
        base = (me ^ j) * width
        for n in range(width // tile):
            cols = slice(tile * n, tile * n + tile)
            there = pl.ds(pl.multiple_of(base + tile * n, tile), tile)
            x = read_rows(pieces[j], cols)[CTX:].astype(F32)
            d = diffs[j, :, cols]
            for b in branches:
                delta = dot(hidden[b], widen[j, b, :, cols])
                slots(j, b)[:, cols] = (x + d * (ratios[b + 1 : b + 2, there] + delta)).astype(BF16)

    mix(0)
    for j in range(4):
        if j < 3:
            mix(j + 1)
        consume(j)
    return hidden


def add_product(out, cols, j, rows, weights):
    part = dot(rows[...], weights[j])
    if j == 0:
        out[:, cols] = part
    else:
        out[:, cols] += part


def decay_of(low, fade_widen, anchor):
    return -jnp.exp(anchor[...] + dot(jnp.tanh(low).astype(BF16), fade_widen[...]))


def take_pieces(refs, counts):
    pieces = []
    for count in counts:
        pieces.append(refs[:count])
        refs = refs[count:]
    return pieces, refs


def late_kernel(where_ref, *refs, counts):
    pieces, refs = take_pieces(refs, counts)
    narrows, refs = refs[0:4], refs[4:]
    ratios, widen, w_k, w_v_far, w_r_far, pair, recept, fading_rows, w_v, w_r, diffs, mixed, ready = refs
    channels, width = recept.shape[1], w_k.shape[1]

    def fetch(j, i):
        there = pl.ds(pl.multiple_of((where_ref[0] ^ j) * width, width), width)
        source, target = ((w_v_far, w_v), (w_r_far, w_r))[i]
        return pltpu.make_async_copy(source.at[there, :], target.at[j], ready.at[j, i])

    for j in range(4):
        for i in range(2):
            fetch(j, i).start()

    def slots(j, b):
        return fading_rows.at[j] if b == 0 else mixed.at[j % 2, b - 1]

    def consume(j):
        add_product(pair, slice(0, channels), j, slots(j, 1), w_k)
        fetch(j, 0).wait()
        add_product(pair, slice(channels, 2 * channels), j, slots(j, 2), w_v)
        fetch(j, 1).wait()
        add_product(recept, slice(None), j, slots(j, 3), w_r)

    mix_rows(where_ref[0], where_ref[1], LAST, pieces, narrows, (ratios, widen), diffs, slots, consume)


def decay_kernel(where_ref, rows, *refs):
    fadings, (fade_widen, anchor, sums, pair, out, partial, reach, whole) = refs[0:4], refs[4:]
    tokens, _ = out.shape
    low = dot(rows[0], fadings[0][...])
    for j in range(1, 4):
        low = low + dot(rows[j], fadings[j][...])
    out[...] = decay_of(low, fade_widen, anchor)
    count = tokens // SUB

    def note(n, state, decay, offset):
        partial[n] = state
        reach[n : n + 1, :] = decay
        reach[count + n : count + n + 1, :] = offset

    numbers = range(LAST // SUB, LAST // SUB + count)
    state, decay, _ = add_states(where_ref[1], sums, pair, out, numbers, LAST, note)
    store(whole, decay, state)


def early_kernel(where_ref, *refs, counts):
    pieces, refs = take_pieces(refs, counts)
    narrows, fadings, refs = refs[0:4], refs[4:8], refs[8:]
    ratios, widen, w_k, w_v, fade_widen, anchor, sums, partial, reach, late_whole = refs[:10]
    pair, decay, entering, offsets, whole, packed, diffs, hidden, mixed = refs[10:]
    channels = decay.shape[1]
    low = [None]

    def slots(j, b):
        return mixed.at[j % 2, b]

    def consume(j):
        part = dot(slots(j, 0)[...], fadings[j][...])
        low[0] = part if j == 0 else low[0] + part
        add_product(pair, slice(0, channels), j, slots(j, 1), w_k)
        add_product(pair, slice(channels, 2 * channels), j, slots(j, 2), w_v)

    ranks = mix_rows(
        where_ref[0], where_ref[1], 0, pieces, narrows, (ratios, widen), diffs, slots, consume, branches=(0, 1, 2)
    )
    hidden[...] = ranks[3]
    decay[...] = decay_of(low[0], fade_widen, anchor)

    def note(n, state, _, offset):
        entering[n] = state.astype(BF16)
        offsets[n : n + 1, :] = offset

    count, more = LAST // SUB, partial.shape[0]
    state, total, offset = add_states(where_ref[1], sums, pair, decay, range(count), 0, note)
    final = combine((total, state), (late_whole[SUB : SUB + 1], late_whole[0:SUB]))
    store(whole, *final)
    pack(packed, *final)
    for n in range(more):
        entering[count + n] = (partial[n] + reach[n : n + 1, :] * state).astype(BF16)
        offsets[count + n : count + n + 1, :] = offset + reach[more + n : more + n + 1, :]


def recept_kernel(where_ref, *refs, counts):
    pieces, refs = take_pieces(refs, counts)
    diffs, hidden, ratios, widen, w_r, out, mixed = refs
    width = diffs.shape[2]
    tile = 256
    for j in range(4):
        base = (where_ref[0] ^ j) * width
        for n in range(width // tile):
            cols = slice(tile * n, tile * n + tile)
            there = pl.ds(pl.multiple_of(base + tile * n, tile), tile)
            x = read_rows(pieces[j], cols)[CTX:].astype(F32)
            delta = dot(hidden[...], widen[j, 3, :, cols])
            mixed[j, :, cols] = (x + diffs[j, :, cols] * (ratios[4:5, there] + delta)).astype(BF16)
        add_product(out, slice(None), j, mixed.at[j], w_r)


def recept_early(where, pieces, diffs, hidden, ratios, widen, w_r):
    tokens, width = diffs.shape[1:]
    counts = tuple(len(p) for p in pieces)
    operands = [a for p in pieces for a in p]
    return pl.pallas_call(
        functools.partial(recept_kernel, counts=counts),
        in_specs=[SMEM] + [VMEM] * (len(operands) + 5),
        out_specs=VMEM,
        scratch_shapes=[pltpu.VMEM((4, tokens, width), BF16)],
        out_shape=pltpu.VMEM((tokens, w_r.shape[2]), F32),
        compiler_params=pltpu.CompilerParams(vmem_limit_bytes=7 * 2**20),
        cost_estimate=pl.CostEstimate(flops=2 * 10**9, bytes_accessed=5 * 10**6, transcendentals=0),
    )(where, *operands, *map(in_vmem, (diffs, hidden, ratios, widen, w_r)))


def project_late(where, pieces, narrows, ratios, widen, w_k, w_v, w_r):
    width, channels = w_k.shape[1:]
    counts = tuple(len(p) for p in pieces)
    tokens = sum(a.shape[0] for a in pieces[0]) - CTX
    operands = [a for p in pieces for a in p] + narrows
    return pl.pallas_call(
        functools.partial(late_kernel, counts=counts),
        in_specs=[SMEM] + [VMEM] * (len(operands) + 3) + [pl.BlockSpec(memory_space=pltpu.HBM)] * 2,
        out_specs=[VMEM] * 5,
        scratch_shapes=[
            pltpu.VMEM((4, tokens, width), F32),
            pltpu.VMEM((2, 3, tokens, width), BF16),
            pltpu.SemaphoreType.DMA((4, 2)),
        ],
        out_shape=[
            pltpu.VMEM((tokens, 2 * channels), F32),
            pltpu.VMEM((tokens, channels), F32),
            pltpu.VMEM((4, tokens, width), BF16),
            pltpu.VMEM((4, width, channels), BF16),
            pltpu.VMEM((4, width, channels), BF16),
        ],
        compiler_params=pltpu.CompilerParams(vmem_limit_bytes=(4 * 1024 + 40 * tokens) * 1024),
        cost_estimate=pl.CostEstimate(flops=25 * 10**6 * tokens, bytes_accessed=17 * 10**6, transcendentals=0),
    )(where, *operands, *map(in_vmem, (ratios, widen, w_k)), in_hbm(w_v), in_hbm(w_r))


def decay_late(where, rows, fadings, fade_widen, anchor, sums, pair):
    tokens, channels = rows.shape[1], anchor.shape[1]
    count = tokens // SUB
    return pl.pallas_call(
        decay_kernel,
        in_specs=[SMEM] + [VMEM] * 9,
        out_specs=[VMEM] * 4,
        out_shape=[
            pltpu.VMEM((tokens, channels), F32),
            pltpu.VMEM((count, SUB, channels), F32),
            pltpu.VMEM((2 * count, channels), F32),
            pltpu.VMEM((SUB + 8, channels), F32),
        ],
        compiler_params=pltpu.CompilerParams(vmem_limit_bytes=5 * 2**20),
        cost_estimate=pl.CostEstimate(flops=10**9, bytes_accessed=2 * 10**6, transcendentals=0),
    )(where, in_vmem(rows), *fadings, *map(in_vmem, (fade_widen, anchor, sums, pair)))


def project_early(where, pieces, narrows, fadings, weights, *rest):
    width, channels = weights[2].shape[1:]
    counts = tuple(len(p) for p in pieces)
    operands = [a for p in pieces for a in p] + narrows + fadings
    return pl.pallas_call(
        functools.partial(early_kernel, counts=counts),
        in_specs=[SMEM] + [VMEM] * (len(operands) + len(weights) + len(rest)),
        out_specs=[VMEM] * 8,
        scratch_shapes=[pltpu.VMEM((2, 3, LAST, width), BF16)],
        out_shape=[
            pltpu.VMEM((LAST, 2 * channels), F32),
            pltpu.VMEM((LAST, channels), F32),
            pltpu.VMEM((8, SUB, channels), BF16),
            pltpu.VMEM((8, channels), F32),
            jax.ShapeDtypeStruct((SUB + 8, channels), F32),
            jax.ShapeDtypeStruct((SUB + 8, channels), BF16),
            pltpu.VMEM((4, LAST, width), F32),
            pltpu.VMEM((LAST, 64), BF16),
        ],
        compiler_params=pltpu.CompilerParams(vmem_limit_bytes=(5 * 1024 + 16 * LAST) * 1024),
        cost_estimate=pl.CostEstimate(flops=25 * 10**6 * LAST, bytes_accessed=17 * 10**6, transcendentals=0),
    )(where, *operands, *map(in_vmem, (*weights, *rest)))


def split_two(w):
    high = w.astype(BF16)
    low = (w - high.astype(F32)).astype(BF16)
    return jnp.concatenate([high, low], 0)


def add_states(start, sums, pair, decays, numbers, first_token, note):
    channels = decays.shape[1]
    line = lax.broadcasted_iota(jnp.int32, (SUB, 1), 0)
    lane = lax.broadcasted_iota(jnp.int32, (SUB, 128), 1)
    state = jnp.zeros((SUB, channels), F32)
    decay = jnp.ones((1, channels), F32)
    offset = jnp.zeros((1, channels), F32)
    for n, c in enumerate(numbers):
        note(n, state, decay, offset)
        at = SUB * c - first_token
        w = jnp.maximum(decays[at : at + SUB, :], FLOOR)
        k = pair[at : at + SUB, 0:channels]
        v = pair[at : at + SUB, channels : 2 * channels].astype(BF16)
        tail = dot(sums[7 * SUB : 8 * SUB, :], split_two(w))
        ends_late = (c * SUB + SUB - 1) >= start
        begins_late = (c * SUB - 1) >= start if c else jnp.bool_(False)
        late = (line + c * SUB) >= start
        log_total = tail[0:1, :] + w[0:1, :]
        total = jnp.where(begins_late == ends_late, jnp.exp(log_total), 0.0)
        kk = jnp.where(late == ends_late, k * jnp.exp(tail), 0.0).astype(BF16)
        pieces = []
        for p in range(channels // 128):
            cols = slice(128 * p, 128 * p + 128)
            both = dot_tn(v[:, cols], kk[:, cols])
            pieces.append(jnp.where(lane < GROUP, both[0:GROUP], both[GROUP:128]))
        state = state * total + jnp.concatenate(pieces, 1)
        decay = decay * total
        offset = offset + log_total
    return state, decay, offset


def local_kernel(where_ref, sums, reward, entering, offsets, recept, pair, decay, local, queries, *, first, count, first_token):
    start = where_ref[1]
    channels = local.shape[1]
    line = lax.broadcasted_iota(jnp.int32, (SUB, 1), 0)
    lane = lax.broadcasted_iota(jnp.int32, (SUB, 128), 1)
    two_t = lax.broadcasted_iota(jnp.int32, (2 * SUB, SUB), 0) % SUB
    two_s = lax.broadcasted_iota(jnp.int32, (2 * SUB, SUB), 1)

    def apart(a):
        zero = jnp.zeros_like(a)
        return jnp.concatenate([jnp.where(lane < GROUP, a, zero), jnp.where(lane < GROUP, zero, a)], 0)

    for n in range(count):
        c = first + n
        at = SUB * c - first_token
        there = slice(at, at + SUB)
        r = recept[there, :]
        k, v = [pair[there, channels * i : channels * i + channels] for i in range(2)]
        w = decay[there, :]
        v = v.astype(BF16)
        w = jnp.maximum(w, FLOOR)
        sides = []
        exponents = dot(sums[0 : 7 * SUB, :], split_two(w))
        for level, half in enumerate(HALVES):
            right = (line // half) % 2 == 1
            e = jnp.exp(exponents[SUB * level : SUB * level + SUB, :])
            sides.append((jnp.where(right, r, k) * e).astype(BF16))
        before_here = exponents[6 * SUB : 7 * SUB, :]
        late = (line + c * SUB) >= start
        begins_late = (c * SUB - 1) >= start if c else jnp.bool_(False)
        reach = jnp.where(late == begins_late, r * jnp.exp(before_here), 0.0).astype(BF16)
        offset = offsets[c : c + 1, :]
        rows = slice(SUB * n, SUB * n + SUB)
        queries[rows, :] = jnp.where(late, 0.0, r * jnp.exp(offset + before_here)).astype(BF16)
        own = (r * reward[...]).astype(BF16)
        k_own = k.astype(BF16)
        same = ((two_t + c * SUB) >= start) == ((two_s + c * SUB) >= start)
        for p in range(channels // 128):
            cols = slice(128 * p, 128 * p + 128)
            scores = jnp.where(two_t == two_s, dot_nt(apart(own[:, cols]), k_own[:, cols]), 0.0)
            for level, half in enumerate(HALVES):
                side = sides[level][:, cols]
                part = dot_nt(apart(side), side)
                here = (two_t // (2 * half) == two_s // (2 * half)) & ((two_t // half) % 2 == 1) & ((two_s // half) % 2 == 0)
                scores = jnp.where(here & same, part, scores)
            both = dot(scores.astype(BF16), v[:, cols])
            out = jnp.where(lane < GROUP, both[0:SUB], both[SUB : 2 * SUB])
            local[rows, cols] = out + dot_nt(reach[:, cols], apart(entering[c, :, cols]))


def local_outputs(where, sums, reward, entering, offsets, recept, pair, decay, numbers, first_token):
    channels = entering.shape[2]
    tokens = len(numbers) * SUB
    return pl.pallas_call(
        functools.partial(local_kernel, first=numbers[0], count=len(numbers), first_token=first_token),
        in_specs=[SMEM] + [VMEM] * 7,
        out_specs=[VMEM] * 2,
        out_shape=[pltpu.VMEM((tokens, channels), F32), pltpu.VMEM((tokens, channels), BF16)],
        compiler_params=pltpu.CompilerParams(vmem_limit_bytes=8 * 1024 * 1024),
        cost_estimate=pl.CostEstimate(flops=2 * 10**9, bytes_accessed=3 * 10**6, transcendentals=0),
    )(where, *map(in_vmem, (sums, reward, entering, offsets, recept, pair, decay)))


def unpack(ref):
    return ref[SUB : SUB + 1].astype(F32) + ref[SUB + 1 : SUB + 2].astype(F32), ref[0:SUB].astype(F32)


def pack(ref, decay, state):
    high = decay.astype(BF16)
    low = (decay - high.astype(F32)).astype(BF16)
    wide = (8, decay.shape[1])
    line = lax.broadcasted_iota(jnp.int32, wide, 0)
    high, low = high.astype(F32), low.astype(F32)
    ref[0:SUB, :] = state.astype(BF16)
    ref[SUB : SUB + 8, :] = jnp.where(line == 0, high, jnp.where(line == 1, low, 0.0)).astype(BF16)


def store(ref, decay, state):
    ref[0:SUB, :] = state
    ref[SUB : SUB + 8, :] = jnp.broadcast_to(decay, (8, decay.shape[1]))


def combine(earlier, later):
    return earlier[0] * later[0], later[0] * earlier[1] + later[1]


def choose(flag, a, b):
    return tuple(jnp.where(flag, u, v) for u, v in zip(a, b))


def along_axis(here, own, received, before):
    pieces = [own] + [unpack(ref) for ref in received]
    length = len(pieces)
    start = (jnp.ones_like(own[0]), jnp.zeros_like(own[1]))
    inside, so_far = start, None
    for m in range(length):
        from_m = pieces[m]
        for other in range(1, length):
            from_m = choose(here == other, pieces[m ^ other], from_m)
        if m:
            inside = choose(here == m, so_far, inside)
        so_far = from_m if so_far is None else combine(so_far, from_m)
    return inside if before is None else combine(inside, before), so_far


def merge_kernel(where_ref, *refs, place, count, opening):
    whole, refs = refs[0], refs[1:]
    before = None
    if not opening:
        before, refs = (refs[0][SUB : SUB + 1], refs[0][0:SUB]), refs[1:]
    received, (whole_out, packed_out, before_out) = refs[:count], refs[count:]
    own = (whole[SUB : SUB + 1], whole[0:SUB])
    before, total = along_axis(where_ref[place], own, received, before)
    store(whole_out, *total)
    pack(packed_out, *total)
    store(before_out, *before)


def merge(where, place, whole, before, received):
    channels = whole.shape[1]
    operands = [whole] + ([] if before is None else [before]) + received
    return pl.pallas_call(
        functools.partial(merge_kernel, place=place, count=len(received), opening=before is None),
        in_specs=[SMEM] + [VMEM] * len(operands),
        out_specs=[VMEM] * 3,
        out_shape=[
            jax.ShapeDtypeStruct((SUB + 8, channels), F32),
            jax.ShapeDtypeStruct((SUB + 8, channels), BF16),
            jax.ShapeDtypeStruct((SUB + 8, channels), F32),
        ],
        compiler_params=pltpu.CompilerParams(vmem_limit_bytes=4 * 1024 * 1024),
        cost_estimate=pl.CostEstimate(flops=10**8, bytes_accessed=10**6, transcendentals=0),
    )(where, *operands)


def finish_kernel(where_ref, *refs, parts, place):
    locals_, queries, refs = refs[:parts], refs[parts : 2 * parts], refs[2 * parts :]
    gain, shift, whole, before, *received, out, held, ready = refs
    own = (whole[SUB : SUB + 1], whole[0:SUB])
    (_, incoming), _ = along_axis(where_ref[place], own, received, (before[SUB : SUB + 1], before[0:SUB]))
    incoming = incoming.astype(BF16)
    channels = gain.shape[1]
    lane = lax.broadcasted_iota(jnp.int32, (SUB, 128), 1)
    row = lax.broadcasted_iota(jnp.int32, (128, 128), 0)
    col = lax.broadcasted_iota(jnp.int32, (128, 128), 1)
    average = jnp.where((row // GROUP) == (col // GROUP), 1.0 / GROUP, 0.0).astype(BF16)
    copies = []
    at = 0
    for i in range(parts):
        rows = slice(at, at + locals_[i].shape[0])
        at = rows.stop
        for p in range(channels // 128):
            cols = slice(128 * p, 128 * p + 128)
            st = incoming[:, cols]
            zero = jnp.zeros_like(st)
            st = jnp.concatenate([jnp.where(lane < GROUP, st, zero), jnp.where(lane < GROUP, zero, st)], 0)
            o = locals_[i][:, cols] + dot_nt(queries[i][:, cols], st)
            centred = o - dot(o.astype(BF16), average)
            variance = dot((centred * centred).astype(BF16), average)
            normed = centred * lax.rsqrt(variance + 0.00064)
            held[rows, cols] = (normed * gain[:, cols] + shift[:, cols]).astype(BF16)
        copies.append(pltpu.make_async_copy(held.at[rows, :], out.at[rows, :], ready.at[i]))
        copies[-1].start()
    for copy in copies:
        copy.wait()


def finish(where, place, locals_, queries, gain, shift, whole, before, received):
    parts = len(locals_)
    tokens, channels = sum(a.shape[0] for a in locals_), gain.shape[1]
    return pl.pallas_call(
        functools.partial(finish_kernel, parts=parts, place=place),
        in_specs=[SMEM] + [VMEM] * (2 * parts + 4 + len(received)),
        out_specs=pl.BlockSpec(memory_space=pltpu.HBM),
        scratch_shapes=[pltpu.VMEM((tokens, channels), BF16), pltpu.SemaphoreType.DMA((parts,))],
        out_shape=jax.ShapeDtypeStruct((tokens, channels), BF16),
        compiler_params=pltpu.CompilerParams(vmem_limit_bytes=8 * 1024 * 1024),
        cost_estimate=pl.CostEstimate(flops=10**9, bytes_accessed=2 * 10**6, transcendentals=0),
    )(where, *map(in_vmem, (*locals_, *queries, gain, shift)), whole, before, *received)


def inner(
    layer_inputs,
    article_opening,
    blending_ratios,
    blending_narrow_operand,
    blending_widen_operand,
    fading_narrow_operand,
    fading_widen_operand,
    fading_anchor,
    immediate_reward,
    acceptance_weights,
    lookup_weights,
    payload_weights,
    group_scaling_weight,
    group_scaling_shift,
):
    x = layer_inputs
    places = [lax.axis_index(axis).astype(jnp.int32) for axis in (MP, *SEQ)]
    where = jnp.stack([places[0], article_opening[0], *places[1:]])
    shards = lax.axis_size(SEQ)

    def across_far(a):
        return lax.ppermute(a, ("y_hi", "y_lo"), [(i, i ^ 3) for i in range(4)])

    def partner(a):
        return xor_permute(a, MP, 1)

    def across(a):
        return xor_permute(a, MP, 2)

    late_a, late_b, own_early, last = cut(where, x)
    own_late = [late_a, late_b]
    far_late_a = across(late_a)
    far_narrow = across_far(blending_narrow_operand)
    near_narrow = partner(blending_narrow_operand)
    far_fading = across_far(fading_narrow_operand)
    near_fading = partner(fading_narrow_operand)
    near_late_a = partner(late_a)
    before = lax.ppermute(last, SEQ, [(i, i + 1) for i in range(shards - 1)])
    far_late_b = across(late_b)
    near_late_b = partner(late_b)
    own_early = lax.dynamic_update_slice(own_early, before, (0, 0))
    far_early = across(own_early)
    near_early = partner(own_early)
    sums = jnp.asarray(sum_rows(), BF16)
    widen, w_k, ratios, narrow, fade_widen, anchor, sums, reward, gain, shift, fading = load(
        where, ("lanes", blending_widen_operand), ("rows", lookup_weights), ("plain", blending_ratios),
        ("plain", blending_narrow_operand), ("plain", fading_widen_operand), ("plain", fading_anchor[None]),
        ("plain", sums), ("plain", immediate_reward[None]), ("plain", group_scaling_weight[None]),
        ("plain", group_scaling_shift[None]), ("plain", fading_narrow_operand),
    )
    next_late_a = partner(far_late_a)
    next_narrow = partner(far_narrow)
    next_fading = partner(far_fading)
    next_late_b = partner(far_late_b)
    narrows = [narrow, near_narrow, far_narrow, next_narrow]
    fadings = [fading, near_fading, far_fading, next_fading]
    pieces = [own_late, [near_late_a, near_late_b], [far_late_a, far_late_b], [next_late_a, next_late_b]]
    late, late_recept, fading_rows, w_v, w_r = project_late(
        where, pieces, narrows, ratios, widen, w_k, payload_weights, acceptance_weights
    )
    far_early, late = lax.optimization_barrier((far_early, late))
    late_decay, partial, reach, late_whole = decay_late(where, fading_rows, fadings, fade_widen, anchor, sums, late)
    next_early = partner(far_early)
    pieces = [[own_early], [near_early], [far_early], [next_early]]
    early, decay, entering, offsets, whole, packed, diffs, hidden = project_early(
        where, pieces, narrows, fadings, (ratios, widen, w_k, w_v), fade_widen, anchor, sums,
        partial, reach, late_whole,
    )
    early_recept = recept_early(where, pieces, diffs, hidden, ratios, widen, w_r)
    middle, end = LAST // SUB, x.shape[0] // SUB
    jobs = (
        (early_recept, early, decay, tuple(range(middle)), 0),
        (late_recept, late, late_decay, tuple(range(middle, end)), LAST),
    )
    outputs = []
    for job in jobs:
        outputs.append(local_outputs(where, sums, reward, entering, offsets, *job))
    before = None
    for axis in reversed(SEQ):
        received = []
        for k in range(1, lax.axis_size(axis)):
            received.append(xor_permute(packed, axis, k))
        place = 2 + SEQ.index(axis)
        if axis != SEQ[0]:
            whole, packed, before = merge(where, place, whole, before, received)
    locals_, queries = zip(*outputs)
    return finish(where, place, locals_, queries, gain, shift, whole, before, received)


def solution(mesh):
    torus = Mesh(mesh.devices.reshape(4, 4, 2, 2, 2), ("z", "x", "y_hi", "y_lo", "core"))
    placed = (
        P(SEQ, MP),
        P(SEQ),
        P(),
        P(MP, None),
        P(),
        P(MP, None),
        P(None, MP),
        P(MP),
        P(MP),
        P(None, MP),
        P(None, MP),
        P(None, MP),
        P(MP),
        P(MP),
    )
    return jax.shard_map(inner, mesh=torus, in_specs=placed, out_specs=P(SEQ, MP), check_vma=False)
```

time: 88.5 us -> 85.8 us (0.969)
  local copies, waits for them, and re-layouts: 2.85 us -> 0.09 us
  waiting for transfers between devices: 18.8 us -> 16.6 us
  Pallas kernels: 41.7 us -> 43.2 us
    ppermute x20, waiting for transfers between devices: 18.4 us -> 7.12 us  [xor_permute(): return lax.ppermute(array, axes, [(i, i ^ flip) for i in range(length)])]
    ppermute x1, waiting for transfers between devices: 0.35 us -> 9.43 us  [inner(): before = lax.ppermute(last, SEQ, [(i, i + 1) for i in range(shards - 1)])]
    slice x5 -> x0, local copies, waits for them, and re-layouts: 2.77 us -> none  [the longest x2 2.01 us: inner(): own_late = [x[LAST - CTX:cut], x[cut:]]]
    ppermute x1, starting transfers between devices: 5.4 us -> 2.72 us  [inner(): before = lax.ppermute(last, SEQ, [(i, i + 1) for i in range(shards - 1)])]
    pallas_call x5 -> x7, Pallas kernels: 28.1 us -> 30.6 us  [the longest x1 10.1 us: project_late(): pl.pallas_call(functools.partial(late_kernel, counts=counts), in_specs=[S...]
    ppermute x2, starting transfers between devices: 2.03 us -> 3.86 us  [across_far(): return lax.ppermute(a, ('y_hi', 'y_lo'), [(i, i ^ 3) for i in range(4)])]
    ppermute x20, starting transfers between devices: 15.3 us -> 17 us  [xor_permute(): return lax.ppermute(array, axes, [(i, i ^ flip) for i in range(length)])]
    pallas_call x1, Pallas kernels: 3.88 us -> 2.82 us  [finish(): pl.pallas_call(functools.partial(finish_kernel, parts=parts, place=place)...]
  transfers between devices with their start and end apart: 23 -> 23, of which waited for: 7 -> 6; matrix products, arithmetic and copies ran while one was open for 3% -> 0% of each run, Pallas kernels for 32% -> 36%
where the time goes in v3:
time: 85.8 us; the launch traced here: 84.4 us
  Pallas kernels  43.2 us (50%)
  starting transfers between devices  23.5 us (27%)
  waiting for transfers between devices  16.6 us (19%)
  between operations  1.02 us (1%)
    ppermute x20, starting transfers between devices, xor_permute(): return lax.ppermute(array, axes, [(i, i ^ flip) for i in range(length)])  17 us
    pallas_call x1, Pallas kernels, project_late(): pl.pallas_call(functools.partial(late_kernel, counts=counts), in_specs=[S...  10.1 us
    pallas_call x2, Pallas kernels, local_outputs(): pl.pallas_call(functools.partial(local_kernel, first=numbers[0], count=le...  9.72 us
    ppermute x1, waiting for transfers between devices, inner(): before = lax.ppermute(last, SEQ, [(i, i + 1) for i in range(shards - 1)])  9.43 us
    pallas_call x1, Pallas kernels, project_early(): pl.pallas_call(functools.partial(early_kernel, counts=counts), in_specs=[...  8.56 us
    ppermute x20, waiting for transfers between devices, xor_permute(): return lax.ppermute(array, axes, [(i, i ^ flip) for i in range(length)])  7.12 us
    pallas_call x1, Pallas kernels, load(): pl.pallas_call(functools.partial(load_kernel, kinds=kinds), in_specs=[SME...  4.05 us
    ppermute x2, starting transfers between devices, across_far(): return lax.ppermute(a, ('y_hi', 'y_lo'), [(i, i ^ 3) for i in range(4)])  3.86 us
  transfers between devices with their start and end apart: 23, of which 6 were waited for; matrix products, arithmetic and copies ran while one was open for 0% of the time, Pallas kernels for 36%

profile of v3, /device:TPU:8, one launch (start us, length us, event | category | flops | bytes accessed | tf_op | source)
XLA Modules:
  0.0 84.4 jit_solution(13499351675120282026)
XLA Ops:
  0.0 1.6 %collective-permute-start.10 = (bf16[1024,256]{1,0:T(8,128)(2,1)}, bf16[1024,256]{1,0:T(8,128)(2,1)S(1)}, u32[]{:S(2)}, u32[]{:S(2)}) collective-permute-start(bf16[1024,256]{1,0:T(8,128)(2,1)} %refs_3_.1), channel_id=1, source_target_pairs={{0,6},{2,4},{4,2},{6,0},{1,7},{3,5},{5,3},{7,1},{8,14},{10,12},{12... | collective-permute-start | bytes 1572872 | tf_op jit(solution)/shard_map/ppermute | solution.py:636
  2.3 1.8 %shard_map.146 = (bf16[144,1024]{1,0:T(8,128)(2,1)S(1)}, bf16[128,1024]{1,0:T(8,128)(2,1)S(1)}, bf16[272,1024]{1,0:T(8,128)(2,1)S(1)}, bf16[16,1024]{1,0:T(8,128)(2,1)S(1)}) custom-call(s32[5]{0:T(128)S(1)} %stack.19.where_ref, bf16[512,1024]{1,0:T(8,128)(2,1)} %x.1), custom_call_target="tpu_custom_call" | custom-call | flops 1000000 | bytes 2000000 | tf_op jit(solution)/shard_map/pallas_call | solution.py:87
  4.1 2.0 %collective-permute-start.5 = (bf16[144,1024]{1,0:T(8,128)(2,1)S(1)}, bf16[144,1024]{1,0:T(8,128)(2,1)S(1)}, u32[]{:S(2)}, u32[]{:S(2)}) collective-permute-start(bf16[144,1024]{1,0:T(8,128)(2,1)S(1)} %get-tuple-element.53.refs_0_), channel_id=1, source_target_pairs={{0,2},{1,3},{2,0},{3,1},{4,6},{5,7},{6,4},{7,5},{8,10},{9,11},{10,... | collective-permute-start | bytes 884744 | tf_op jit(solution)/shard_map/ppermute | solution.py:28
  6.2 2.7 %collective-permute-start = (bf16[16,1024]{1,0:T(8,128)(2,1)S(1)}, bf16[16,1024]{1,0:T(8,128)(2,1)S(1)}, u32[]{:S(2)}, u32[]{:S(2)}) collective-permute-start(bf16[16,1024]{1,0:T(8,128)(2,1)S(1)} %get-tuple-element.52), channel_id=1, source_target_pairs={{0,4},{4,8},{8,12},{12,16},{16,20},{20,24},{24,28},{28,32},{32,36}... | collective-permute-start | bytes 98312 | tf_op jit(solution)/shard_map/ppermute | solution.py:652
  9.0 9.4 %collective-permute-done = bf16[16,1024]{1,0:T(8,128)(2,1)S(1)} collective-permute-done((bf16[16,1024]{1,0:T(8,128)(2,1)S(1)}, bf16[16,1024]{1,0:T(8,128)(2,1)S(1)}, u32[]{:S(2)}, u32[]{:S(2)}) %collective-permute-start) | collective-permute-done | bytes 32800 | tf_op jit(solution)/shard_map/ppermute | solution.py:652
  19.5 4.0 %shard_map.145 = (bf16[4,4,64,1024]{3,2,1,0:T(8,128)(2,1)S(1)}, bf16[4,1024,512]{2,1,0:T(8,128)(2,1)S(1)}, f32[5,4096]{1,0:T(8,128)S(1)}, bf16[1024,256]{1,0:T(8...) custom-call(s32[5]{0:T(128)S(1)} %stack.19.where_ref, ...), custom_call_target="tpu_custom_call" | custom-call | flops 3000000000 | bytes 8000000 | tf_op jit(solution)/shard_map/pallas_call | solution.py:133
  23.6 2.3 %collective-permute-start.14 = (bf16[1024,128]{1,0:T(8,128)(2,1)S(1)}, bf16[1024,128]{1,0:T(8,128)(2,1)S(1)}, u32[]{:S(2)}, u32[]{:S(2)}) collective-permute-start(bf16[1024,128]{1,0:T(8,128)(2,1)S(1)} %copy-done), channel_id=1, source_target_pairs={{0,6},{2,4},{4,2},{6,0},{1,7},{3,5},{5,3},{7,1},{8,14},{10,12},{12... | collective-permute-start | bytes 786440 | tf_op jit(solution)/shard_map/ppermute | solution.py:636
  25.9 3.0 %collective-permute-start.2 = (bf16[272,1024]{1,0:T(8,128)(2,1)S(1)}, bf16[272,1024]{1,0:T(8,128)(2,1)S(1)}, u32[]{:S(2)}, u32[]{:S(2)}) collective-permute-start(bf16[272,1024]{1,0:T(8,128)(2,1)S(1)} %constant_dynamic-update-slice_fusion.refs_0_), channel_id=1, source_target_pairs={{0,2},{1,3},{2,0},{3,1},{4,6},{5,7},{6,4},{7,5},{8,10},{9,11},{10,... | collective-permute-start | bytes 1671176 | tf_op jit(solution)/shard_map/ppermute | solution.py:28
  28.9 10.1 %shard_map.147 = (f32[256,1024]{1,0:T(8,128)S(1)}, f32[256,512]{1,0:T(8,128)S(1)}, bf16[4,256,1024]{2,1,0:T(8,128)(2,1)S(1)}, bf16[4,1024,512]{2,1,0:T(8,128)(2,1)S(1)}, bf16[4,1024,512]{2,1,0:T(8,128)(2,1)S(1)}) custom-call(s32[5]{0:T(128)S(1)} %stack.19.where_ref, bf16[144,1024]{1,0:T(8,128)(2,1)S(1)} %get-tuple-element.53.refs_0_, ...), custom_call_target="tpu_custom_call" | custom-call | flops 6400000000 | bytes 17000000 | tf_op jit(solution)/shard_map/pallas_call | solution.py:333
  39.0 2.8 %collective-permute-done.2.refs_2_ = bf16[272,1024]{1,0:T(8,128)(2,1)S(1)} collective-permute-done((bf16[272,1024]{1,0:T(8,128)(2,1)S(1)}, bf16[272,1024]{1,0:T(8,128)(2,1)S(1)}, u32[]{:S(2)}, u32[]{:S(2)}) %collective-permute-start.2) | collective-permute-done | bytes 557088 | tf_op jit(solution)/shard_map/ppermute | solution.py:28
  42.3 1.8 %collective-permute-done.13.refs_1_.refs_9_ = bf16[1024,128]{1,0:T(8,128)(2,1)S(1)} collective-permute-done((bf16[1024,128]{1,0:T(8,128)(2,1)S(1)}, bf16[1024,128]{1,0:T(8,128)(2,1)S(1)}, u32[]{:S(2)}, u32[]{:S(2)}) %collective-permute-start.13) | collective-permute-done | bytes 262176 | tf_op jit(solution)/shard_map/ppermute | solution.py:28
  44.5 2.3 %shard_map.148 = (f32[256,512]{1,0:T(8,128)S(1)}, f32[4,64,512]{2,1,0:T(8,128)S(1)}, f32[8,512]{1,0:T(8,128)S(1)}, f32[72,512]{1,0:T(8,128)S(1)}) custom-call(s32[5]{0:T(128)S(1)} %stack.19.where_ref, bf16[4,256,1024]{2,1,0:T(8,128)(2,1)S(1)} %get-tuple-element.65.rows, bf16[1024,128]{1,0:T(8,128)(2,1)S(1)} %get-tuple-element.61.refs_0_.refs_8_, ...), custom_call_target="tpu_custom_call" | custom-call | flops 1000000000 | bytes 2000000 | tf_op jit(solution)/shard_map/pallas_call | solution.py:357
  46.8 8.6 %shard_map.149 = (f32[256,1024]{1,0:T(8,128)S(1)}, f32[256,512]{1,0:T(8,128)S(1)}, bf16[8,64,512]{2,1,0:T(8,128)(2,1)S(1)}, f32[8,512]{1,0:T(8,128)S(1)}, f32[72...) custom-call(s32[5]{0:T(128)S(1)} %stack.19.where_ref, ...), custom_call_target="tpu_custom_call" | custom-call | flops 6400000000 | bytes 17000000 | tf_op jit(solution)/shard_map/pallas_call | solution.py:376
  55.4 1.0 %collective-permute-start.16 = (bf16[72,512]{1,0:T(8,128)(2,1)S(1)}, bf16[72,512]{1,0:T(8,128)(2,1)S(1)}, u32[]{:S(2)}, u32[]{:S(2)}) collective-permute-start(bf16[72,512]{1,0:T(8,128)(2,1)S(1)} %get-tuple-element.86), channel_id=1, source_target_pairs={{0,4},{4,0},{1,5},{5,1},{2,6},{6,2},{3,7},{7,3},{8,12},{12,8},{9,1... | collective-permute-start | bytes 221192 | tf_op jit(solution)/shard_map/ppermute | solution.py:28
  56.4 4.8 %shard_map.152 = (f32[256,512]{1,0:T(8,128)S(1)}, bf16[256,512]{1,0:T(8,128)(2,1)S(1)}) custom-call(s32[5]{0:T(128)S(1)} %stack.19.where_ref, bf16[512,128]{1,0:T(8,128)(2,1)S(1)} %get-tuple-element.49.refs_6_.refs_18_.sums, f32[1,512]{1,0:T(1,128)S(1)} %get-tuple-element.50.reward, bf16[8,64,512]{2,1,0:T(8,128)(2,1)S(1)} %get-tuple-element.70.entering, ...), custom_call_target="tpu_custom_call" | custom-call | flops 2000000000 | bytes 3000000 | tf_op jit(solution)/shard_map/pallas_call | solution.py:486
  61.9 2.8 %collective-permute-start.19 = (bf16[72,512]{1,0:T(8,128)(2,1)S(1)}, bf16[72,512]{1,0:T(8,128)(2,1)S(1)}, u32[]{:S(2)}, u32[]{:S(2)}) collective-permute-start(bf16[72,512]{1,0:T(8,128)(2,1)S(1)} %get-tuple-element.89), channel_id=1, source_target_pairs={{0,24},{8,16},{16,8},{24,0},{1,25},{9,17},{17,9},{25,1},{2,26},{10... | collective-permute-start | bytes 221192 | tf_op jit(solution)/shard_map/ppermute | solution.py:28
  64.7 0.8 collective-permute-start.18
  66.1 2.6 %shard_map.150.recept = f32[256,512]{1,0:T(8,128)S(1)} custom-call(s32[5]{0:T(128)S(1)} %stack.19.where_ref, bf16[272,1024]{1,0:T(8,128)(2,1)S(1)} %constant_dynamic-update-slice_fusion.refs_0_, bf16[272,1024]{1,0:T(8,128)(2,1)S(1)} %collective-permute-done.1.refs_1_, bf16[272,1024]{1,0:T(8,128)(2,1)S(1)} %collective-permute-done.2.refs_2_, ...), custom_call_target="tpu_custom_call" | custom-call | flops 2000000000 | bytes 5000000 | tf_op jit(solution)/shard_map/pallas_call | solution.py:317
  68.7 2.0 %collective-permute-done.18.refs_3_ = bf16[72,512]{1,0:T(8,128)(2,1)S(1)} collective-permute-done((bf16[72,512]{1,0:T(8,128)(2,1)S(1)}, bf16[72,512]{1,0:T(8,128)(2,1)S(1)}, u32[]{:S(2)}, u32[]{:S(2)}) %collective-permute-start.18) | collective-permute-done | bytes 73760 | tf_op jit(solution)/shard_map/ppermute | solution.py:28
  70.7 0.7 shard_map.154
  71.4 4.1 %collective-permute-start.22 = (bf16[72,512]{1,0:T(8,128)(2,1)S(1)}, bf16[72,512]{1,0:T(8,128)(2,1)S(1)}, u32[]{:S(2)}, u32[]{:S(2)}) collective-permute-start(bf16[72,512]{1,0:T(8,128)(2,1)S(1)} %get-tuple-element.92), channel_id=1, source_target_pairs={{0,96},{32,64},{64,32},{96,0},{1,97},{33,65},{65,33},{97,1},{2,98}... | collective-permute-start | bytes 221192 | tf_op jit(solution)/shard_map/ppermute | solution.py:28
  75.6 0.9 %collective-permute-start.20 = (bf16[72,512]{1,0:T(8,128)(2,1)S(1)}, bf16[72,512]{1,0:T(8,128)(2,1)S(1)}, u32[]{:S(2)}, u32[]{:S(2)}) collective-permute-start(bf16[72,512]{1,0:T(8,128)(2,1)S(1)} %get-tuple-element.92), channel_id=1, source_target_pairs={{0,32},{32,0},{64,96},{96,64},{1,33},{33,1},{65,97},{97,65},{2,34}... | collective-permute-start | bytes 221192 | tf_op jit(solution)/shard_map/ppermute | solution.py:28
  76.5 4.9 %shard_map.151 = (f32[256,512]{1,0:T(8,128)S(1)}, bf16[256,512]{1,0:T(8,128)(2,1)S(1)}) custom-call(s32[5]{0:T(128)S(1)} %stack.19.where_ref, bf16[512,128]{1,0:T(8,128)(2,1)S(1)} %get-tuple-element.49.refs_6_.refs_18_.sums, f32[1,512]{1,0:T(1,128)S(1)} %get-tuple-element.50.reward, bf16[8,64,512]{2,1,0:T(8,128)(2,1)S(1)} %get-tuple-element.70.entering, ...), custom_call_target="tpu_custom_call" | custom-call | flops 2000000000 | bytes 3000000 | tf_op jit(solution)/shard_map/pallas_call | solution.py:486
  81.4 2.8 %shard_map.155 = bf16[512,512]{1,0:T(8,128)(2,1)} custom-call(s32[5]{0:T(128)S(1)} %stack.19.where_ref, f32[256,512]{1,0:T(8,128)S(1)} %get-tuple-element.77.refs_0_, f32[256,512]{1,0:T(8,128)S(1)} %get-tuple-element.80.refs_1_, bf16[256,512]{1,0:T(8,128)(2,1)S(1)} %get-tuple-element.81.refs_2_, bf16[256,512]{1,0:T(8,128)(2,1)S(1)} %get-tuple-element.82.refs_3_, ...), custom_call_target="tpu_custom_call" | custom-call | flops 1000000000 | bytes 2000000 | tf_op jit(solution)/shard_map/pallas_call | solution.py:603
  (37 shorter events, 3.5 us)
Async XLA Ops:
  0.0 18.4 %collective-permute-start.10 = (bf16[1024,256]{1,0:T(8,128)(2,1)}, bf16[1024,256]{1,0:T(8,128)(2,1)S(1)}, u32[]{:S(2)}, u32[]{:S(2)}) collective-permute-start(bf16[1024,256]{1,0:T(8,128)(2,1)} %refs_3_.1), channel_id=1, source_target_pairs={{0,6},{2,4},{4,2},{6,0},{1,7},{3,5},{5,3},{7,1},{8,14},{10,12},{12... | collective-permute-start | bytes 1572872 | tf_op jit(solution)/shard_map/ppermute | solution.py:636
  4.1 15.3 %collective-permute-start.5 = (bf16[144,1024]{1,0:T(8,128)(2,1)S(1)}, bf16[144,1024]{1,0:T(8,128)(2,1)S(1)}, u32[]{:S(2)}, u32[]{:S(2)}) collective-permute-start(bf16[144,1024]{1,0:T(8,128)(2,1)S(1)} %get-tuple-element.53.refs_0_), channel_id=1, source_target_pairs={{0,2},{1,3},{2,0},{3,1},{4,6},{5,7},{6,4},{7,5},{8,10},{9,11},{10,... | collective-permute-start | bytes 884744 | tf_op jit(solution)/shard_map/ppermute | solution.py:28
  6.1 12.8 %collective-permute-start.6 = (bf16[128,1024]{1,0:T(8,128)(2,1)S(1)}, bf16[128,1024]{1,0:T(8,128)(2,1)S(1)}, u32[]{:S(2)}, u32[]{:S(2)}) collective-permute-start(bf16[128,1024]{1,0:T(8,128)(2,1)S(1)} %get-tuple-element.54.refs_1_), channel_id=1, source_target_pairs={{0,2},{1,3},{2,0},{3,1},{4,6},{5,7},{6,4},{7,5},{8,10},{9,11},{10,... | collective-permute-start | bytes 786440 | tf_op jit(solution)/shard_map/ppermute | solution.py:28
  6.2 12.8 %collective-permute-start.4 = (bf16[128,1024]{1,0:T(8,128)(2,1)S(1)}, bf16[128,1024]{1,0:T(8,128)(2,1)S(1)}, u32[]{:S(2)}, u32[]{:S(2)}) collective-permute-start(bf16[128,1024]{1,0:T(8,128)(2,1)S(1)} %get-tuple-element.54.refs_1_), channel_id=1, source_target_pairs={{0,1},{1,0},{2,3},{3,2},{4,5},{5,4},{6,7},{7,6},{8,9},{9,8},{10,11... | collective-permute-start | bytes 786440 | tf_op jit(solution)/shard_map/ppermute | solution.py:28
  6.2 12.2 %collective-permute-start = (bf16[16,1024]{1,0:T(8,128)(2,1)S(1)}, bf16[16,1024]{1,0:T(8,128)(2,1)S(1)}, u32[]{:S(2)}, u32[]{:S(2)}) collective-permute-start(bf16[16,1024]{1,0:T(8,128)(2,1)S(1)} %get-tuple-element.52), channel_id=1, source_target_pairs={{0,4},{4,8},{8,12},{12,16},{16,20},{20,24},{24,28},{28,32},{32,36}... | collective-permute-start | bytes 98312 | tf_op jit(solution)/shard_map/ppermute | solution.py:652
  18.4 7.5 %collective-permute-start.9 = (bf16[1024,256]{1,0:T(8,128)(2,1)}, bf16[1024,256]{1,0:T(8,128)(2,1)S(1)}, u32[]{:S(2)}, u32[]{:S(2)}) collective-permute-start(bf16[1024,256]{1,0:T(8,128)(2,1)} %refs_3_.1), channel_id=1, source_target_pairs={{0,1},{1,0},{2,3},{3,2},{4,5},{5,4},{6,7},{7,6},{8,9},{9,8},{10,11... | collective-permute-start | bytes 1572872 | tf_op jit(solution)/shard_map/ppermute | solution.py:28
  18.4 10.5 %collective-permute-start.11 = (bf16[1024,256]{1,0:T(8,128)(2,1)S(1)}, bf16[1024,256]{1,0:T(8,128)(2,1)S(1)}, u32[]{:S(2)}, u32[]{:S(2)}) collective-permute-start(bf16[1024,256]{1,0:T(8,128)(2,1)S(1)} %collective-permute-done.10.refs_10_.refs_6_), channel_id=1, source_target_pairs={{0,1},{1,0},{2,3},{3,2},{4,5},{5,4},{6,7},{7,6},{8,9},{9,8},{10,11... | collective-permute-start | bytes 1572872 | tf_op jit(solution)/shard_map/ppermute | solution.py:28
  18.9 4.7 %collective-permute-start.3 = (bf16[144,1024]{1,0:T(8,128)(2,1)S(1)}, bf16[144,1024]{1,0:T(8,128)(2,1)S(1)}, u32[]{:S(2)}, u32[]{:S(2)}) collective-permute-start(bf16[144,1024]{1,0:T(8,128)(2,1)S(1)} %get-tuple-element.53.refs_0_), channel_id=1, source_target_pairs={{0,1},{1,0},{2,3},{3,2},{4,5},{5,4},{6,7},{7,6},{8,9},{9,8},{10,11... | collective-permute-start | bytes 884744 | tf_op jit(solution)/shard_map/ppermute | solution.py:28
  19.0 9.8 %collective-permute-start.8 = (bf16[128,1024]{1,0:T(8,128)(2,1)S(1)}, bf16[128,1024]{1,0:T(8,128)(2,1)S(1)}, u32[]{:S(2)}, u32[]{:S(2)}) collective-permute-start(bf16[128,1024]{1,0:T(8,128)(2,1)S(1)} %collective-permute-done.6.refs_5_), channel_id=1, source_target_pairs={{0,1},{1,0},{2,3},{3,2},{4,5},{5,4},{6,7},{7,6},{8,9},{9,8},{10,11... | collective-permute-start | bytes 786440 | tf_op jit(solution)/shard_map/ppermute | solution.py:28
  19.4 9.4 %collective-permute-start.7 = (bf16[144,1024]{1,0:T(8,128)(2,1)S(1)}, bf16[144,1024]{1,0:T(8,128)(2,1)S(1)}, u32[]{:S(2)}, u32[]{:S(2)}) collective-permute-start(bf16[144,1024]{1,0:T(8,128)(2,1)S(1)} %collective-permute-done.5.refs_4_), channel_id=1, source_target_pairs={{0,1},{1,0},{2,3},{3,2},{4,5},{5,4},{6,7},{7,6},{8,9},{9,8},{10,11... | collective-permute-start | bytes 884744 | tf_op jit(solution)/shard_map/ppermute | solution.py:28
  19.5 4.1 %copy-start = (bf16[1024,128]{1,0:T(8,128)(2,1)S(1)}, bf16[1024,128]{1,0:T(8,128)(2,1)}, u32[]{:S(2)}) copy-start(bf16[1024,128]{1,0:T(8,128)(2,1)} %refs_10_.1) | copy-start | bytes 786436
  23.6 18.7 %collective-permute-start.14 = (bf16[1024,128]{1,0:T(8,128)(2,1)S(1)}, bf16[1024,128]{1,0:T(8,128)(2,1)S(1)}, u32[]{:S(2)}, u32[]{:S(2)}) collective-permute-start(bf16[1024,128]{1,0:T(8,128)(2,1)S(1)} %copy-done), channel_id=1, source_target_pairs={{0,6},{2,4},{4,2},{6,0},{1,7},{3,5},{5,3},{7,1},{8,14},{10,12},{12... | collective-permute-start | bytes 786440 | tf_op jit(solution)/shard_map/ppermute | solution.py:636
  25.9 15.9 %collective-permute-start.2 = (bf16[272,1024]{1,0:T(8,128)(2,1)S(1)}, bf16[272,1024]{1,0:T(8,128)(2,1)S(1)}, u32[]{:S(2)}, u32[]{:S(2)}) collective-permute-start(bf16[272,1024]{1,0:T(8,128)(2,1)S(1)} %constant_dynamic-update-slice_fusion.refs_0_), channel_id=1, source_target_pairs={{0,2},{1,3},{2,0},{3,1},{4,6},{5,7},{6,4},{7,5},{8,10},{9,11},{10,... | collective-permute-start | bytes 1671176 | tf_op jit(solution)/shard_map/ppermute | solution.py:28
  28.9 17.9 %collective-permute-start.1 = (bf16[272,1024]{1,0:T(8,128)(2,1)S(1)}, bf16[272,1024]{1,0:T(8,128)(2,1)S(1)}, u32[]{:S(2)}, u32[]{:S(2)}) collective-permute-start(bf16[272,1024]{1,0:T(8,128)(2,1)S(1)} %constant_dynamic-update-slice_fusion.refs_0_), channel_id=1, source_target_pairs={{0,1},{1,0},{2,3},{3,2},{4,5},{5,4},{6,7},{7,6},{8,9},{9,8},{10,11... | collective-permute-start | bytes 1671176 | tf_op jit(solution)/shard_map/ppermute | solution.py:28
  41.8 5.0 %collective-permute-start.12 = (bf16[272,1024]{1,0:T(8,128)(2,1)S(1)}, bf16[272,1024]{1,0:T(8,128)(2,1)S(1)}, u32[]{:S(2)}, u32[]{:S(2)}) collective-permute-start(bf16[272,1024]{1,0:T(8,128)(2,1)S(1)} %collective-permute-done.2.refs_2_), channel_id=1, source_target_pairs={{0,1},{1,0},{2,3},{3,2},{4,5},{5,4},{6,7},{7,6},{8,9},{9,8},{10,11... | collective-permute-start | bytes 1671176 | tf_op jit(solution)/shard_map/ppermute | solution.py:28
  41.8 2.3 %collective-permute-start.13 = (bf16[1024,128]{1,0:T(8,128)(2,1)S(1)}, bf16[1024,128]{1,0:T(8,128)(2,1)S(1)}, u32[]{:S(2)}, u32[]{:S(2)}) collective-permute-start(bf16[1024,128]{1,0:T(8,128)(2,1)S(1)} %copy-done), channel_id=1, source_target_pairs={{0,1},{1,0},{2,3},{3,2},{4,5},{5,4},{6,7},{7,6},{8,9},{9,8},{10,11... | collective-permute-start | bytes 786440 | tf_op jit(solution)/shard_map/ppermute | solution.py:28
  42.3 2.2 %collective-permute-start.15 = (bf16[1024,128]{1,0:T(8,128)(2,1)S(1)}, bf16[1024,128]{1,0:T(8,128)(2,1)S(1)}, u32[]{:S(2)}, u32[]{:S(2)}) collective-permute-start(bf16[1024,128]{1,0:T(8,128)(2,1)S(1)} %collective-permute-done.14.refs_2_.refs_10_), channel_id=1, source_target_pairs={{0,1},{1,0},{2,3},{3,2},{4,5},{5,4},{6,7},{7,6},{8,9},{9,8},{10,11... | collective-permute-start | bytes 786440 | tf_op jit(solution)/shard_map/ppermute | solution.py:28
  55.4 5.9 %collective-permute-start.16 = (bf16[72,512]{1,0:T(8,128)(2,1)S(1)}, bf16[72,512]{1,0:T(8,128)(2,1)S(1)}, u32[]{:S(2)}, u32[]{:S(2)}) collective-permute-start(bf16[72,512]{1,0:T(8,128)(2,1)S(1)} %get-tuple-element.86), channel_id=1, source_target_pairs={{0,4},{4,0},{1,5},{5,1},{2,6},{6,2},{3,7},{7,3},{8,12},{12,8},{9,1... | collective-permute-start | bytes 221192 | tf_op jit(solution)/shard_map/ppermute | solution.py:28
  61.9 6.8 %collective-permute-start.19 = (bf16[72,512]{1,0:T(8,128)(2,1)S(1)}, bf16[72,512]{1,0:T(8,128)(2,1)S(1)}, u32[]{:S(2)}, u32[]{:S(2)}) collective-permute-start(bf16[72,512]{1,0:T(8,128)(2,1)S(1)} %get-tuple-element.89), channel_id=1, source_target_pairs={{0,24},{8,16},{16,8},{24,0},{1,25},{9,17},{17,9},{25,1},{2,26},{10... | collective-permute-start | bytes 221192 | tf_op jit(solution)/shard_map/ppermute | solution.py:28
  64.7 6.0 %collective-permute-start.18 = (bf16[72,512]{1,0:T(8,128)(2,1)S(1)}, bf16[72,512]{1,0:T(8,128)(2,1)S(1)}, u32[]{:S(2)}, u32[]{:S(2)}) collective-permute-start(bf16[72,512]{1,0:T(8,128)(2,1)S(1)} %get-tuple-element.89), channel_id=1, source_target_pairs={{0,16},{8,24},{16,0},{24,8},{1,17},{9,25},{17,1},{25,9},{2,18},{10... | collective-permute-start | bytes 221192 | tf_op jit(solution)/shard_map/ppermute | solution.py:28
  65.5 5.2 %collective-permute-start.17 = (bf16[72,512]{1,0:T(8,128)(2,1)S(1)}, bf16[72,512]{1,0:T(8,128)(2,1)S(1)}, u32[]{:S(2)}, u32[]{:S(2)}) collective-permute-start(bf16[72,512]{1,0:T(8,128)(2,1)S(1)} %get-tuple-element.89), channel_id=1, source_target_pairs={{0,8},{8,0},{16,24},{24,16},{1,9},{9,1},{17,25},{25,17},{2,10},{10... | collective-permute-start | bytes 221192 | tf_op jit(solution)/shard_map/ppermute | solution.py:28
  71.4 10.0 %collective-permute-start.22 = (bf16[72,512]{1,0:T(8,128)(2,1)S(1)}, bf16[72,512]{1,0:T(8,128)(2,1)S(1)}, u32[]{:S(2)}, u32[]{:S(2)}) collective-permute-start(bf16[72,512]{1,0:T(8,128)(2,1)S(1)} %get-tuple-element.92), channel_id=1, source_target_pairs={{0,96},{32,64},{64,32},{96,0},{1,97},{33,65},{65,33},{97,1},{2,98}... | collective-permute-start | bytes 221192 | tf_op jit(solution)/shard_map/ppermute | solution.py:28
  75.6 5.9 %collective-permute-start.21 = (bf16[72,512]{1,0:T(8,128)(2,1)S(1)}, bf16[72,512]{1,0:T(8,128)(2,1)S(1)}, u32[]{:S(2)}, u32[]{:S(2)}) collective-permute-start(bf16[72,512]{1,0:T(8,128)(2,1)S(1)} %get-tuple-element.92), channel_id=1, source_target_pairs={{0,64},{32,96},{64,0},{96,32},{1,65},{33,97},{65,1},{97,33},{2,66}... | collective-permute-start | bytes 221192 | tf_op jit(solution)/shard_map/ppermute | solution.py:28
  75.6 5.9 %collective-permute-start.20 = (bf16[72,512]{1,0:T(8,128)(2,1)S(1)}, bf16[72,512]{1,0:T(8,128)(2,1)S(1)}, u32[]{:S(2)}, u32[]{:S(2)}) collective-permute-start(bf16[72,512]{1,0:T(8,128)(2,1)S(1)} %get-tuple-element.92), channel_id=1, source_target_pairs={{0,32},{32,0},{64,96},{96,64},{1,33},{33,1},{65,97},{97,65},{2,34}... | collective-permute-start | bytes 221192 | tf_op jit(solution)/shard_map/ppermute | solution.py:28

commit v4 on v3

--- a/solution.py
+++ b/solution.py
@@ -146,12 +146,12 @@
     return parts[0] if len(parts) == 1 else jnp.concatenate(parts, 0)
 
 
-def mix_rows(me, start, first_token, pieces, narrows, weights, diffs, slots, consume, branches=(0, 1, 2, 3)):
+def mix_rows(me, start, first_token, pieces, narrows, weights, diffs, slots, consume, branches=(0, 1, 2, 3), ranked=None):
     ratios, widen = weights
     tokens, width = diffs.shape[1:]
     tile = 256
     line = lax.broadcasted_iota(jnp.int32, (tokens, tile), 0)
-    first = line == 0
+    first = lax.broadcasted_iota(jnp.int32, (8, tile), 0) == 0
     opens = line + first_token == start
 
     rank = jnp.zeros((tokens, 256), F32)
@@ -162,12 +162,15 @@
             cols = slice(tile * n, tile * n + tile)
             rows = read_rows(pieces[j], cols).astype(F32)
             x = rows[CTX:]
-            before = jnp.where(first, rows[CTX - 1 : CTX], pltpu.roll(x, 1, 0))
+            before = pltpu.roll(x, 1, 0)
+            before = jnp.concatenate([jnp.where(first, rows[CTX - 1 : CTX], before[0:8]), before[8:]], 0)
             d = jnp.where(opens, 0.0, before) - x
             diffs[j, :, cols] = d
             ratio = ratios[0:1, pl.ds(pl.multiple_of(base + tile * n, tile), tile)]
             parts.append((x + d * ratio).astype(BF16))
         rank = rank + dot(jnp.concatenate(parts, 1), narrows[j][...])
+    if ranked:
+        ranked()
     total = jnp.tanh(rank).astype(BF16)
     hidden = [total[:, 64 * b : 64 * b + 64] for b in range(4)]
 
@@ -213,29 +216,37 @@
 def late_kernel(where_ref, *refs, counts):
     pieces, refs = take_pieces(refs, counts)
     narrows, refs = refs[0:4], refs[4:]
-    ratios, widen, w_k, w_v_far, w_r_far, pair, recept, fading_rows, w_v, w_r, diffs, mixed, ready = refs
+    ratios, widen, w_k_far, w_v_far, w_r_far, pair, recept, fading_rows, w_k, w_v, w_r, diffs, mixed, ready = refs
     channels, width = recept.shape[1], w_k.shape[1]
 
     def fetch(j, i):
         there = pl.ds(pl.multiple_of((where_ref[0] ^ j) * width, width), width)
-        source, target = ((w_v_far, w_v), (w_r_far, w_r))[i]
+        source, target = ((w_k_far, w_k), (w_v_far, w_v), (w_r_far, w_r))[i]
         return pltpu.make_async_copy(source.at[there, :], target.at[j], ready.at[j, i])
 
-    for j in range(4):
-        for i in range(2):
+    def start_fetches(j):
+        for i in range(3):
             fetch(j, i).start()
+
+    start_fetches(0)
+    start_fetches(1)
 
     def slots(j, b):
         return fading_rows.at[j] if b == 0 else mixed.at[j % 2, b - 1]
 
     def consume(j):
+        fetch(j, 0).wait()
         add_product(pair, slice(0, channels), j, slots(j, 1), w_k)
-        fetch(j, 0).wait()
+        fetch(j, 1).wait()
         add_product(pair, slice(channels, 2 * channels), j, slots(j, 2), w_v)
-        fetch(j, 1).wait()
+        fetch(j, 2).wait()
         add_product(recept, slice(None), j, slots(j, 3), w_r)
 
-    mix_rows(where_ref[0], where_ref[1], LAST, pieces, narrows, (ratios, widen), diffs, slots, consume)
+    def ranked():
+        start_fetches(2)
+        start_fetches(3)
+
+    mix_rows(where_ref[0], where_ref[1], LAST, pieces, narrows, (ratios, widen), diffs, slots, consume, ranked=ranked)
 
 
 def decay_kernel(where_ref, rows, *refs):
@@ -326,18 +337,18 @@
 
 
 def project_late(where, pieces, narrows, ratios, widen, w_k, w_v, w_r):
-    width, channels = w_k.shape[1:]
+    width, channels = w_k.shape[0] // 4, w_k.shape[1]
     counts = tuple(len(p) for p in pieces)
     tokens = sum(a.shape[0] for a in pieces[0]) - CTX
     operands = [a for p in pieces for a in p] + narrows
     return pl.pallas_call(
         functools.partial(late_kernel, counts=counts),
-        in_specs=[SMEM] + [VMEM] * (len(operands) + 3) + [pl.BlockSpec(memory_space=pltpu.HBM)] * 2,
-        out_specs=[VMEM] * 5,
+        in_specs=[SMEM] + [VMEM] * (len(operands) + 2) + [pl.BlockSpec(memory_space=pltpu.HBM)] * 3,
+        out_specs=[VMEM] * 6,
         scratch_shapes=[
             pltpu.VMEM((4, tokens, width), F32),
             pltpu.VMEM((2, 3, tokens, width), BF16),
-            pltpu.SemaphoreType.DMA((4, 2)),
+            pltpu.SemaphoreType.DMA((4, 3)),
         ],
         out_shape=[
             pltpu.VMEM((tokens, 2 * channels), F32),
@@ -345,10 +356,11 @@
             pltpu.VMEM((4, tokens, width), BF16),
             pltpu.VMEM((4, width, channels), BF16),
             pltpu.VMEM((4, width, channels), BF16),
+            pltpu.VMEM((4, width, channels), BF16),
         ],
         compiler_params=pltpu.CompilerParams(vmem_limit_bytes=(4 * 1024 + 40 * tokens) * 1024),
         cost_estimate=pl.CostEstimate(flops=25 * 10**6 * tokens, bytes_accessed=17 * 10**6, transcendentals=0),
-    )(where, *operands, *map(in_vmem, (ratios, widen, w_k)), in_hbm(w_v), in_hbm(w_r))
+    )(where, *operands, *map(in_vmem, (ratios, widen)), *map(in_hbm, (w_k, w_v, w_r)))
 
 
 def decay_late(where, rows, fadings, fade_widen, anchor, sums, pair):
@@ -572,21 +584,23 @@
     (_, incoming), _ = along_axis(where_ref[place], own, received, (before[SUB : SUB + 1], before[0:SUB]))
     incoming = incoming.astype(BF16)
     channels = gain.shape[1]
-    lane = lax.broadcasted_iota(jnp.int32, (SUB, 128), 1)
-    row = lax.broadcasted_iota(jnp.int32, (128, 128), 0)
-    col = lax.broadcasted_iota(jnp.int32, (128, 128), 1)
+    wide = 256
+    lane = lax.broadcasted_iota(jnp.int32, (SUB, wide), 1) // GROUP
+    row = lax.broadcasted_iota(jnp.int32, (wide, wide), 0)
+    col = lax.broadcasted_iota(jnp.int32, (wide, wide), 1)
     average = jnp.where((row // GROUP) == (col // GROUP), 1.0 / GROUP, 0.0).astype(BF16)
+    blocks = []
+    for p in range(channels // wide):
+        st = incoming[:, wide * p : wide * p + wide]
+        blocks.append(jnp.concatenate([jnp.where(lane == h, st, jnp.zeros_like(st)) for h in range(wide // GROUP)], 0))
     copies = []
     at = 0
     for i in range(parts):
         rows = slice(at, at + locals_[i].shape[0])
         at = rows.stop
-        for p in range(channels // 128):
-            cols = slice(128 * p, 128 * p + 128)
-            st = incoming[:, cols]
-            zero = jnp.zeros_like(st)
-            st = jnp.concatenate([jnp.where(lane < GROUP, st, zero), jnp.where(lane < GROUP, zero, st)], 0)
-            o = locals_[i][:, cols] + dot_nt(queries[i][:, cols], st)
+        for p in range(channels // wide):
+            cols = slice(wide * p, wide * p + wide)
+            o = locals_[i][:, cols] + dot_nt(queries[i][:, cols], blocks[p])
             centred = o - dot(o.astype(BF16), average)
             variance = dot((centred * centred).astype(BF16), average)
             normed = centred * lax.rsqrt(variance + 0.00064)
@@ -656,8 +670,8 @@
     far_early = across(own_early)
     near_early = partner(own_early)
     sums = jnp.asarray(sum_rows(), BF16)
-    widen, w_k, ratios, narrow, fade_widen, anchor, sums, reward, gain, shift, fading = load(
-        where, ("lanes", blending_widen_operand), ("rows", lookup_weights), ("plain", blending_ratios),
+    widen, ratios, narrow, fade_widen, anchor, sums, reward, gain, shift, fading = load(
+        where, ("lanes", blending_widen_operand), ("plain", blending_ratios),
         ("plain", blending_narrow_operand), ("plain", fading_widen_operand), ("plain", fading_anchor[None]),
         ("plain", sums), ("plain", immediate_reward[None]), ("plain", group_scaling_weight[None]),
         ("plain", group_scaling_shift[None]), ("plain", fading_narrow_operand),
@@ -669,8 +683,8 @@
     narrows = [narrow, near_narrow, far_narrow, next_narrow]
     fadings = [fading, near_fading, far_fading, next_fading]
     pieces = [own_late, [near_late_a, near_late_b], [far_late_a, far_late_b], [next_late_a, next_late_b]]
-    late, late_recept, fading_rows, w_v, w_r = project_late(
-        where, pieces, narrows, ratios, widen, w_k, payload_weights, acceptance_weights
+    late, late_recept, fading_rows, w_k, w_v, w_r = project_late(
+        where, pieces, narrows, ratios, widen, lookup_weights, payload_weights, acceptance_weights
     )
     far_early, late = lax.optimization_barrier((far_early, late))
     late_decay, partial, reach, late_whole = decay_late(where, fading_rows, fadings, fade_widen, anchor, sums, late)

time: 85.8 us -> 83.9 us (0.978)
  Pallas kernels: 43.2 us -> 41.5 us
    pallas_call x1, Pallas kernels: 4.05 us -> 2.79 us  [load(): pl.pallas_call(functools.partial(load_kernel, kinds=kinds), in_specs=[SME...]
  transfers between devices with their start and end apart: 23 -> 23, of which waited for: 6 -> 5; matrix products, arithmetic and copies ran while one was open for 0% -> 0% of each run, Pallas kernels for 36% -> 36%
where the time goes in v4:
time: 83.9 us; the launch traced here: 82.5 us
  Pallas kernels  41.5 us (49%)
  starting transfers between devices  23.5 us (28%)
  waiting for transfers between devices  16.3 us (19%)
  between operations  1.01 us (1%)
    ppermute x20, starting transfers between devices, xor_permute(): return lax.ppermute(array, axes, [(i, i ^ flip) for i in range(length)])  17 us
    pallas_call x1, Pallas kernels, project_late(): pl.pallas_call(functools.partial(late_kernel, counts=counts), in_specs=[S...  10.4 us
    pallas_call x2, Pallas kernels, local_outputs(): pl.pallas_call(functools.partial(local_kernel, first=numbers[0], count=le...  9.74 us
    ppermute x1, waiting for transfers between devices, inner(): before = lax.ppermute(last, SEQ, [(i, i + 1) for i in range(shards - 1)])  9.43 us
    pallas_call x1, Pallas kernels, project_early(): pl.pallas_call(functools.partial(early_kernel, counts=counts), in_specs=[...  8.24 us
    ppermute x20, waiting for transfers between devices, xor_permute(): return lax.ppermute(array, axes, [(i, i ^ flip) for i in range(length)])  6.86 us
    ppermute x2, starting transfers between devices, across_far(): return lax.ppermute(a, ('y_hi', 'y_lo'), [(i, i ^ 3) for i in range(4)])  3.86 us
    pallas_call x1, Pallas kernels, load(): pl.pallas_call(functools.partial(load_kernel, kinds=kinds), in_specs=[SME...  2.79 us
  transfers between devices with their start and end apart: 23, of which 5 were waited for; matrix products, arithmetic and copies ran while one was open for 0% of the time, Pallas kernels for 36%

profile of v4, /device:TPU:8, one launch (start us, length us, event | category | flops | bytes accessed | tf_op | source)
XLA Modules:
  0.0 82.5 jit_solution(9019657849770549507)
XLA Ops:
  0.0 1.6 %collective-permute-start.10 = (bf16[1024,256]{1,0:T(8,128)(2,1)}, bf16[1024,256]{1,0:T(8,128)(2,1)S(1)}, u32[]{:S(2)}, u32[]{:S(2)}) collective-permute-start(bf16[1024,256]{1,0:T(8,128)(2,1)} %refs_2_.1), channel_id=1, source_target_pairs={{0,6},{2,4},{4,2},{6,0},{1,7},{3,5},{5,3},{7,1},{8,14},{10,12},{12... | collective-permute-start | bytes 1572872 | tf_op jit(solution)/shard_map/ppermute | solution.py:650
  2.3 1.8 %shard_map.146 = (bf16[144,1024]{1,0:T(8,128)(2,1)S(1)}, bf16[128,1024]{1,0:T(8,128)(2,1)S(1)}, bf16[272,1024]{1,0:T(8,128)(2,1)S(1)}, bf16[16,1024]{1,0:T(8,128)(2,1)S(1)}) custom-call(s32[5]{0:T(128)S(1)} %stack.19.where_ref, bf16[512,1024]{1,0:T(8,128)(2,1)} %x.1), custom_call_target="tpu_custom_call" | custom-call | flops 1000000 | bytes 2000000 | tf_op jit(solution)/shard_map/pallas_call | solution.py:87
  4.1 2.0 %collective-permute-start.5 = (bf16[144,1024]{1,0:T(8,128)(2,1)S(1)}, bf16[144,1024]{1,0:T(8,128)(2,1)S(1)}, u32[]{:S(2)}, u32[]{:S(2)}) collective-permute-start(bf16[144,1024]{1,0:T(8,128)(2,1)S(1)} %get-tuple-element.53.refs_0_), channel_id=1, source_target_pairs={{0,2},{1,3},{2,0},{3,1},{4,6},{5,7},{6,4},{7,5},{8,10},{9,11},{10,... | collective-permute-start | bytes 884744 | tf_op jit(solution)/shard_map/ppermute | solution.py:28
  6.2 2.7 %collective-permute-start = (bf16[16,1024]{1,0:T(8,128)(2,1)S(1)}, bf16[16,1024]{1,0:T(8,128)(2,1)S(1)}, u32[]{:S(2)}, u32[]{:S(2)}) collective-permute-start(bf16[16,1024]{1,0:T(8,128)(2,1)S(1)} %get-tuple-element.52), channel_id=1, source_target_pairs={{0,4},{4,8},{8,12},{12,16},{16,20},{20,24},{24,28},{28,32},{32,36}... | collective-permute-start | bytes 98312 | tf_op jit(solution)/shard_map/ppermute | solution.py:666
  9.0 9.4 %collective-permute-done = bf16[16,1024]{1,0:T(8,128)(2,1)S(1)} collective-permute-done((bf16[16,1024]{1,0:T(8,128)(2,1)S(1)}, bf16[16,1024]{1,0:T(8,128)(2,1)S(1)}, u32[]{:S(2)}, u32[]{:S(2)}) %collective-permute-start) | collective-permute-done | bytes 32800 | tf_op jit(solution)/shard_map/ppermute | solution.py:666
  19.5 2.8 %shard_map.145 = (bf16[4,4,64,1024]{3,2,1,0:T(8,128)(2,1)S(1)}, f32[5,4096]{1,0:T(8,128)S(1)}, bf16[1024,256]{1,0:T(8,128)(2,1)S(1)}, bf16[128,512]{1,0:T(8,128)...) custom-call(s32[5]{0:T(128)S(1)} %stack.19.where_ref, ...), custom_call_target="tpu_custom_call" | custom-call | flops 3000000000 | bytes 8000000 | tf_op jit(solution)/shard_map/pallas_call | solution.py:133
  22.4 2.3 %collective-permute-start.14 = (bf16[1024,128]{1,0:T(8,128)(2,1)S(1)}, bf16[1024,128]{1,0:T(8,128)(2,1)S(1)}, u32[]{:S(2)}, u32[]{:S(2)}) collective-permute-start(bf16[1024,128]{1,0:T(8,128)(2,1)S(1)} %copy-done), channel_id=1, source_target_pairs={{0,6},{2,4},{4,2},{6,0},{1,7},{3,5},{5,3},{7,1},{8,14},{10,12},{12... | collective-permute-start | bytes 786440 | tf_op jit(solution)/shard_map/ppermute | solution.py:650
  24.6 3.0 %collective-permute-start.2 = (bf16[272,1024]{1,0:T(8,128)(2,1)S(1)}, bf16[272,1024]{1,0:T(8,128)(2,1)S(1)}, u32[]{:S(2)}, u32[]{:S(2)}) collective-permute-start(bf16[272,1024]{1,0:T(8,128)(2,1)S(1)} %constant_dynamic-update-slice_fusion.refs_0_), channel_id=1, source_target_pairs={{0,2},{1,3},{2,0},{3,1},{4,6},{5,7},{6,4},{7,5},{8,10},{9,11},{10,... | collective-permute-start | bytes 1671176 | tf_op jit(solution)/shard_map/ppermute | solution.py:28
  27.6 10.4 %shard_map.147 = (f32[256,1024]{1,0:T(8,128)S(1)}, f32[256,512]{1,0:T(8,128)S(1)}, bf16[4,256,1024]{2,1,0:T(8,128)(2,1)S(1)}, bf16[4,1024,512]{2,1,0:T(8,128)(2,...) custom-call(s32[5]{0:T(128)S(1)} %stack.19.where_ref, ...), custom_call_target="tpu_custom_call" | custom-call | flops 6400000000 | bytes 17000000 | tf_op jit(solution)/shard_map/pallas_call | solution.py:344
  38.0 2.5 %collective-permute-done.2.refs_2_ = bf16[272,1024]{1,0:T(8,128)(2,1)S(1)} collective-permute-done((bf16[272,1024]{1,0:T(8,128)(2,1)S(1)}, bf16[272,1024]{1,0:T(8,128)(2,1)S(1)}, u32[]{:S(2)}, u32[]{:S(2)}) %collective-permute-start.2) | collective-permute-done | bytes 557088 | tf_op jit(solution)/shard_map/ppermute | solution.py:28
  41.1 1.8 %collective-permute-done.13.refs_1_.refs_9_ = bf16[1024,128]{1,0:T(8,128)(2,1)S(1)} collective-permute-done((bf16[1024,128]{1,0:T(8,128)(2,1)S(1)}, bf16[1024,128]{1,0:T(8,128)(2,1)S(1)}, u32[]{:S(2)}, u32[]{:S(2)}) %collective-permute-start.13) | collective-permute-done | bytes 262176 | tf_op jit(solution)/shard_map/ppermute | solution.py:28
  43.2 2.3 %shard_map.148 = (f32[256,512]{1,0:T(8,128)S(1)}, f32[4,64,512]{2,1,0:T(8,128)S(1)}, f32[8,512]{1,0:T(8,128)S(1)}, f32[72,512]{1,0:T(8,128)S(1)}) custom-call(s32[5]{0:T(128)S(1)} %stack.19.where_ref, bf16[4,256,1024]{2,1,0:T(8,128)(2,1)S(1)} %get-tuple-element.65.rows, bf16[1024,128]{1,0:T(8,128)(2,1)S(1)} %get-tuple-element.60.refs_0_.refs_8_, ...), custom_call_target="tpu_custom_call" | custom-call | flops 1000000000 | bytes 2000000 | tf_op jit(solution)/shard_map/pallas_call | solution.py:369
  45.6 8.2 %shard_map.149 = (f32[256,1024]{1,0:T(8,128)S(1)}, f32[256,512]{1,0:T(8,128)S(1)}, bf16[8,64,512]{2,1,0:T(8,128)(2,1)S(1)}, f32[8,512]{1,0:T(8,128)S(1)}, f32[72...) custom-call(s32[5]{0:T(128)S(1)} %stack.19.where_ref, ...), custom_call_target="tpu_custom_call" | custom-call | flops 6400000000 | bytes 17000000 | tf_op jit(solution)/shard_map/pallas_call | solution.py:388
  53.8 1.0 %collective-permute-start.16 = (bf16[72,512]{1,0:T(8,128)(2,1)S(1)}, bf16[72,512]{1,0:T(8,128)(2,1)S(1)}, u32[]{:S(2)}, u32[]{:S(2)}) collective-permute-start(bf16[72,512]{1,0:T(8,128)(2,1)S(1)} %get-tuple-element.86), channel_id=1, source_target_pairs={{0,4},{4,0},{1,5},{5,1},{2,6},{6,2},{3,7},{7,3},{8,12},{12,8},{9,1... | collective-permute-start | bytes 221192 | tf_op jit(solution)/shard_map/ppermute | solution.py:28
  54.8 4.9 %shard_map.152 = (f32[256,512]{1,0:T(8,128)S(1)}, bf16[256,512]{1,0:T(8,128)(2,1)S(1)}) custom-call(s32[5]{0:T(128)S(1)} %stack.19.where_ref, bf16[512,128]{1,0:T(8,128)(2,1)S(1)} %get-tuple-element.49.refs_6_.refs_18_.sums, f32[1,512]{1,0:T(1,128)S(1)} %get-tuple-element.50.reward, bf16[8,64,512]{2,1,0:T(8,128)(2,1)S(1)} %get-tuple-element.70.entering, ...), custom_call_target="tpu_custom_call" | custom-call | flops 2000000000 | bytes 3000000 | tf_op jit(solution)/shard_map/pallas_call | solution.py:498
  60.3 2.8 %collective-permute-start.19 = (bf16[72,512]{1,0:T(8,128)(2,1)S(1)}, bf16[72,512]{1,0:T(8,128)(2,1)S(1)}, u32[]{:S(2)}, u32[]{:S(2)}) collective-permute-start(bf16[72,512]{1,0:T(8,128)(2,1)S(1)} %get-tuple-element.89), channel_id=1, source_target_pairs={{0,24},{8,16},{16,8},{24,0},{1,25},{9,17},{17,9},{25,1},{2,26},{10... | collective-permute-start | bytes 221192 | tf_op jit(solution)/shard_map/ppermute | solution.py:28
  63.2 0.8 collective-permute-start.18
  64.5 2.6 %shard_map.150.recept = f32[256,512]{1,0:T(8,128)S(1)} custom-call(s32[5]{0:T(128)S(1)} %stack.19.where_ref, bf16[272,1024]{1,0:T(8,128)(2,1)S(1)} %constant_dynamic-update-slice_fusion.refs_0_, bf16[272,1024]{1,0:T(8,128)(2,1)S(1)} %collective-permute-done.1.refs_1_, bf16[272,1024]{1,0:T(8,128)(2,1)S(1)} %collective-permute-done.2.refs_2_, ...), custom_call_target="tpu_custom_call" | custom-call | flops 2000000000 | bytes 5000000 | tf_op jit(solution)/shard_map/pallas_call | solution.py:328
  67.1 2.1 %collective-permute-done.18.refs_3_ = bf16[72,512]{1,0:T(8,128)(2,1)S(1)} collective-permute-done((bf16[72,512]{1,0:T(8,128)(2,1)S(1)}, bf16[72,512]{1,0:T(8,128)(2,1)S(1)}, u32[]{:S(2)}, u32[]{:S(2)}) %collective-permute-start.18) | collective-permute-done | bytes 73760 | tf_op jit(solution)/shard_map/ppermute | solution.py:28
  69.2 0.7 shard_map.154
  69.9 4.1 %collective-permute-start.22 = (bf16[72,512]{1,0:T(8,128)(2,1)S(1)}, bf16[72,512]{1,0:T(8,128)(2,1)S(1)}, u32[]{:S(2)}, u32[]{:S(2)}) collective-permute-start(bf16[72,512]{1,0:T(8,128)(2,1)S(1)} %get-tuple-element.92), channel_id=1, source_target_pairs={{0,96},{32,64},{64,32},{96,0},{1,97},{33,65},{65,33},{97,1},{2,98}... | collective-permute-start | bytes 221192 | tf_op jit(solution)/shard_map/ppermute | solution.py:28
  74.0 0.9 %collective-permute-start.20 = (bf16[72,512]{1,0:T(8,128)(2,1)S(1)}, bf16[72,512]{1,0:T(8,128)(2,1)S(1)}, u32[]{:S(2)}, u32[]{:S(2)}) collective-permute-start(bf16[72,512]{1,0:T(8,128)(2,1)S(1)} %get-tuple-element.92), channel_id=1, source_target_pairs={{0,32},{32,0},{64,96},{96,64},{1,33},{33,1},{65,97},{97,65},{2,34}... | collective-permute-start | bytes 221192 | tf_op jit(solution)/shard_map/ppermute | solution.py:28
  75.0 4.9 %shard_map.151 = (f32[256,512]{1,0:T(8,128)S(1)}, bf16[256,512]{1,0:T(8,128)(2,1)S(1)}) custom-call(s32[5]{0:T(128)S(1)} %stack.19.where_ref, bf16[512,128]{1,0:T(8,128)(2,1)S(1)} %get-tuple-element.49.refs_6_.refs_18_.sums, f32[1,512]{1,0:T(1,128)S(1)} %get-tuple-element.50.reward, bf16[8,64,512]{2,1,0:T(8,128)(2,1)S(1)} %get-tuple-element.70.entering, ...), custom_call_target="tpu_custom_call" | custom-call | flops 2000000000 | bytes 3000000 | tf_op jit(solution)/shard_map/pallas_call | solution.py:498
  79.9 2.4 %shard_map.155 = bf16[512,512]{1,0:T(8,128)(2,1)} custom-call(s32[5]{0:T(128)S(1)} %stack.19.where_ref, f32[256,512]{1,0:T(8,128)S(1)} %get-tuple-element.77.refs_0_, f32[256,512]{1,0:T(8,128)S(1)} %get-tuple-element.80.refs_1_, bf16[256,512]{1,0:T(8,128)(2,1)S(1)} %get-tuple-element.81.refs_2_, bf16[256,512]{1,0:T(8,128)(2,1)S(1)} %get-tuple-element.82.refs_3_, ...), custom_call_target="tpu_custom_call" | custom-call | flops 1000000000 | bytes 2000000 | tf_op jit(solution)/shard_map/pallas_call | solution.py:617
  (37 shorter events, 3.4 us)
Async XLA Ops:
  0.0 18.4 %collective-permute-start.10 = (bf16[1024,256]{1,0:T(8,128)(2,1)}, bf16[1024,256]{1,0:T(8,128)(2,1)S(1)}, u32[]{:S(2)}, u32[]{:S(2)}) collective-permute-start(bf16[1024,256]{1,0:T(8,128)(2,1)} %refs_2_.1), channel_id=1, source_target_pairs={{0,6},{2,4},{4,2},{6,0},{1,7},{3,5},{5,3},{7,1},{8,14},{10,12},{12... | collective-permute-start | bytes 1572872 | tf_op jit(solution)/shard_map/ppermute | solution.py:650
  4.1 15.3 %collective-permute-start.5 = (bf16[144,1024]{1,0:T(8,128)(2,1)S(1)}, bf16[144,1024]{1,0:T(8,128)(2,1)S(1)}, u32[]{:S(2)}, u32[]{:S(2)}) collective-permute-start(bf16[144,1024]{1,0:T(8,128)(2,1)S(1)} %get-tuple-element.53.refs_0_), channel_id=1, source_target_pairs={{0,2},{1,3},{2,0},{3,1},{4,6},{5,7},{6,4},{7,5},{8,10},{9,11},{10,... | collective-permute-start | bytes 884744 | tf_op jit(solution)/shard_map/ppermute | solution.py:28
  6.1 12.8 %collective-permute-start.6 = (bf16[128,1024]{1,0:T(8,128)(2,1)S(1)}, bf16[128,1024]{1,0:T(8,128)(2,1)S(1)}, u32[]{:S(2)}, u32[]{:S(2)}) collective-permute-start(bf16[128,1024]{1,0:T(8,128)(2,1)S(1)} %get-tuple-element.54.refs_1_), channel_id=1, source_target_pairs={{0,2},{1,3},{2,0},{3,1},{4,6},{5,7},{6,4},{7,5},{8,10},{9,11},{10,... | collective-permute-start | bytes 786440 | tf_op jit(solution)/shard_map/ppermute | solution.py:28
  6.2 12.8 %collective-permute-start.4 = (bf16[128,1024]{1,0:T(8,128)(2,1)S(1)}, bf16[128,1024]{1,0:T(8,128)(2,1)S(1)}, u32[]{:S(2)}, u32[]{:S(2)}) collective-permute-start(bf16[128,1024]{1,0:T(8,128)(2,1)S(1)} %get-tuple-element.54.refs_1_), channel_id=1, source_target_pairs={{0,1},{1,0},{2,3},{3,2},{4,5},{5,4},{6,7},{7,6},{8,9},{9,8},{10,11... | collective-permute-start | bytes 786440 | tf_op jit(solution)/shard_map/ppermute | solution.py:28
  6.2 12.2 %collective-permute-start = (bf16[16,1024]{1,0:T(8,128)(2,1)S(1)}, bf16[16,1024]{1,0:T(8,128)(2,1)S(1)}, u32[]{:S(2)}, u32[]{:S(2)}) collective-permute-start(bf16[16,1024]{1,0:T(8,128)(2,1)S(1)} %get-tuple-element.52), channel_id=1, source_target_pairs={{0,4},{4,8},{8,12},{12,16},{16,20},{20,24},{24,28},{28,32},{32,36}... | collective-permute-start | bytes 98312 | tf_op jit(solution)/shard_map/ppermute | solution.py:666
  18.4 6.2 %collective-permute-start.9 = (bf16[1024,256]{1,0:T(8,128)(2,1)}, bf16[1024,256]{1,0:T(8,128)(2,1)S(1)}, u32[]{:S(2)}, u32[]{:S(2)}) collective-permute-start(bf16[1024,256]{1,0:T(8,128)(2,1)} %refs_2_.1), channel_id=1, source_target_pairs={{0,1},{1,0},{2,3},{3,2},{4,5},{5,4},{6,7},{7,6},{8,9},{9,8},{10,11... | collective-permute-start | bytes 1572872 | tf_op jit(solution)/shard_map/ppermute | solution.py:28
  18.4 9.2 %collective-permute-start.11 = (bf16[1024,256]{1,0:T(8,128)(2,1)S(1)}, bf16[1024,256]{1,0:T(8,128)(2,1)S(1)}, u32[]{:S(2)}, u32[]{:S(2)}) collective-permute-start(bf16[1024,256]{1,0:T(8,128)(2,1)S(1)} %collective-permute-done.10.refs_10_.refs_6_), channel_id=1, source_target_pairs={{0,1},{1,0},{2,3},{3,2},{4,5},{5,4},{6,7},{7,6},{8,9},{9,8},{10,11... | collective-permute-start | bytes 1572872 | tf_op jit(solution)/shard_map/ppermute | solution.py:28
  18.9 3.4 %collective-permute-start.3 = (bf16[144,1024]{1,0:T(8,128)(2,1)S(1)}, bf16[144,1024]{1,0:T(8,128)(2,1)S(1)}, u32[]{:S(2)}, u32[]{:S(2)}) collective-permute-start(bf16[144,1024]{1,0:T(8,128)(2,1)S(1)} %get-tuple-element.53.refs_0_), channel_id=1, source_target_pairs={{0,1},{1,0},{2,3},{3,2},{4,5},{5,4},{6,7},{7,6},{8,9},{9,8},{10,11... | collective-permute-start | bytes 884744 | tf_op jit(solution)/shard_map/ppermute | solution.py:28
  19.0 8.6 %collective-permute-start.8 = (bf16[128,1024]{1,0:T(8,128)(2,1)S(1)}, bf16[128,1024]{1,0:T(8,128)(2,1)S(1)}, u32[]{:S(2)}, u32[]{:S(2)}) collective-permute-start(bf16[128,1024]{1,0:T(8,128)(2,1)S(1)} %collective-permute-done.6.refs_5_), channel_id=1, source_target_pairs={{0,1},{1,0},{2,3},{3,2},{4,5},{5,4},{6,7},{7,6},{8,9},{9,8},{10,11... | collective-permute-start | bytes 786440 | tf_op jit(solution)/shard_map/ppermute | solution.py:28
  19.4 8.2 %collective-permute-start.7 = (bf16[144,1024]{1,0:T(8,128)(2,1)S(1)}, bf16[144,1024]{1,0:T(8,128)(2,1)S(1)}, u32[]{:S(2)}, u32[]{:S(2)}) collective-permute-start(bf16[144,1024]{1,0:T(8,128)(2,1)S(1)} %collective-permute-done.5.refs_4_), channel_id=1, source_target_pairs={{0,1},{1,0},{2,3},{3,2},{4,5},{5,4},{6,7},{7,6},{8,9},{9,8},{10,11... | collective-permute-start | bytes 884744 | tf_op jit(solution)/shard_map/ppermute | solution.py:28
  19.5 2.8 %copy-start = (bf16[1024,128]{1,0:T(8,128)(2,1)S(1)}, bf16[1024,128]{1,0:T(8,128)(2,1)}, u32[]{:S(2)}) copy-start(bf16[1024,128]{1,0:T(8,128)(2,1)} %refs_9_.1) | copy-start | bytes 786436
  22.4 18.7 %collective-permute-start.14 = (bf16[1024,128]{1,0:T(8,128)(2,1)S(1)}, bf16[1024,128]{1,0:T(8,128)(2,1)S(1)}, u32[]{:S(2)}, u32[]{:S(2)}) collective-permute-start(bf16[1024,128]{1,0:T(8,128)(2,1)S(1)} %copy-done), channel_id=1, source_target_pairs={{0,6},{2,4},{4,2},{6,0},{1,7},{3,5},{5,3},{7,1},{8,14},{10,12},{12... | collective-permute-start | bytes 786440 | tf_op jit(solution)/shard_map/ppermute | solution.py:650
  24.6 15.9 %collective-permute-start.2 = (bf16[272,1024]{1,0:T(8,128)(2,1)S(1)}, bf16[272,1024]{1,0:T(8,128)(2,1)S(1)}, u32[]{:S(2)}, u32[]{:S(2)}) collective-permute-start(bf16[272,1024]{1,0:T(8,128)(2,1)S(1)} %constant_dynamic-update-slice_fusion.refs_0_), channel_id=1, source_target_pairs={{0,2},{1,3},{2,0},{3,1},{4,6},{5,7},{6,4},{7,5},{8,10},{9,11},{10,... | collective-permute-start | bytes 1671176 | tf_op jit(solution)/shard_map/ppermute | solution.py:28
  27.6 17.9 %collective-permute-start.1 = (bf16[272,1024]{1,0:T(8,128)(2,1)S(1)}, bf16[272,1024]{1,0:T(8,128)(2,1)S(1)}, u32[]{:S(2)}, u32[]{:S(2)}) collective-permute-start(bf16[272,1024]{1,0:T(8,128)(2,1)S(1)} %constant_dynamic-update-slice_fusion.refs_0_), channel_id=1, source_target_pairs={{0,1},{1,0},{2,3},{3,2},{4,5},{5,4},{6,7},{7,6},{8,9},{9,8},{10,11... | collective-permute-start | bytes 1671176 | tf_op jit(solution)/shard_map/ppermute | solution.py:28
  40.5 5.0 %collective-permute-start.12 = (bf16[272,1024]{1,0:T(8,128)(2,1)S(1)}, bf16[272,1024]{1,0:T(8,128)(2,1)S(1)}, u32[]{:S(2)}, u32[]{:S(2)}) collective-permute-start(bf16[272,1024]{1,0:T(8,128)(2,1)S(1)} %collective-permute-done.2.refs_2_), channel_id=1, source_target_pairs={{0,1},{1,0},{2,3},{3,2},{4,5},{5,4},{6,7},{7,6},{8,9},{9,8},{10,11... | collective-permute-start | bytes 1671176 | tf_op jit(solution)/shard_map/ppermute | solution.py:28
  40.5 2.3 %collective-permute-start.13 = (bf16[1024,128]{1,0:T(8,128)(2,1)S(1)}, bf16[1024,128]{1,0:T(8,128)(2,1)S(1)}, u32[]{:S(2)}, u32[]{:S(2)}) collective-permute-start(bf16[1024,128]{1,0:T(8,128)(2,1)S(1)} %copy-done), channel_id=1, source_target_pairs={{0,1},{1,0},{2,3},{3,2},{4,5},{5,4},{6,7},{7,6},{8,9},{9,8},{10,11... | collective-permute-start | bytes 786440 | tf_op jit(solution)/shard_map/ppermute | solution.py:28
  41.0 2.2 %collective-permute-start.15 = (bf16[1024,128]{1,0:T(8,128)(2,1)S(1)}, bf16[1024,128]{1,0:T(8,128)(2,1)S(1)}, u32[]{:S(2)}, u32[]{:S(2)}) collective-permute-start(bf16[1024,128]{1,0:T(8,128)(2,1)S(1)} %collective-permute-done.14.refs_2_.refs_10_), channel_id=1, source_target_pairs={{0,1},{1,0},{2,3},{3,2},{4,5},{5,4},{6,7},{7,6},{8,9},{9,8},{10,11... | collective-permute-start | bytes 786440 | tf_op jit(solution)/shard_map/ppermute | solution.py:28
  53.8 5.9 %collective-permute-start.16 = (bf16[72,512]{1,0:T(8,128)(2,1)S(1)}, bf16[72,512]{1,0:T(8,128)(2,1)S(1)}, u32[]{:S(2)}, u32[]{:S(2)}) collective-permute-start(bf16[72,512]{1,0:T(8,128)(2,1)S(1)} %get-tuple-element.86), channel_id=1, source_target_pairs={{0,4},{4,0},{1,5},{5,1},{2,6},{6,2},{3,7},{7,3},{8,12},{12,8},{9,1... | collective-permute-start | bytes 221192 | tf_op jit(solution)/shard_map/ppermute | solution.py:28
  60.3 6.8 %collective-permute-start.19 = (bf16[72,512]{1,0:T(8,128)(2,1)S(1)}, bf16[72,512]{1,0:T(8,128)(2,1)S(1)}, u32[]{:S(2)}, u32[]{:S(2)}) collective-permute-start(bf16[72,512]{1,0:T(8,128)(2,1)S(1)} %get-tuple-element.89), channel_id=1, source_target_pairs={{0,24},{8,16},{16,8},{24,0},{1,25},{9,17},{17,9},{25,1},{2,26},{10... | collective-permute-start | bytes 221192 | tf_op jit(solution)/shard_map/ppermute | solution.py:28
  63.2 6.0 %collective-permute-start.18 = (bf16[72,512]{1,0:T(8,128)(2,1)S(1)}, bf16[72,512]{1,0:T(8,128)(2,1)S(1)}, u32[]{:S(2)}, u32[]{:S(2)}) collective-permute-start(bf16[72,512]{1,0:T(8,128)(2,1)S(1)} %get-tuple-element.89), channel_id=1, source_target_pairs={{0,16},{8,24},{16,0},{24,8},{1,17},{9,25},{17,1},{25,9},{2,18},{10... | collective-permute-start | bytes 221192 | tf_op jit(solution)/shard_map/ppermute | solution.py:28
  64.0 5.2 %collective-permute-start.17 = (bf16[72,512]{1,0:T(8,128)(2,1)S(1)}, bf16[72,512]{1,0:T(8,128)(2,1)S(1)}, u32[]{:S(2)}, u32[]{:S(2)}) collective-permute-start(bf16[72,512]{1,0:T(8,128)(2,1)S(1)} %get-tuple-element.89), channel_id=1, source_target_pairs={{0,8},{8,0},{16,24},{24,16},{1,9},{9,1},{17,25},{25,17},{2,10},{10... | collective-permute-start | bytes 221192 | tf_op jit(solution)/shard_map/ppermute | solution.py:28
  69.9 10.0 %collective-permute-start.22 = (bf16[72,512]{1,0:T(8,128)(2,1)S(1)}, bf16[72,512]{1,0:T(8,128)(2,1)S(1)}, u32[]{:S(2)}, u32[]{:S(2)}) collective-permute-start(bf16[72,512]{1,0:T(8,128)(2,1)S(1)} %get-tuple-element.92), channel_id=1, source_target_pairs={{0,96},{32,64},{64,32},{96,0},{1,97},{33,65},{65,33},{97,1},{2,98}... | collective-permute-start | bytes 221192 | tf_op jit(solution)/shard_map/ppermute | solution.py:28
  74.0 5.9 %collective-permute-start.21 = (bf16[72,512]{1,0:T(8,128)(2,1)S(1)}, bf16[72,512]{1,0:T(8,128)(2,1)S(1)}, u32[]{:S(2)}, u32[]{:S(2)}) collective-permute-start(bf16[72,512]{1,0:T(8,128)(2,1)S(1)} %get-tuple-element.92), channel_id=1, source_target_pairs={{0,64},{32,96},{64,0},{96,32},{1,65},{33,97},{65,1},{97,33},{2,66}... | collective-permute-start | bytes 221192 | tf_op jit(solution)/shard_map/ppermute | solution.py:28
  74.0 5.9 %collective-permute-start.20 = (bf16[72,512]{1,0:T(8,128)(2,1)S(1)}, bf16[72,512]{1,0:T(8,128)(2,1)S(1)}, u32[]{:S(2)}, u32[]{:S(2)}) collective-permute-start(bf16[72,512]{1,0:T(8,128)(2,1)S(1)} %get-tuple-element.92), channel_id=1, source_target_pairs={{0,32},{32,0},{64,96},{96,64},{1,33},{33,1},{65,97},{97,65},{2,34}... | collective-permute-start | bytes 221192 | tf_op jit(solution)/shard_map/ppermute | solution.py:28

commit v5 on v4

--- a/solution.py
+++ b/solution.py
@@ -452,23 +452,37 @@
 
     def apart(a):
         zero = jnp.zeros_like(a)
-        return jnp.concatenate([jnp.where(lane < GROUP, a, zero), jnp.where(lane < GROUP, zero, a)], 0)
+        first = lane[0 : a.shape[0]] < GROUP
+        return jnp.concatenate([jnp.where(first, a, zero), jnp.where(first, zero, a)], 0)
+
+    def spread(part, half):
+        rows = []
+        for at in range(0, SUB, half):
+            rows += [part[at : at + half]] * 2
+        return jnp.concatenate(rows, 0)
+
+    row = lax.broadcasted_iota(jnp.int32, (128, 128), 0)
+    col = lax.broadcasted_iota(jnp.int32, (128, 128), 1)
+    ones = jnp.where((row // GROUP) == (col // GROUP), 1.0, 0.0).astype(BF16)
 
     for n in range(count):
         c = first + n
         at = SUB * c - first_token
         there = slice(at, at + SUB)
         r = recept[there, :]
-        k, v = [pair[there, channels * i : channels * i + channels] for i in range(2)]
+        k, v_wide = [pair[there, channels * i : channels * i + channels] for i in range(2)]
         w = decay[there, :]
-        v = v.astype(BF16)
+        v = v_wide.astype(BF16)
         w = jnp.maximum(w, FLOOR)
-        sides = []
+        sides, rights = [], []
         exponents = dot(sums[0 : 7 * SUB, :], split_two(w))
         for level, half in enumerate(HALVES):
             right = (line // half) % 2 == 1
-            e = jnp.exp(exponents[SUB * level : SUB * level + SUB, :])
-            sides.append((jnp.where(right, r, k) * e).astype(BF16))
+            side = jnp.where(right, r, k) * jnp.exp(exponents[SUB * level : SUB * level + SUB, :])
+            sides.append(side.astype(BF16))
+            if half >= 8:
+                tops = [side[top : top + half] for top in range(half, SUB, 2 * half)]
+                rights.append(jnp.concatenate(tops, 0).astype(BF16))
         before_here = exponents[6 * SUB : 7 * SUB, :]
         late = (line + c * SUB) >= start
         begins_late = (c * SUB - 1) >= start if c else jnp.bool_(False)
@@ -476,19 +490,22 @@
         offset = offsets[c : c + 1, :]
         rows = slice(SUB * n, SUB * n + SUB)
         queries[rows, :] = jnp.where(late, 0.0, r * jnp.exp(offset + before_here)).astype(BF16)
-        own = (r * reward[...]).astype(BF16)
-        k_own = k.astype(BF16)
+        own = (r * reward[...] * k).astype(BF16)
         same = ((two_t + c * SUB) >= start) == ((two_s + c * SUB) >= start)
         for p in range(channels // 128):
             cols = slice(128 * p, 128 * p + 128)
-            scores = jnp.where(two_t == two_s, dot_nt(apart(own[:, cols]), k_own[:, cols]), 0.0)
+            scores = jnp.zeros((2 * SUB, SUB), F32)
             for level, half in enumerate(HALVES):
                 side = sides[level][:, cols]
-                part = dot_nt(apart(side), side)
+                if half >= 8:
+                    part = spread(dot_nt(apart(rights[level][:, cols]), side), half)
+                else:
+                    part = dot_nt(apart(side), side)
                 here = (two_t // (2 * half) == two_s // (2 * half)) & ((two_t // half) % 2 == 1) & ((two_s // half) % 2 == 0)
-                scores = jnp.where(here & same, part, scores)
-            both = dot(scores.astype(BF16), v[:, cols])
+                scores = jnp.where(here, part, scores)
+            both = dot(jnp.where(same, scores, 0.0).astype(BF16), v[:, cols])
             out = jnp.where(lane < GROUP, both[0:SUB], both[SUB : 2 * SUB])
+            out = out + dot(own[:, cols], ones) * v_wide[:, cols]
             local[rows, cols] = out + dot_nt(reach[:, cols], apart(entering[c, :, cols]))
 
 
@@ -698,7 +715,8 @@
     middle, end = LAST // SUB, x.shape[0] // SUB
     jobs = (
         (early_recept, early, decay, tuple(range(middle)), 0),
-        (late_recept, late, late_decay, tuple(range(middle, end)), LAST),
+        (late_recept, late, late_decay, tuple(range(middle, middle + 1)), LAST),
+        (late_recept, late, late_decay, tuple(range(middle + 1, end)), LAST),
     )
     outputs = []
     for job in jobs:

time: 83.9 us -> 84.4 us (level)
    pallas_call x2 -> x3, Pallas kernels: 9.74 us -> 10.2 us  [local_outputs(): pl.pallas_call(functools.partial(local_kernel, first=numbers[0], count=le...]
  transfers between devices with their start and end apart: 23 -> 23, of which waited for: 5 -> 6; matrix products, arithmetic and copies ran while one was open for 0% -> 0% of each run, Pallas kernels for 36% -> 36%
where the time goes in v5:
time: 84.4 us; the launch traced here: 83.4 us
  Pallas kernels  42.3 us (50%)
  starting transfers between devices  23.5 us (28%)
  waiting for transfers between devices  16.5 us (20%)
  between operations  1 us (1%)
    ppermute x20, starting transfers between devices, xor_permute(): return lax.ppermute(array, axes, [(i, i ^ flip) for i in range(length)])  17 us
    pallas_call x1, Pallas kernels, project_late(): pl.pallas_call(functools.partial(late_kernel, counts=counts), in_specs=[S...  10.4 us
    pallas_call x3, Pallas kernels, local_outputs(): pl.pallas_call(functools.partial(local_kernel, first=numbers[0], count=le...  10.2 us
    ppermute x1, waiting for transfers between devices, inner(): before = lax.ppermute(last, SEQ, [(i, i + 1) for i in range(shards - 1)])  9.43 us
    pallas_call x1, Pallas kernels, project_early(): pl.pallas_call(functools.partial(early_kernel, counts=counts), in_specs=[...  8.24 us
    ppermute x20, waiting for transfers between devices, xor_permute(): return lax.ppermute(array, axes, [(i, i ^ flip) for i in range(length)])  7.04 us
    ppermute x2, starting transfers between devices, across_far(): return lax.ppermute(a, ('y_hi', 'y_lo'), [(i, i ^ 3) for i in range(4)])  3.86 us
    pallas_call x1, Pallas kernels, load(): pl.pallas_call(functools.partial(load_kernel, kinds=kinds), in_specs=[SME...  2.79 us
  transfers between devices with their start and end apart: 23, of which 6 were waited for; matrix products, arithmetic and copies ran while one was open for 0% of the time, Pallas kernels for 36%

profile of v5, /device:TPU:8, one launch (start us, length us, event | category | flops | bytes accessed | tf_op | source)
XLA Modules:
  0.0 83.4 jit_solution(15606936448569524573)
XLA Ops:
  0.0 1.6 %collective-permute-start.10 = (bf16[1024,256]{1,0:T(8,128)(2,1)}, bf16[1024,256]{1,0:T(8,128)(2,1)S(1)}, u32[]{:S(2)}, u32[]{:S(2)}) collective-permute-start(bf16[1024,256]{1,0:T(8,128)(2,1)} %refs_2_.1), channel_id=1, source_target_pairs={{0,6},{2,4},{4,2},{6,0},{1,7},{3,5},{5,3},{7,1},{8,14},{10,12},{12... | collective-permute-start | bytes 1572872 | tf_op jit(solution)/shard_map/ppermute | solution.py:667
  2.3 1.8 %shard_map.146 = (bf16[144,1024]{1,0:T(8,128)(2,1)S(1)}, bf16[128,1024]{1,0:T(8,128)(2,1)S(1)}, bf16[272,1024]{1,0:T(8,128)(2,1)S(1)}, bf16[16,1024]{1,0:T(8,128)(2,1)S(1)}) custom-call(s32[5]{0:T(128)S(1)} %stack.19.where_ref, bf16[512,1024]{1,0:T(8,128)(2,1)} %x.1), custom_call_target="tpu_custom_call" | custom-call | flops 1000000 | bytes 2000000 | tf_op jit(solution)/shard_map/pallas_call | solution.py:87
  4.1 2.0 %collective-permute-start.5 = (bf16[144,1024]{1,0:T(8,128)(2,1)S(1)}, bf16[144,1024]{1,0:T(8,128)(2,1)S(1)}, u32[]{:S(2)}, u32[]{:S(2)}) collective-permute-start(bf16[144,1024]{1,0:T(8,128)(2,1)S(1)} %get-tuple-element.55.refs_0_), channel_id=1, source_target_pairs={{0,2},{1,3},{2,0},{3,1},{4,6},{5,7},{6,4},{7,5},{8,10},{9,11},{10,... | collective-permute-start | bytes 884744 | tf_op jit(solution)/shard_map/ppermute | solution.py:28
  6.2 2.7 %collective-permute-start = (bf16[16,1024]{1,0:T(8,128)(2,1)S(1)}, bf16[16,1024]{1,0:T(8,128)(2,1)S(1)}, u32[]{:S(2)}, u32[]{:S(2)}) collective-permute-start(bf16[16,1024]{1,0:T(8,128)(2,1)S(1)} %get-tuple-element.54), channel_id=1, source_target_pairs={{0,4},{4,8},{8,12},{12,16},{16,20},{20,24},{24,28},{28,32},{32,36}... | collective-permute-start | bytes 98312 | tf_op jit(solution)/shard_map/ppermute | solution.py:683
  9.0 9.4 %collective-permute-done = bf16[16,1024]{1,0:T(8,128)(2,1)S(1)} collective-permute-done((bf16[16,1024]{1,0:T(8,128)(2,1)S(1)}, bf16[16,1024]{1,0:T(8,128)(2,1)S(1)}, u32[]{:S(2)}, u32[]{:S(2)}) %collective-permute-start) | collective-permute-done | bytes 32800 | tf_op jit(solution)/shard_map/ppermute | solution.py:683
  19.5 2.8 %shard_map.145 = (bf16[4,4,64,1024]{3,2,1,0:T(8,128)(2,1)S(1)}, f32[5,4096]{1,0:T(8,128)S(1)}, bf16[1024,256]{1,0:T(8,128)(2,1)S(1)}, bf16[128,512]{1,0:T(8,128)...) custom-call(s32[5]{0:T(128)S(1)} %stack.19.where_ref, ...), custom_call_target="tpu_custom_call" | custom-call | flops 3000000000 | bytes 8000000 | tf_op jit(solution)/shard_map/pallas_call | solution.py:133
  22.4 2.3 %collective-permute-start.14 = (bf16[1024,128]{1,0:T(8,128)(2,1)S(1)}, bf16[1024,128]{1,0:T(8,128)(2,1)S(1)}, u32[]{:S(2)}, u32[]{:S(2)}) collective-permute-start(bf16[1024,128]{1,0:T(8,128)(2,1)S(1)} %copy-done), channel_id=1, source_target_pairs={{0,6},{2,4},{4,2},{6,0},{1,7},{3,5},{5,3},{7,1},{8,14},{10,12},{12... | collective-permute-start | bytes 786440 | tf_op jit(solution)/shard_map/ppermute | solution.py:667
  24.6 3.0 %collective-permute-start.2 = (bf16[272,1024]{1,0:T(8,128)(2,1)S(1)}, bf16[272,1024]{1,0:T(8,128)(2,1)S(1)}, u32[]{:S(2)}, u32[]{:S(2)}) collective-permute-start(bf16[272,1024]{1,0:T(8,128)(2,1)S(1)} %constant_dynamic-update-slice_fusion.refs_0_), channel_id=1, source_target_pairs={{0,2},{1,3},{2,0},{3,1},{4,6},{5,7},{6,4},{7,5},{8,10},{9,11},{10,... | collective-permute-start | bytes 1671176 | tf_op jit(solution)/shard_map/ppermute | solution.py:28
  27.6 10.4 %shard_map.147 = (f32[256,1024]{1,0:T(8,128)S(1)}, f32[256,512]{1,0:T(8,128)S(1)}, bf16[4,256,1024]{2,1,0:T(8,128)(2,1)S(1)}, bf16[4,1024,512]{2,1,0:T(8,128)(2,...) custom-call(s32[5]{0:T(128)S(1)} %stack.19.where_ref, ...), custom_call_target="tpu_custom_call" | custom-call | flops 6400000000 | bytes 17000000 | tf_op jit(solution)/shard_map/pallas_call | solution.py:344
  38.0 2.5 %collective-permute-done.2.refs_2_ = bf16[272,1024]{1,0:T(8,128)(2,1)S(1)} collective-permute-done((bf16[272,1024]{1,0:T(8,128)(2,1)S(1)}, bf16[272,1024]{1,0:T(8,128)(2,1)S(1)}, u32[]{:S(2)}, u32[]{:S(2)}) %collective-permute-start.2) | collective-permute-done | bytes 557088 | tf_op jit(solution)/shard_map/ppermute | solution.py:28
  41.1 1.8 %collective-permute-done.13.refs_1_.refs_9_ = bf16[1024,128]{1,0:T(8,128)(2,1)S(1)} collective-permute-done((bf16[1024,128]{1,0:T(8,128)(2,1)S(1)}, bf16[1024,128]{1,0:T(8,128)(2,1)S(1)}, u32[]{:S(2)}, u32[]{:S(2)}) %collective-permute-start.13) | collective-permute-done | bytes 262176 | tf_op jit(solution)/shard_map/ppermute | solution.py:28
  43.2 2.3 %shard_map.148 = (f32[256,512]{1,0:T(8,128)S(1)}, f32[4,64,512]{2,1,0:T(8,128)S(1)}, f32[8,512]{1,0:T(8,128)S(1)}, f32[72,512]{1,0:T(8,128)S(1)}) custom-call(s32[5]{0:T(128)S(1)} %stack.19.where_ref, bf16[4,256,1024]{2,1,0:T(8,128)(2,1)S(1)} %get-tuple-element.67.rows, bf16[1024,128]{1,0:T(8,128)(2,1)S(1)} %get-tuple-element.62.refs_0_.refs_8_, ...), custom_call_target="tpu_custom_call" | custom-call | flops 1000000000 | bytes 2000000 | tf_op jit(solution)/shard_map/pallas_call | solution.py:369
  45.6 8.2 %shard_map.149 = (f32[256,1024]{1,0:T(8,128)S(1)}, f32[256,512]{1,0:T(8,128)S(1)}, bf16[8,64,512]{2,1,0:T(8,128)(2,1)S(1)}, f32[8,512]{1,0:T(8,128)S(1)}, f32[72...) custom-call(s32[5]{0:T(128)S(1)} %stack.19.where_ref, ...), custom_call_target="tpu_custom_call" | custom-call | flops 6400000000 | bytes 17000000 | tf_op jit(solution)/shard_map/pallas_call | solution.py:388
  53.8 1.0 %collective-permute-start.16 = (bf16[72,512]{1,0:T(8,128)(2,1)S(1)}, bf16[72,512]{1,0:T(8,128)(2,1)S(1)}, u32[]{:S(2)}, u32[]{:S(2)}) collective-permute-start(bf16[72,512]{1,0:T(8,128)(2,1)S(1)} %get-tuple-element.90), channel_id=1, source_target_pairs={{0,4},{4,0},{1,5},{5,1},{2,6},{6,2},{3,7},{7,3},{8,12},{12,8},{9,1... | collective-permute-start | bytes 221192 | tf_op jit(solution)/shard_map/ppermute | solution.py:28
  54.8 1.8 %shard_map.152 = (f32[64,512]{1,0:T(8,128)S(1)}, bf16[64,512]{1,0:T(8,128)(2,1)S(1)}) custom-call(s32[5]{0:T(128)S(1)} %stack.19.where_ref, bf16[512,128]{1,0:T(8,128)(2,1)S(1)} %get-tuple-element.51.refs_6_.refs_18_.sums, f32[1,512]{1,0:T(1,128)S(1)} %get-tuple-element.52.reward, bf16[8,64,512]{2,1,0:T(8,128)(2,1)S(1)} %get-tuple-element.72.entering, ...), custom_call_target="tpu_custom_call" | custom-call | flops 2000000000 | bytes 3000000 | tf_op jit(solution)/shard_map/pallas_call | solution.py:515
  56.7 3.7 %shard_map.153 = (f32[192,512]{1,0:T(8,128)S(1)}, bf16[192,512]{1,0:T(8,128)(2,1)S(1)}) custom-call(s32[5]{0:T(128)S(1)} %stack.19.where_ref, bf16[512,128]{1,0:T(8,128)(2,1)S(1)} %get-tuple-element.51.refs_6_.refs_18_.sums, f32[1,512]{1,0:T(1,128)S(1)} %get-tuple-element.52.reward, bf16[8,64,512]{2,1,0:T(8,128)(2,1)S(1)} %get-tuple-element.72.entering, ...), custom_call_target="tpu_custom_call" | custom-call | flops 2000000000 | bytes 3000000 | tf_op jit(solution)/shard_map/pallas_call | solution.py:515
  61.0 2.8 %collective-permute-start.19 = (bf16[72,512]{1,0:T(8,128)(2,1)S(1)}, bf16[72,512]{1,0:T(8,128)(2,1)S(1)}, u32[]{:S(2)}, u32[]{:S(2)}) collective-permute-start(bf16[72,512]{1,0:T(8,128)(2,1)S(1)} %get-tuple-element.93), channel_id=1, source_target_pairs={{0,24},{8,16},{16,8},{24,0},{1,25},{9,17},{17,9},{25,1},{2,26},{10... | collective-permute-start | bytes 221192 | tf_op jit(solution)/shard_map/ppermute | solution.py:28
  63.8 0.8 collective-permute-start.18
  65.2 2.6 %shard_map.150.recept = f32[256,512]{1,0:T(8,128)S(1)} custom-call(s32[5]{0:T(128)S(1)} %stack.19.where_ref, bf16[272,1024]{1,0:T(8,128)(2,1)S(1)} %constant_dynamic-update-slice_fusion.refs_0_, bf16[272,1024]{1,0:T(8,128)(2,1)S(1)} %collective-permute-done.1.refs_1_, bf16[272,1024]{1,0:T(8,128)(2,1)S(1)} %collective-permute-done.2.refs_2_, ...), custom_call_target="tpu_custom_call" | custom-call | flops 2000000000 | bytes 5000000 | tf_op jit(solution)/shard_map/pallas_call | solution.py:328
  67.8 2.1 %collective-permute-done.18.refs_3_ = bf16[72,512]{1,0:T(8,128)(2,1)S(1)} collective-permute-done((bf16[72,512]{1,0:T(8,128)(2,1)S(1)}, bf16[72,512]{1,0:T(8,128)(2,1)S(1)}, u32[]{:S(2)}, u32[]{:S(2)}) %collective-permute-start.18) | collective-permute-done | bytes 73760 | tf_op jit(solution)/shard_map/ppermute | solution.py:28
  70.6 4.1 %collective-permute-start.22 = (bf16[72,512]{1,0:T(8,128)(2,1)S(1)}, bf16[72,512]{1,0:T(8,128)(2,1)S(1)}, u32[]{:S(2)}, u32[]{:S(2)}) collective-permute-start(bf16[72,512]{1,0:T(8,128)(2,1)S(1)} %get-tuple-element.96), channel_id=1, source_target_pairs={{0,96},{32,64},{64,32},{96,0},{1,97},{33,65},{65,33},{97,1},{2,98}... | collective-permute-start | bytes 221192 | tf_op jit(solution)/shard_map/ppermute | solution.py:28
  74.7 0.9 %collective-permute-start.20 = (bf16[72,512]{1,0:T(8,128)(2,1)S(1)}, bf16[72,512]{1,0:T(8,128)(2,1)S(1)}, u32[]{:S(2)}, u32[]{:S(2)}) collective-permute-start(bf16[72,512]{1,0:T(8,128)(2,1)S(1)} %get-tuple-element.96), channel_id=1, source_target_pairs={{0,32},{32,0},{64,96},{96,64},{1,33},{33,1},{65,97},{97,65},{2,34}... | collective-permute-start | bytes 221192 | tf_op jit(solution)/shard_map/ppermute | solution.py:28
  75.6 4.7 %shard_map.151 = (f32[256,512]{1,0:T(8,128)S(1)}, bf16[256,512]{1,0:T(8,128)(2,1)S(1)}) custom-call(s32[5]{0:T(128)S(1)} %stack.19.where_ref, bf16[512,128]{1,0:T(8,128)(2,1)S(1)} %get-tuple-element.51.refs_6_.refs_18_.sums, f32[1,512]{1,0:T(1,128)S(1)} %get-tuple-element.52.reward, bf16[8,64,512]{2,1,0:T(8,128)(2,1)S(1)} %get-tuple-element.72.entering, ...), custom_call_target="tpu_custom_call" | custom-call | flops 2000000000 | bytes 3000000 | tf_op jit(solution)/shard_map/pallas_call | solution.py:515
  80.6 2.7 %shard_map.156 = bf16[512,512]{1,0:T(8,128)(2,1)} custom-call(s32[5]{0:T(128)S(1)} %stack.19.where_ref, f32[256,512]{1,0:T(8,128)S(1)} %get-tuple-element.79.refs_0_, f32[64,512]{1,0:T(8,128)S(1)} %get-tuple-element.82.refs_1_, f32[192,512]{1,0:T(8,128)S(1)} %get-tuple-element.83.refs_2_, bf16[256,512]{1,0:T(8,128)(2,1)S(1)} %get-tuple-element.84.refs_3_, ...), custom_call_target="tpu_custom_call" | custom-call | flops 1000000000 | bytes 2000000 | tf_op jit(solution)/shard_map/pallas_call | solution.py:634
  (38 shorter events, 4.3 us)
Async XLA Ops:
  0.0 18.4 %collective-permute-start.10 = (bf16[1024,256]{1,0:T(8,128)(2,1)}, bf16[1024,256]{1,0:T(8,128)(2,1)S(1)}, u32[]{:S(2)}, u32[]{:S(2)}) collective-permute-start(bf16[1024,256]{1,0:T(8,128)(2,1)} %refs_2_.1), channel_id=1, source_target_pairs={{0,6},{2,4},{4,2},{6,0},{1,7},{3,5},{5,3},{7,1},{8,14},{10,12},{12... | collective-permute-start | bytes 1572872 | tf_op jit(solution)/shard_map/ppermute | solution.py:667
  4.1 15.3 %collective-permute-start.5 = (bf16[144,1024]{1,0:T(8,128)(2,1)S(1)}, bf16[144,1024]{1,0:T(8,128)(2,1)S(1)}, u32[]{:S(2)}, u32[]{:S(2)}) collective-permute-start(bf16[144,1024]{1,0:T(8,128)(2,1)S(1)} %get-tuple-element.55.refs_0_), channel_id=1, source_target_pairs={{0,2},{1,3},{2,0},{3,1},{4,6},{5,7},{6,4},{7,5},{8,10},{9,11},{10,... | collective-permute-start | bytes 884744 | tf_op jit(solution)/shard_map/ppermute | solution.py:28
  6.1 12.8 %collective-permute-start.6 = (bf16[128,1024]{1,0:T(8,128)(2,1)S(1)}, bf16[128,1024]{1,0:T(8,128)(2,1)S(1)}, u32[]{:S(2)}, u32[]{:S(2)}) collective-permute-start(bf16[128,1024]{1,0:T(8,128)(2,1)S(1)} %get-tuple-element.56.refs_1_), channel_id=1, source_target_pairs={{0,2},{1,3},{2,0},{3,1},{4,6},{5,7},{6,4},{7,5},{8,10},{9,11},{10,... | collective-permute-start | bytes 786440 | tf_op jit(solution)/shard_map/ppermute | solution.py:28
  6.2 12.8 %collective-permute-start.4 = (bf16[128,1024]{1,0:T(8,128)(2,1)S(1)}, bf16[128,1024]{1,0:T(8,128)(2,1)S(1)}, u32[]{:S(2)}, u32[]{:S(2)}) collective-permute-start(bf16[128,1024]{1,0:T(8,128)(2,1)S(1)} %get-tuple-element.56.refs_1_), channel_id=1, source_target_pairs={{0,1},{1,0},{2,3},{3,2},{4,5},{5,4},{6,7},{7,6},{8,9},{9,8},{10,11... | collective-permute-start | bytes 786440 | tf_op jit(solution)/shard_map/ppermute | solution.py:28
  6.2 12.2 %collective-permute-start = (bf16[16,1024]{1,0:T(8,128)(2,1)S(1)}, bf16[16,1024]{1,0:T(8,128)(2,1)S(1)}, u32[]{:S(2)}, u32[]{:S(2)}) collective-permute-start(bf16[16,1024]{1,0:T(8,128)(2,1)S(1)} %get-tuple-element.54), channel_id=1, source_target_pairs={{0,4},{4,8},{8,12},{12,16},{16,20},{20,24},{24,28},{28,32},{32,36}... | collective-permute-start | bytes 98312 | tf_op jit(solution)/shard_map/ppermute | solution.py:683
  18.4 6.2 %collective-permute-start.9 = (bf16[1024,256]{1,0:T(8,128)(2,1)}, bf16[1024,256]{1,0:T(8,128)(2,1)S(1)}, u32[]{:S(2)}, u32[]{:S(2)}) collective-permute-start(bf16[1024,256]{1,0:T(8,128)(2,1)} %refs_2_.1), channel_id=1, source_target_pairs={{0,1},{1,0},{2,3},{3,2},{4,5},{5,4},{6,7},{7,6},{8,9},{9,8},{10,11... | collective-permute-start | bytes 1572872 | tf_op jit(solution)/shard_map/ppermute | solution.py:28
  18.4 9.2 %collective-permute-start.11 = (bf16[1024,256]{1,0:T(8,128)(2,1)S(1)}, bf16[1024,256]{1,0:T(8,128)(2,1)S(1)}, u32[]{:S(2)}, u32[]{:S(2)}) collective-permute-start(bf16[1024,256]{1,0:T(8,128)(2,1)S(1)} %collective-permute-done.10.refs_10_.refs_6_), channel_id=1, source_target_pairs={{0,1},{1,0},{2,3},{3,2},{4,5},{5,4},{6,7},{7,6},{8,9},{9,8},{10,11... | collective-permute-start | bytes 1572872 | tf_op jit(solution)/shard_map/ppermute | solution.py:28
  18.9 3.4 %collective-permute-start.3 = (bf16[144,1024]{1,0:T(8,128)(2,1)S(1)}, bf16[144,1024]{1,0:T(8,128)(2,1)S(1)}, u32[]{:S(2)}, u32[]{:S(2)}) collective-permute-start(bf16[144,1024]{1,0:T(8,128)(2,1)S(1)} %get-tuple-element.55.refs_0_), channel_id=1, source_target_pairs={{0,1},{1,0},{2,3},{3,2},{4,5},{5,4},{6,7},{7,6},{8,9},{9,8},{10,11... | collective-permute-start | bytes 884744 | tf_op jit(solution)/shard_map/ppermute | solution.py:28
  19.0 8.6 %collective-permute-start.8 = (bf16[128,1024]{1,0:T(8,128)(2,1)S(1)}, bf16[128,1024]{1,0:T(8,128)(2,1)S(1)}, u32[]{:S(2)}, u32[]{:S(2)}) collective-permute-start(bf16[128,1024]{1,0:T(8,128)(2,1)S(1)} %collective-permute-done.6.refs_5_), channel_id=1, source_target_pairs={{0,1},{1,0},{2,3},{3,2},{4,5},{5,4},{6,7},{7,6},{8,9},{9,8},{10,11... | collective-permute-start | bytes 786440 | tf_op jit(solution)/shard_map/ppermute | solution.py:28
  19.4 8.2 %collective-permute-start.7 = (bf16[144,1024]{1,0:T(8,128)(2,1)S(1)}, bf16[144,1024]{1,0:T(8,128)(2,1)S(1)}, u32[]{:S(2)}, u32[]{:S(2)}) collective-permute-start(bf16[144,1024]{1,0:T(8,128)(2,1)S(1)} %collective-permute-done.5.refs_4_), channel_id=1, source_target_pairs={{0,1},{1,0},{2,3},{3,2},{4,5},{5,4},{6,7},{7,6},{8,9},{9,8},{10,11... | collective-permute-start | bytes 884744 | tf_op jit(solution)/shard_map/ppermute | solution.py:28
  19.5 2.8 %copy-start = (bf16[1024,128]{1,0:T(8,128)(2,1)S(1)}, bf16[1024,128]{1,0:T(8,128)(2,1)}, u32[]{:S(2)}) copy-start(bf16[1024,128]{1,0:T(8,128)(2,1)} %refs_9_.1) | copy-start | bytes 786436
  22.4 18.7 %collective-permute-start.14 = (bf16[1024,128]{1,0:T(8,128)(2,1)S(1)}, bf16[1024,128]{1,0:T(8,128)(2,1)S(1)}, u32[]{:S(2)}, u32[]{:S(2)}) collective-permute-start(bf16[1024,128]{1,0:T(8,128)(2,1)S(1)} %copy-done), channel_id=1, source_target_pairs={{0,6},{2,4},{4,2},{6,0},{1,7},{3,5},{5,3},{7,1},{8,14},{10,12},{12... | collective-permute-start | bytes 786440 | tf_op jit(solution)/shard_map/ppermute | solution.py:667
  24.6 15.9 %collective-permute-start.2 = (bf16[272,1024]{1,0:T(8,128)(2,1)S(1)}, bf16[272,1024]{1,0:T(8,128)(2,1)S(1)}, u32[]{:S(2)}, u32[]{:S(2)}) collective-permute-start(bf16[272,1024]{1,0:T(8,128)(2,1)S(1)} %constant_dynamic-update-slice_fusion.refs_0_), channel_id=1, source_target_pairs={{0,2},{1,3},{2,0},{3,1},{4,6},{5,7},{6,4},{7,5},{8,10},{9,11},{10,... | collective-permute-start | bytes 1671176 | tf_op jit(solution)/shard_map/ppermute | solution.py:28
  27.6 17.9 %collective-permute-start.1 = (bf16[272,1024]{1,0:T(8,128)(2,1)S(1)}, bf16[272,1024]{1,0:T(8,128)(2,1)S(1)}, u32[]{:S(2)}, u32[]{:S(2)}) collective-permute-start(bf16[272,1024]{1,0:T(8,128)(2,1)S(1)} %constant_dynamic-update-slice_fusion.refs_0_), channel_id=1, source_target_pairs={{0,1},{1,0},{2,3},{3,2},{4,5},{5,4},{6,7},{7,6},{8,9},{9,8},{10,11... | collective-permute-start | bytes 1671176 | tf_op jit(solution)/shard_map/ppermute | solution.py:28
  40.5 5.0 %collective-permute-start.12 = (bf16[272,1024]{1,0:T(8,128)(2,1)S(1)}, bf16[272,1024]{1,0:T(8,128)(2,1)S(1)}, u32[]{:S(2)}, u32[]{:S(2)}) collective-permute-start(bf16[272,1024]{1,0:T(8,128)(2,1)S(1)} %collective-permute-done.2.refs_2_), channel_id=1, source_target_pairs={{0,1},{1,0},{2,3},{3,2},{4,5},{5,4},{6,7},{7,6},{8,9},{9,8},{10,11... | collective-permute-start | bytes 1671176 | tf_op jit(solution)/shard_map/ppermute | solution.py:28
  40.5 2.3 %collective-permute-start.13 = (bf16[1024,128]{1,0:T(8,128)(2,1)S(1)}, bf16[1024,128]{1,0:T(8,128)(2,1)S(1)}, u32[]{:S(2)}, u32[]{:S(2)}) collective-permute-start(bf16[1024,128]{1,0:T(8,128)(2,1)S(1)} %copy-done), channel_id=1, source_target_pairs={{0,1},{1,0},{2,3},{3,2},{4,5},{5,4},{6,7},{7,6},{8,9},{9,8},{10,11... | collective-permute-start | bytes 786440 | tf_op jit(solution)/shard_map/ppermute | solution.py:28
  41.0 2.2 %collective-permute-start.15 = (bf16[1024,128]{1,0:T(8,128)(2,1)S(1)}, bf16[1024,128]{1,0:T(8,128)(2,1)S(1)}, u32[]{:S(2)}, u32[]{:S(2)}) collective-permute-start(bf16[1024,128]{1,0:T(8,128)(2,1)S(1)} %collective-permute-done.14.refs_2_.refs_10_), channel_id=1, source_target_pairs={{0,1},{1,0},{2,3},{3,2},{4,5},{5,4},{6,7},{7,6},{8,9},{9,8},{10,11... | collective-permute-start | bytes 786440 | tf_op jit(solution)/shard_map/ppermute | solution.py:28
  53.8 6.6 %collective-permute-start.16 = (bf16[72,512]{1,0:T(8,128)(2,1)S(1)}, bf16[72,512]{1,0:T(8,128)(2,1)S(1)}, u32[]{:S(2)}, u32[]{:S(2)}) collective-permute-start(bf16[72,512]{1,0:T(8,128)(2,1)S(1)} %get-tuple-element.90), channel_id=1, source_target_pairs={{0,4},{4,0},{1,5},{5,1},{2,6},{6,2},{3,7},{7,3},{8,12},{12,8},{9,1... | collective-permute-start | bytes 221192 | tf_op jit(solution)/shard_map/ppermute | solution.py:28
  61.0 6.8 %collective-permute-start.19 = (bf16[72,512]{1,0:T(8,128)(2,1)S(1)}, bf16[72,512]{1,0:T(8,128)(2,1)S(1)}, u32[]{:S(2)}, u32[]{:S(2)}) collective-permute-start(bf16[72,512]{1,0:T(8,128)(2,1)S(1)} %get-tuple-element.93), channel_id=1, source_target_pairs={{0,24},{8,16},{16,8},{24,0},{1,25},{9,17},{17,9},{25,1},{2,26},{10... | collective-permute-start | bytes 221192 | tf_op jit(solution)/shard_map/ppermute | solution.py:28
  63.8 6.0 %collective-permute-start.18 = (bf16[72,512]{1,0:T(8,128)(2,1)S(1)}, bf16[72,512]{1,0:T(8,128)(2,1)S(1)}, u32[]{:S(2)}, u32[]{:S(2)}) collective-permute-start(bf16[72,512]{1,0:T(8,128)(2,1)S(1)} %get-tuple-element.93), channel_id=1, source_target_pairs={{0,16},{8,24},{16,0},{24,8},{1,17},{9,25},{17,1},{25,9},{2,18},{10... | collective-permute-start | bytes 221192 | tf_op jit(solution)/shard_map/ppermute | solution.py:28
  64.6 5.2 %collective-permute-start.17 = (bf16[72,512]{1,0:T(8,128)(2,1)S(1)}, bf16[72,512]{1,0:T(8,128)(2,1)S(1)}, u32[]{:S(2)}, u32[]{:S(2)}) collective-permute-start(bf16[72,512]{1,0:T(8,128)(2,1)S(1)} %get-tuple-element.93), channel_id=1, source_target_pairs={{0,8},{8,0},{16,24},{24,16},{1,9},{9,1},{17,25},{25,17},{2,10},{10... | collective-permute-start | bytes 221192 | tf_op jit(solution)/shard_map/ppermute | solution.py:28
  70.6 9.8 %collective-permute-start.22 = (bf16[72,512]{1,0:T(8,128)(2,1)S(1)}, bf16[72,512]{1,0:T(8,128)(2,1)S(1)}, u32[]{:S(2)}, u32[]{:S(2)}) collective-permute-start(bf16[72,512]{1,0:T(8,128)(2,1)S(1)} %get-tuple-element.96), channel_id=1, source_target_pairs={{0,96},{32,64},{64,32},{96,0},{1,97},{33,65},{65,33},{97,1},{2,98}... | collective-permute-start | bytes 221192 | tf_op jit(solution)/shard_map/ppermute | solution.py:28
  74.7 5.9 %collective-permute-start.21 = (bf16[72,512]{1,0:T(8,128)(2,1)S(1)}, bf16[72,512]{1,0:T(8,128)(2,1)S(1)}, u32[]{:S(2)}, u32[]{:S(2)}) collective-permute-start(bf16[72,512]{1,0:T(8,128)(2,1)S(1)} %get-tuple-element.96), channel_id=1, source_target_pairs={{0,64},{32,96},{64,0},{96,32},{1,65},{33,97},{65,1},{97,33},{2,66}... | collective-permute-start | bytes 221192 | tf_op jit(solution)/shard_map/ppermute | solution.py:28
  74.7 5.9 %collective-permute-start.20 = (bf16[72,512]{1,0:T(8,128)(2,1)S(1)}, bf16[72,512]{1,0:T(8,128)(2,1)S(1)}, u32[]{:S(2)}, u32[]{:S(2)}) collective-permute-start(bf16[72,512]{1,0:T(8,128)(2,1)S(1)} %get-tuple-element.96), channel_id=1, source_target_pairs={{0,32},{32,0},{64,96},{96,64},{1,33},{33,1},{65,97},{97,65},{2,34}... | collective-permute-start | bytes 221192 | tf_op jit(solution)/shard_map/ppermute | solution.py:28

commit v6 on v5

--- a/solution.py
+++ b/solution.py
@@ -611,10 +611,9 @@
         st = incoming[:, wide * p : wide * p + wide]
         blocks.append(jnp.concatenate([jnp.where(lane == h, st, jnp.zeros_like(st)) for h in range(wide // GROUP)], 0))
     copies = []
-    at = 0
-    for i in range(parts):
-        rows = slice(at, at + locals_[i].shape[0])
-        at = rows.stop
+    sizes = [a.shape[0] for a in locals_]
+    for i in sorted(range(parts), key=lambda i: -sizes[i]):
+        rows = slice(sum(sizes[:i]), sum(sizes[: i + 1]))
         for p in range(channels // wide):
             cols = slice(wide * p, wide * p + wide)
             o = locals_[i][:, cols] + dot_nt(queries[i][:, cols], blocks[p])

time: 84.4 us -> 84.3 us (level)
  no operation moved by 1% of the time
where the time goes in v6:
time: 84.3 us; the launch traced here: 83.4 us
  Pallas kernels  42.3 us (50%)
  starting transfers between devices  23.5 us (28%)
  waiting for transfers between devices  16.5 us (20%)
  between operations  1 us (1%)
    ppermute x20, starting transfers between devices, xor_permute(): return lax.ppermute(array, axes, [(i, i ^ flip) for i in range(length)])  17 us
    pallas_call x1, Pallas kernels, project_late(): pl.pallas_call(functools.partial(late_kernel, counts=counts), in_specs=[S...  10.4 us
    pallas_call x3, Pallas kernels, local_outputs(): pl.pallas_call(functools.partial(local_kernel, first=numbers[0], count=le...  10.2 us
    ppermute x1, waiting for transfers between devices, inner(): before = lax.ppermute(last, SEQ, [(i, i + 1) for i in range(shards - 1)])  9.43 us
    pallas_call x1, Pallas kernels, project_early(): pl.pallas_call(functools.partial(early_kernel, counts=counts), in_specs=[...  8.24 us
    ppermute x20, waiting for transfers between devices, xor_permute(): return lax.ppermute(array, axes, [(i, i ^ flip) for i in range(length)])  7.04 us
    ppermute x2, starting transfers between devices, across_far(): return lax.ppermute(a, ('y_hi', 'y_lo'), [(i, i ^ 3) for i in range(4)])  3.86 us
    pallas_call x1, Pallas kernels, load(): pl.pallas_call(functools.partial(load_kernel, kinds=kinds), in_specs=[SME...  2.79 us
  transfers between devices with their start and end apart: 23, of which 6 were waited for; matrix products, arithmetic and copies ran while one was open for 0% of the time, Pallas kernels for 36%

profile of v6, /device:TPU:8, one launch (start us, length us, event | category | flops | bytes accessed | tf_op | source)
XLA Modules:
  0.0 83.4 jit_solution(1696392271015418410)
XLA Ops:
  0.0 1.6 %collective-permute-start.10 = (bf16[1024,256]{1,0:T(8,128)(2,1)}, bf16[1024,256]{1,0:T(8,128)(2,1)S(1)}, u32[]{:S(2)}, u32[]{:S(2)}) collective-permute-start(bf16[1024,256]{1,0:T(8,128)(2,1)} %refs_2_.1), channel_id=1, source_target_pairs={{0,6},{2,4},{4,2},{6,0},{1,7},{3,5},{5,3},{7,1},{8,14},{10,12},{12... | collective-permute-start | bytes 1572872 | tf_op jit(solution)/shard_map/ppermute | solution.py:666
  2.3 1.8 %shard_map.146 = (bf16[144,1024]{1,0:T(8,128)(2,1)S(1)}, bf16[128,1024]{1,0:T(8,128)(2,1)S(1)}, bf16[272,1024]{1,0:T(8,128)(2,1)S(1)}, bf16[16,1024]{1,0:T(8,128)(2,1)S(1)}) custom-call(s32[5]{0:T(128)S(1)} %stack.19.where_ref, bf16[512,1024]{1,0:T(8,128)(2,1)} %x.1), custom_call_target="tpu_custom_call" | custom-call | flops 1000000 | bytes 2000000 | tf_op jit(solution)/shard_map/pallas_call | solution.py:87
  4.1 2.0 %collective-permute-start.5 = (bf16[144,1024]{1,0:T(8,128)(2,1)S(1)}, bf16[144,1024]{1,0:T(8,128)(2,1)S(1)}, u32[]{:S(2)}, u32[]{:S(2)}) collective-permute-start(bf16[144,1024]{1,0:T(8,128)(2,1)S(1)} %get-tuple-element.55.refs_0_), channel_id=1, source_target_pairs={{0,2},{1,3},{2,0},{3,1},{4,6},{5,7},{6,4},{7,5},{8,10},{9,11},{10,... | collective-permute-start | bytes 884744 | tf_op jit(solution)/shard_map/ppermute | solution.py:28
  6.2 2.7 %collective-permute-start = (bf16[16,1024]{1,0:T(8,128)(2,1)S(1)}, bf16[16,1024]{1,0:T(8,128)(2,1)S(1)}, u32[]{:S(2)}, u32[]{:S(2)}) collective-permute-start(bf16[16,1024]{1,0:T(8,128)(2,1)S(1)} %get-tuple-element.54), channel_id=1, source_target_pairs={{0,4},{4,8},{8,12},{12,16},{16,20},{20,24},{24,28},{28,32},{32,36}... | collective-permute-start | bytes 98312 | tf_op jit(solution)/shard_map/ppermute | solution.py:682
  9.0 9.4 %collective-permute-done = bf16[16,1024]{1,0:T(8,128)(2,1)S(1)} collective-permute-done((bf16[16,1024]{1,0:T(8,128)(2,1)S(1)}, bf16[16,1024]{1,0:T(8,128)(2,1)S(1)}, u32[]{:S(2)}, u32[]{:S(2)}) %collective-permute-start) | collective-permute-done | bytes 32800 | tf_op jit(solution)/shard_map/ppermute | solution.py:682
  19.5 2.8 %shard_map.145 = (bf16[4,4,64,1024]{3,2,1,0:T(8,128)(2,1)S(1)}, f32[5,4096]{1,0:T(8,128)S(1)}, bf16[1024,256]{1,0:T(8,128)(2,1)S(1)}, bf16[128,512]{1,0:T(8,128)...) custom-call(s32[5]{0:T(128)S(1)} %stack.19.where_ref, ...), custom_call_target="tpu_custom_call" | custom-call | flops 3000000000 | bytes 8000000 | tf_op jit(solution)/shard_map/pallas_call | solution.py:133
  22.4 2.3 %collective-permute-start.14 = (bf16[1024,128]{1,0:T(8,128)(2,1)S(1)}, bf16[1024,128]{1,0:T(8,128)(2,1)S(1)}, u32[]{:S(2)}, u32[]{:S(2)}) collective-permute-start(bf16[1024,128]{1,0:T(8,128)(2,1)S(1)} %copy-done), channel_id=1, source_target_pairs={{0,6},{2,4},{4,2},{6,0},{1,7},{3,5},{5,3},{7,1},{8,14},{10,12},{12... | collective-permute-start | bytes 786440 | tf_op jit(solution)/shard_map/ppermute | solution.py:666
  24.6 3.0 %collective-permute-start.2 = (bf16[272,1024]{1,0:T(8,128)(2,1)S(1)}, bf16[272,1024]{1,0:T(8,128)(2,1)S(1)}, u32[]{:S(2)}, u32[]{:S(2)}) collective-permute-start(bf16[272,1024]{1,0:T(8,128)(2,1)S(1)} %constant_dynamic-update-slice_fusion.refs_0_), channel_id=1, source_target_pairs={{0,2},{1,3},{2,0},{3,1},{4,6},{5,7},{6,4},{7,5},{8,10},{9,11},{10,... | collective-permute-start | bytes 1671176 | tf_op jit(solution)/shard_map/ppermute | solution.py:28
  27.6 10.4 %shard_map.147 = (f32[256,1024]{1,0:T(8,128)S(1)}, f32[256,512]{1,0:T(8,128)S(1)}, bf16[4,256,1024]{2,1,0:T(8,128)(2,1)S(1)}, bf16[4,1024,512]{2,1,0:T(8,128)(2,...) custom-call(s32[5]{0:T(128)S(1)} %stack.19.where_ref, ...), custom_call_target="tpu_custom_call" | custom-call | flops 6400000000 | bytes 17000000 | tf_op jit(solution)/shard_map/pallas_call | solution.py:344
  38.0 2.5 %collective-permute-done.2.refs_2_ = bf16[272,1024]{1,0:T(8,128)(2,1)S(1)} collective-permute-done((bf16[272,1024]{1,0:T(8,128)(2,1)S(1)}, bf16[272,1024]{1,0:T(8,128)(2,1)S(1)}, u32[]{:S(2)}, u32[]{:S(2)}) %collective-permute-start.2) | collective-permute-done | bytes 557088 | tf_op jit(solution)/shard_map/ppermute | solution.py:28
  41.1 1.8 %collective-permute-done.13.refs_1_.refs_9_ = bf16[1024,128]{1,0:T(8,128)(2,1)S(1)} collective-permute-done((bf16[1024,128]{1,0:T(8,128)(2,1)S(1)}, bf16[1024,128]{1,0:T(8,128)(2,1)S(1)}, u32[]{:S(2)}, u32[]{:S(2)}) %collective-permute-start.13) | collective-permute-done | bytes 262176 | tf_op jit(solution)/shard_map/ppermute | solution.py:28
  43.2 2.3 %shard_map.148 = (f32[256,512]{1,0:T(8,128)S(1)}, f32[4,64,512]{2,1,0:T(8,128)S(1)}, f32[8,512]{1,0:T(8,128)S(1)}, f32[72,512]{1,0:T(8,128)S(1)}) custom-call(s32[5]{0:T(128)S(1)} %stack.19.where_ref, bf16[4,256,1024]{2,1,0:T(8,128)(2,1)S(1)} %get-tuple-element.67.rows, bf16[1024,128]{1,0:T(8,128)(2,1)S(1)} %get-tuple-element.62.refs_0_.refs_8_, ...), custom_call_target="tpu_custom_call" | custom-call | flops 1000000000 | bytes 2000000 | tf_op jit(solution)/shard_map/pallas_call | solution.py:369
  45.6 8.2 %shard_map.149 = (f32[256,1024]{1,0:T(8,128)S(1)}, f32[256,512]{1,0:T(8,128)S(1)}, bf16[8,64,512]{2,1,0:T(8,128)(2,1)S(1)}, f32[8,512]{1,0:T(8,128)S(1)}, f32[72...) custom-call(s32[5]{0:T(128)S(1)} %stack.19.where_ref, ...), custom_call_target="tpu_custom_call" | custom-call | flops 6400000000 | bytes 17000000 | tf_op jit(solution)/shard_map/pallas_call | solution.py:388
  53.8 1.0 %collective-permute-start.16 = (bf16[72,512]{1,0:T(8,128)(2,1)S(1)}, bf16[72,512]{1,0:T(8,128)(2,1)S(1)}, u32[]{:S(2)}, u32[]{:S(2)}) collective-permute-start(bf16[72,512]{1,0:T(8,128)(2,1)S(1)} %get-tuple-element.90), channel_id=1, source_target_pairs={{0,4},{4,0},{1,5},{5,1},{2,6},{6,2},{3,7},{7,3},{8,12},{12,8},{9,1... | collective-permute-start | bytes 221192 | tf_op jit(solution)/shard_map/ppermute | solution.py:28
  54.8 1.8 %shard_map.152 = (f32[64,512]{1,0:T(8,128)S(1)}, bf16[64,512]{1,0:T(8,128)(2,1)S(1)}) custom-call(s32[5]{0:T(128)S(1)} %stack.19.where_ref, bf16[512,128]{1,0:T(8,128)(2,1)S(1)} %get-tuple-element.51.refs_6_.refs_18_.sums, f32[1,512]{1,0:T(1,128)S(1)} %get-tuple-element.52.reward, bf16[8,64,512]{2,1,0:T(8,128)(2,1)S(1)} %get-tuple-element.72.entering, ...), custom_call_target="tpu_custom_call" | custom-call | flops 2000000000 | bytes 3000000 | tf_op jit(solution)/shard_map/pallas_call | solution.py:515
  56.7 3.7 %shard_map.153 = (f32[192,512]{1,0:T(8,128)S(1)}, bf16[192,512]{1,0:T(8,128)(2,1)S(1)}) custom-call(s32[5]{0:T(128)S(1)} %stack.19.where_ref, bf16[512,128]{1,0:T(8,128)(2,1)S(1)} %get-tuple-element.51.refs_6_.refs_18_.sums, f32[1,512]{1,0:T(1,128)S(1)} %get-tuple-element.52.reward, bf16[8,64,512]{2,1,0:T(8,128)(2,1)S(1)} %get-tuple-element.72.entering, ...), custom_call_target="tpu_custom_call" | custom-call | flops 2000000000 | bytes 3000000 | tf_op jit(solution)/shard_map/pallas_call | solution.py:515
  61.0 2.8 %collective-permute-start.19 = (bf16[72,512]{1,0:T(8,128)(2,1)S(1)}, bf16[72,512]{1,0:T(8,128)(2,1)S(1)}, u32[]{:S(2)}, u32[]{:S(2)}) collective-permute-start(bf16[72,512]{1,0:T(8,128)(2,1)S(1)} %get-tuple-element.93), channel_id=1, source_target_pairs={{0,24},{8,16},{16,8},{24,0},{1,25},{9,17},{17,9},{25,1},{2,26},{10... | collective-permute-start | bytes 221192 | tf_op jit(solution)/shard_map/ppermute | solution.py:28
  63.8 0.8 collective-permute-start.18
  65.2 2.6 %shard_map.150.recept = f32[256,512]{1,0:T(8,128)S(1)} custom-call(s32[5]{0:T(128)S(1)} %stack.19.where_ref, bf16[272,1024]{1,0:T(8,128)(2,1)S(1)} %constant_dynamic-update-slice_fusion.refs_0_, bf16[272,1024]{1,0:T(8,128)(2,1)S(1)} %collective-permute-done.1.refs_1_, bf16[272,1024]{1,0:T(8,128)(2,1)S(1)} %collective-permute-done.2.refs_2_, ...), custom_call_target="tpu_custom_call" | custom-call | flops 2000000000 | bytes 5000000 | tf_op jit(solution)/shard_map/pallas_call | solution.py:328
  67.8 2.1 %collective-permute-done.18.refs_3_ = bf16[72,512]{1,0:T(8,128)(2,1)S(1)} collective-permute-done((bf16[72,512]{1,0:T(8,128)(2,1)S(1)}, bf16[72,512]{1,0:T(8,128)(2,1)S(1)}, u32[]{:S(2)}, u32[]{:S(2)}) %collective-permute-start.18) | collective-permute-done | bytes 73760 | tf_op jit(solution)/shard_map/ppermute | solution.py:28
  70.6 4.1 %collective-permute-start.22 = (bf16[72,512]{1,0:T(8,128)(2,1)S(1)}, bf16[72,512]{1,0:T(8,128)(2,1)S(1)}, u32[]{:S(2)}, u32[]{:S(2)}) collective-permute-start(bf16[72,512]{1,0:T(8,128)(2,1)S(1)} %get-tuple-element.96), channel_id=1, source_target_pairs={{0,96},{32,64},{64,32},{96,0},{1,97},{33,65},{65,33},{97,1},{2,98}... | collective-permute-start | bytes 221192 | tf_op jit(solution)/shard_map/ppermute | solution.py:28
  74.7 0.9 %collective-permute-start.20 = (bf16[72,512]{1,0:T(8,128)(2,1)S(1)}, bf16[72,512]{1,0:T(8,128)(2,1)S(1)}, u32[]{:S(2)}, u32[]{:S(2)}) collective-permute-start(bf16[72,512]{1,0:T(8,128)(2,1)S(1)} %get-tuple-element.96), channel_id=1, source_target_pairs={{0,32},{32,0},{64,96},{96,64},{1,33},{33,1},{65,97},{97,65},{2,34}... | collective-permute-start | bytes 221192 | tf_op jit(solution)/shard_map/ppermute | solution.py:28
  75.6 4.7 %shard_map.151 = (f32[256,512]{1,0:T(8,128)S(1)}, bf16[256,512]{1,0:T(8,128)(2,1)S(1)}) custom-call(s32[5]{0:T(128)S(1)} %stack.19.where_ref, bf16[512,128]{1,0:T(8,128)(2,1)S(1)} %get-tuple-element.51.refs_6_.refs_18_.sums, f32[1,512]{1,0:T(1,128)S(1)} %get-tuple-element.52.reward, bf16[8,64,512]{2,1,0:T(8,128)(2,1)S(1)} %get-tuple-element.72.entering, ...), custom_call_target="tpu_custom_call" | custom-call | flops 2000000000 | bytes 3000000 | tf_op jit(solution)/shard_map/pallas_call | solution.py:515
  80.6 2.6 %shard_map.156 = bf16[512,512]{1,0:T(8,128)(2,1)} custom-call(s32[5]{0:T(128)S(1)} %stack.19.where_ref, f32[256,512]{1,0:T(8,128)S(1)} %get-tuple-element.79.refs_0_, f32[64,512]{1,0:T(8,128)S(1)} %get-tuple-element.82.refs_1_, f32[192,512]{1,0:T(8,128)S(1)} %get-tuple-element.83.refs_2_, bf16[256,512]{1,0:T(8,128)(2,1)S(1)} %get-tuple-element.84.refs_3_, ...), custom_call_target="tpu_custom_call" | custom-call | flops 1000000000 | bytes 2000000 | tf_op jit(solution)/shard_map/pallas_call | solution.py:633
  (38 shorter events, 4.3 us)
Async XLA Ops:
  0.0 18.4 %collective-permute-start.10 = (bf16[1024,256]{1,0:T(8,128)(2,1)}, bf16[1024,256]{1,0:T(8,128)(2,1)S(1)}, u32[]{:S(2)}, u32[]{:S(2)}) collective-permute-start(bf16[1024,256]{1,0:T(8,128)(2,1)} %refs_2_.1), channel_id=1, source_target_pairs={{0,6},{2,4},{4,2},{6,0},{1,7},{3,5},{5,3},{7,1},{8,14},{10,12},{12... | collective-permute-start | bytes 1572872 | tf_op jit(solution)/shard_map/ppermute | solution.py:666
  4.1 15.3 %collective-permute-start.5 = (bf16[144,1024]{1,0:T(8,128)(2,1)S(1)}, bf16[144,1024]{1,0:T(8,128)(2,1)S(1)}, u32[]{:S(2)}, u32[]{:S(2)}) collective-permute-start(bf16[144,1024]{1,0:T(8,128)(2,1)S(1)} %get-tuple-element.55.refs_0_), channel_id=1, source_target_pairs={{0,2},{1,3},{2,0},{3,1},{4,6},{5,7},{6,4},{7,5},{8,10},{9,11},{10,... | collective-permute-start | bytes 884744 | tf_op jit(solution)/shard_map/ppermute | solution.py:28
  6.1 12.8 %collective-permute-start.6 = (bf16[128,1024]{1,0:T(8,128)(2,1)S(1)}, bf16[128,1024]{1,0:T(8,128)(2,1)S(1)}, u32[]{:S(2)}, u32[]{:S(2)}) collective-permute-start(bf16[128,1024]{1,0:T(8,128)(2,1)S(1)} %get-tuple-element.56.refs_1_), channel_id=1, source_target_pairs={{0,2},{1,3},{2,0},{3,1},{4,6},{5,7},{6,4},{7,5},{8,10},{9,11},{10,... | collective-permute-start | bytes 786440 | tf_op jit(solution)/shard_map/ppermute | solution.py:28
  6.2 12.8 %collective-permute-start.4 = (bf16[128,1024]{1,0:T(8,128)(2,1)S(1)}, bf16[128,1024]{1,0:T(8,128)(2,1)S(1)}, u32[]{:S(2)}, u32[]{:S(2)}) collective-permute-start(bf16[128,1024]{1,0:T(8,128)(2,1)S(1)} %get-tuple-element.56.refs_1_), channel_id=1, source_target_pairs={{0,1},{1,0},{2,3},{3,2},{4,5},{5,4},{6,7},{7,6},{8,9},{9,8},{10,11... | collective-permute-start | bytes 786440 | tf_op jit(solution)/shard_map/ppermute | solution.py:28
  6.2 12.2 %collective-permute-start = (bf16[16,1024]{1,0:T(8,128)(2,1)S(1)}, bf16[16,1024]{1,0:T(8,128)(2,1)S(1)}, u32[]{:S(2)}, u32[]{:S(2)}) collective-permute-start(bf16[16,1024]{1,0:T(8,128)(2,1)S(1)} %get-tuple-element.54), channel_id=1, source_target_pairs={{0,4},{4,8},{8,12},{12,16},{16,20},{20,24},{24,28},{28,32},{32,36}... | collective-permute-start | bytes 98312 | tf_op jit(solution)/shard_map/ppermute | solution.py:682
  18.4 6.2 %collective-permute-start.9 = (bf16[1024,256]{1,0:T(8,128)(2,1)}, bf16[1024,256]{1,0:T(8,128)(2,1)S(1)}, u32[]{:S(2)}, u32[]{:S(2)}) collective-permute-start(bf16[1024,256]{1,0:T(8,128)(2,1)} %refs_2_.1), channel_id=1, source_target_pairs={{0,1},{1,0},{2,3},{3,2},{4,5},{5,4},{6,7},{7,6},{8,9},{9,8},{10,11... | collective-permute-start | bytes 1572872 | tf_op jit(solution)/shard_map/ppermute | solution.py:28
  18.4 9.2 %collective-permute-start.11 = (bf16[1024,256]{1,0:T(8,128)(2,1)S(1)}, bf16[1024,256]{1,0:T(8,128)(2,1)S(1)}, u32[]{:S(2)}, u32[]{:S(2)}) collective-permute-start(bf16[1024,256]{1,0:T(8,128)(2,1)S(1)} %collective-permute-done.10.refs_10_.refs_6_), channel_id=1, source_target_pairs={{0,1},{1,0},{2,3},{3,2},{4,5},{5,4},{6,7},{7,6},{8,9},{9,8},{10,11... | collective-permute-start | bytes 1572872 | tf_op jit(solution)/shard_map/ppermute | solution.py:28
  18.9 3.4 %collective-permute-start.3 = (bf16[144,1024]{1,0:T(8,128)(2,1)S(1)}, bf16[144,1024]{1,0:T(8,128)(2,1)S(1)}, u32[]{:S(2)}, u32[]{:S(2)}) collective-permute-start(bf16[144,1024]{1,0:T(8,128)(2,1)S(1)} %get-tuple-element.55.refs_0_), channel_id=1, source_target_pairs={{0,1},{1,0},{2,3},{3,2},{4,5},{5,4},{6,7},{7,6},{8,9},{9,8},{10,11... | collective-permute-start | bytes 884744 | tf_op jit(solution)/shard_map/ppermute | solution.py:28
  19.0 8.6 %collective-permute-start.8 = (bf16[128,1024]{1,0:T(8,128)(2,1)S(1)}, bf16[128,1024]{1,0:T(8,128)(2,1)S(1)}, u32[]{:S(2)}, u32[]{:S(2)}) collective-permute-start(bf16[128,1024]{1,0:T(8,128)(2,1)S(1)} %collective-permute-done.6.refs_5_), channel_id=1, source_target_pairs={{0,1},{1,0},{2,3},{3,2},{4,5},{5,4},{6,7},{7,6},{8,9},{9,8},{10,11... | collective-permute-start | bytes 786440 | tf_op jit(solution)/shard_map/ppermute | solution.py:28
  19.4 8.2 %collective-permute-start.7 = (bf16[144,1024]{1,0:T(8,128)(2,1)S(1)}, bf16[144,1024]{1,0:T(8,128)(2,1)S(1)}, u32[]{:S(2)}, u32[]{:S(2)}) collective-permute-start(bf16[144,1024]{1,0:T(8,128)(2,1)S(1)} %collective-permute-done.5.refs_4_), channel_id=1, source_target_pairs={{0,1},{1,0},{2,3},{3,2},{4,5},{5,4},{6,7},{7,6},{8,9},{9,8},{10,11... | collective-permute-start | bytes 884744 | tf_op jit(solution)/shard_map/ppermute | solution.py:28
  19.5 2.8 %copy-start = (bf16[1024,128]{1,0:T(8,128)(2,1)S(1)}, bf16[1024,128]{1,0:T(8,128)(2,1)}, u32[]{:S(2)}) copy-start(bf16[1024,128]{1,0:T(8,128)(2,1)} %refs_9_.1) | copy-start | bytes 786436
  22.4 18.7 %collective-permute-start.14 = (bf16[1024,128]{1,0:T(8,128)(2,1)S(1)}, bf16[1024,128]{1,0:T(8,128)(2,1)S(1)}, u32[]{:S(2)}, u32[]{:S(2)}) collective-permute-start(bf16[1024,128]{1,0:T(8,128)(2,1)S(1)} %copy-done), channel_id=1, source_target_pairs={{0,6},{2,4},{4,2},{6,0},{1,7},{3,5},{5,3},{7,1},{8,14},{10,12},{12... | collective-permute-start | bytes 786440 | tf_op jit(solution)/shard_map/ppermute | solution.py:666
  24.6 15.9 %collective-permute-start.2 = (bf16[272,1024]{1,0:T(8,128)(2,1)S(1)}, bf16[272,1024]{1,0:T(8,128)(2,1)S(1)}, u32[]{:S(2)}, u32[]{:S(2)}) collective-permute-start(bf16[272,1024]{1,0:T(8,128)(2,1)S(1)} %constant_dynamic-update-slice_fusion.refs_0_), channel_id=1, source_target_pairs={{0,2},{1,3},{2,0},{3,1},{4,6},{5,7},{6,4},{7,5},{8,10},{9,11},{10,... | collective-permute-start | bytes 1671176 | tf_op jit(solution)/shard_map/ppermute | solution.py:28
  27.6 17.9 %collective-permute-start.1 = (bf16[272,1024]{1,0:T(8,128)(2,1)S(1)}, bf16[272,1024]{1,0:T(8,128)(2,1)S(1)}, u32[]{:S(2)}, u32[]{:S(2)}) collective-permute-start(bf16[272,1024]{1,0:T(8,128)(2,1)S(1)} %constant_dynamic-update-slice_fusion.refs_0_), channel_id=1, source_target_pairs={{0,1},{1,0},{2,3},{3,2},{4,5},{5,4},{6,7},{7,6},{8,9},{9,8},{10,11... | collective-permute-start | bytes 1671176 | tf_op jit(solution)/shard_map/ppermute | solution.py:28
  40.5 5.0 %collective-permute-start.12 = (bf16[272,1024]{1,0:T(8,128)(2,1)S(1)}, bf16[272,1024]{1,0:T(8,128)(2,1)S(1)}, u32[]{:S(2)}, u32[]{:S(2)}) collective-permute-start(bf16[272,1024]{1,0:T(8,128)(2,1)S(1)} %collective-permute-done.2.refs_2_), channel_id=1, source_target_pairs={{0,1},{1,0},{2,3},{3,2},{4,5},{5,4},{6,7},{7,6},{8,9},{9,8},{10,11... | collective-permute-start | bytes 1671176 | tf_op jit(solution)/shard_map/ppermute | solution.py:28
  40.5 2.3 %collective-permute-start.13 = (bf16[1024,128]{1,0:T(8,128)(2,1)S(1)}, bf16[1024,128]{1,0:T(8,128)(2,1)S(1)}, u32[]{:S(2)}, u32[]{:S(2)}) collective-permute-start(bf16[1024,128]{1,0:T(8,128)(2,1)S(1)} %copy-done), channel_id=1, source_target_pairs={{0,1},{1,0},{2,3},{3,2},{4,5},{5,4},{6,7},{7,6},{8,9},{9,8},{10,11... | collective-permute-start | bytes 786440 | tf_op jit(solution)/shard_map/ppermute | solution.py:28
  41.0 2.2 %collective-permute-start.15 = (bf16[1024,128]{1,0:T(8,128)(2,1)S(1)}, bf16[1024,128]{1,0:T(8,128)(2,1)S(1)}, u32[]{:S(2)}, u32[]{:S(2)}) collective-permute-start(bf16[1024,128]{1,0:T(8,128)(2,1)S(1)} %collective-permute-done.14.refs_2_.refs_10_), channel_id=1, source_target_pairs={{0,1},{1,0},{2,3},{3,2},{4,5},{5,4},{6,7},{7,6},{8,9},{9,8},{10,11... | collective-permute-start | bytes 786440 | tf_op jit(solution)/shard_map/ppermute | solution.py:28
  53.8 6.6 %collective-permute-start.16 = (bf16[72,512]{1,0:T(8,128)(2,1)S(1)}, bf16[72,512]{1,0:T(8,128)(2,1)S(1)}, u32[]{:S(2)}, u32[]{:S(2)}) collective-permute-start(bf16[72,512]{1,0:T(8,128)(2,1)S(1)} %get-tuple-element.90), channel_id=1, source_target_pairs={{0,4},{4,0},{1,5},{5,1},{2,6},{6,2},{3,7},{7,3},{8,12},{12,8},{9,1... | collective-permute-start | bytes 221192 | tf_op jit(solution)/shard_map/ppermute | solution.py:28
  61.0 6.8 %collective-permute-start.19 = (bf16[72,512]{1,0:T(8,128)(2,1)S(1)}, bf16[72,512]{1,0:T(8,128)(2,1)S(1)}, u32[]{:S(2)}, u32[]{:S(2)}) collective-permute-start(bf16[72,512]{1,0:T(8,128)(2,1)S(1)} %get-tuple-element.93), channel_id=1, source_target_pairs={{0,24},{8,16},{16,8},{24,0},{1,25},{9,17},{17,9},{25,1},{2,26},{10... | collective-permute-start | bytes 221192 | tf_op jit(solution)/shard_map/ppermute | solution.py:28
  63.8 6.0 %collective-permute-start.18 = (bf16[72,512]{1,0:T(8,128)(2,1)S(1)}, bf16[72,512]{1,0:T(8,128)(2,1)S(1)}, u32[]{:S(2)}, u32[]{:S(2)}) collective-permute-start(bf16[72,512]{1,0:T(8,128)(2,1)S(1)} %get-tuple-element.93), channel_id=1, source_target_pairs={{0,16},{8,24},{16,0},{24,8},{1,17},{9,25},{17,1},{25,9},{2,18},{10... | collective-permute-start | bytes 221192 | tf_op jit(solution)/shard_map/ppermute | solution.py:28
  64.6 5.2 %collective-permute-start.17 = (bf16[72,512]{1,0:T(8,128)(2,1)S(1)}, bf16[72,512]{1,0:T(8,128)(2,1)S(1)}, u32[]{:S(2)}, u32[]{:S(2)}) collective-permute-start(bf16[72,512]{1,0:T(8,128)(2,1)S(1)} %get-tuple-element.93), channel_id=1, source_target_pairs={{0,8},{8,0},{16,24},{24,16},{1,9},{9,1},{17,25},{25,17},{2,10},{10... | collective-permute-start | bytes 221192 | tf_op jit(solution)/shard_map/ppermute | solution.py:28
  70.6 9.8 %collective-permute-start.22 = (bf16[72,512]{1,0:T(8,128)(2,1)S(1)}, bf16[72,512]{1,0:T(8,128)(2,1)S(1)}, u32[]{:S(2)}, u32[]{:S(2)}) collective-permute-start(bf16[72,512]{1,0:T(8,128)(2,1)S(1)} %get-tuple-element.96), channel_id=1, source_target_pairs={{0,96},{32,64},{64,32},{96,0},{1,97},{33,65},{65,33},{97,1},{2,98}... | collective-permute-start | bytes 221192 | tf_op jit(solution)/shard_map/ppermute | solution.py:28
  74.7 5.9 %collective-permute-start.21 = (bf16[72,512]{1,0:T(8,128)(2,1)S(1)}, bf16[72,512]{1,0:T(8,128)(2,1)S(1)}, u32[]{:S(2)}, u32[]{:S(2)}) collective-permute-start(bf16[72,512]{1,0:T(8,128)(2,1)S(1)} %get-tuple-element.96), channel_id=1, source_target_pairs={{0,64},{32,96},{64,0},{96,32},{1,65},{33,97},{65,1},{97,33},{2,66}... | collective-permute-start | bytes 221192 | tf_op jit(solution)/shard_map/ppermute | solution.py:28
  74.7 5.9 %collective-permute-start.20 = (bf16[72,512]{1,0:T(8,128)(2,1)S(1)}, bf16[72,512]{1,0:T(8,128)(2,1)S(1)}, u32[]{:S(2)}, u32[]{:S(2)}) collective-permute-start(bf16[72,512]{1,0:T(8,128)(2,1)S(1)} %get-tuple-element.96), channel_id=1, source_target_pairs={{0,32},{32,0},{64,96},{96,64},{1,33},{33,1},{65,97},{97,65},{2,34}... | collective-permute-start | bytes 221192 | tf_op jit(solution)/shard_map/ppermute | solution.py:28
